TPU v7x, 512 devices: a whole 4x4x16 slice. The times are simulated.
512 devices in a mesh: line: 4 (over z_lo), tx: 8 (over z_hi, core), ty: 16 (over y, x).
Axes of the slice: x: 4, y: 4, z: 16 (z_hi: 4, z_lo: 4; z = z_hi * 4 + z_lo), core: 2. Of those that a mesh axis runs over, the one named last changes fastest.
Arguments:
- right_side: float32 [16, 32, 64, 128], P('line', 'tx', 'ty'), may hold values from -3 to 3
- start_field: float32 [16, 32, 64, 128], P('line', 'tx', 'ty'), may hold values from -3 to 3
- line_inverse: bfloat16 [16, 32, 64, 128, 128], P('line', 'tx', 'ty'), as said below
- lower_scale: float32 [16, 32, 64], P('line', 'tx', 'ty'), may hold values from 0.85 to 1
- upper_scale: float32 [16, 32, 64], P('line', 'tx', 'ty'), may hold values from 0.85 to 1
- lower_block: float32 [128, 128], replicated
- upper_block: float32 [128, 128], replicated
- face_blocks: float32 [4, 128, 128], replicated, may hold values from -0.15625 to 0.15625
- face_kind: int32 [4, 16, 32, 64], P(None, 'line', 'tx', 'ty'), may hold values from 0 to 3
- face_scale: float32 [4, 16, 32, 64], P(None, 'line', 'tx', 'ty'), may hold values from 0.25 to 1
- agglomerate: int32 [16, 32, 64], P('line', 'tx', 'ty'), may hold values from 0 to 255
- restriction: float32 [32, 128], replicated, may hold values from -0.5 to 0.5
- coarse_inverse: float32 [4, 8, 256, 32, 32], P('line', 'tx', 'ty'), as said below
Outputs:
- corrected: float32 [16, 32, 64, 128], P('line', 'tx', 'ty')
- residual: float32 [16, 32, 64, 128], P('line', 'tx', 'ty')
Inputs may be any that keep to these rules, and one draw needn't show every extreme that they name: An element's agglomerate is one of the 256 agglomerates of its own column. `line_inverse`: each block is a diagonal of positive entries plus a full-rank part. `coarse_inverse`: each block is a diagonal of positive entries plus a full-rank part.
All inputs are finite; a program needn't handle non-finite values.
Results may differ from a plain program's by a relative error of at most 0.0003.
Values sent between devices are 32-bit elements; how exact they have to be, the bound alone decides.
No kernel may reach another device: no remote copies, remote signals or barrier semaphores. Data moves between devices by JAX's collectives and lax.ppermute only.
A program may use at most 64 MiB of HBM per device.

v0:
```python
import jax
import jax.numpy as jnp
from jax import lax
from jax.sharding import PartitionSpec as P

SWEEPS = 2


highest = lax.Precision.HIGHEST


def with_halo(array, sides, width):
    edges = {}
    for axis, dim in sides:
        count, length = (lax.axis_size(axis), array.shape[dim])
        up = [(i, (i + 1) % count) for i in range(count - 1)]
        last = lax.slice_in_dim(array, length - width, length, axis=dim)
        leading = lax.slice_in_dim(array, 0, width, axis=dim)
        edges[dim] = (
            lax.ppermute(last, axis, up),
            lax.ppermute(leading, axis, [(b, a) for a, b in up]),
        )
    done = []
    for _, dim in sides:
        low, high = edges[dim]
        around = [(width, width) if d in done else (0, 0) for d in range(array.ndim)]
        array = jnp.concatenate([jnp.pad(low, around), array, jnp.pad(high, around)], axis=dim)
        done.append(dim)
    return array


def from_behind(value, axis, steps):
    count = lax.axis_size(axis)
    leading, last = (max(0, -steps), min(count, count - steps))
    return lax.ppermute(value, axis, [(source, source + steps) for source in range(leading, last)])


def split_up(array, dim, count):
    before, after = (array.shape[:dim], array.shape[dim + 1 :])
    return jnp.moveaxis(array.reshape(*before, count, -1, *after), dim, 0)


def summed_on_arrival(array, axis, dim):
    count = lax.axis_size(axis)
    parts = lax.all_to_all(split_up(array, dim, count), axis, 0, 0, tiled=True)
    return jnp.sum(parts, axis=0)


def from_everyone(array, axis):
    count = lax.axis_size(axis)
    return lax.all_to_all(
        jnp.broadcast_to(array[None], (count, *array.shape)), axis, 0, 0, tiled=True
    )


def laid_out(parts, dim):
    parts = jnp.moveaxis(parts, 0, dim)
    dims = parts.shape
    return parts.reshape(*dims[:dim], dims[dim] * dims[dim + 1], *dims[dim + 2 :])


def gather_directly(array, axis, dim):
    parts = from_everyone(array, axis)
    return laid_out(parts, dim)


def couple(field, face_blocks, face_kind, face_scale):
    padded = with_halo(field, (("tx", 1), ("ty", 2)), 1)
    beside = (padded[:, :-2, 1:-1], padded[:, 2:, 1:-1], padded[:, 1:-1, :-2], padded[:, 1:-1, 2:])
    total = jnp.zeros_like(field)
    kinds = jnp.arange(4, dtype=jnp.int32)
    for side in range(4):
        images = jnp.einsum("sxyb,kcb->ksxyc", beside[side], face_blocks, precision=highest)
        chosen = (face_kind[side][None] == kinds[:, None, None, None]).astype(jnp.float32)
        picked = jnp.sum(chosen[..., None] * images, axis=0)
        total = total + face_scale[side][..., None] * picked
    return total


def forward(line_inverse, lower_scale, lower_block, drive, start):

    def forward_step(carry, items):
        inverse, scale, source = items
        inner = source - scale[..., None] * jnp.einsum(
            "cb,xyb->xyc", lower_block, carry, precision=highest
        )
        value = jnp.einsum("xycb,xyb->xyc", inverse.astype(jnp.float32), inner, precision=highest)
        return (value, value)

    final, values = lax.scan(forward_step, start, (line_inverse, lower_scale, drive))
    return values


def backward(line_inverse, upper_scale, upper_block, ahead, start):

    def backward_step(carry, items):
        inverse, scale, source = items
        inner = scale[..., None] * jnp.einsum("cb,xyb->xyc", upper_block, carry, precision=highest)
        value = source - jnp.einsum(
            "xycb,xyb->xyc", inverse.astype(jnp.float32), inner, precision=highest
        )
        return (value, value)

    final, values = lax.scan(backward_step, start, (line_inverse, upper_scale, ahead), reverse=True)
    return values


def body(
    right_side,
    start_field,
    line_inverse,
    lower_scale,
    upper_scale,
    lower_block,
    upper_block,
    face_blocks,
    face_kind,
    face_scale,
    agglomerate,
    restriction,
    coarse_inverse,
):
    width = right_side.shape[-1]
    empty = jnp.zeros(right_side.shape[1:], jnp.float32)
    segments = lax.axis_size("line")
    field = start_field
    previous = start_field
    for sweep in range(SWEEPS):
        previous = field
        drive = right_side - couple(previous, face_blocks, face_kind, face_scale)
        incoming = empty
        for turn in range(segments - 1):
            ahead = forward(line_inverse, lower_scale, lower_block, drive, incoming)
            incoming = from_behind(ahead[-1], "line", 1)
        ahead = forward(line_inverse, lower_scale, lower_block, drive, incoming)
        arriving = empty
        for turn in range(segments - 1):
            behind = backward(line_inverse, upper_scale, upper_block, ahead, arriving)
            arriving = from_behind(behind[0], "line", -1)
        field = backward(line_inverse, upper_scale, upper_block, ahead, arriving)
    residual = couple(previous - field, face_blocks, face_kind, face_scale)
    owned_count = coarse_inverse.shape[2]
    total_aggs = owned_count * lax.axis_size("ty")
    flat = residual.reshape(-1, width)
    projected = jnp.einsum("cb,eb->ec", restriction, flat, precision=highest)
    chosen = (
        agglomerate.reshape(-1)[:, None] == jnp.arange(total_aggs, dtype=jnp.int32)[None, :]
    ).astype(jnp.float32)
    partial_value = jnp.einsum("ea,ec->ac", chosen, projected, precision=highest)
    owned = summed_on_arrival(partial_value, "ty", 0)
    update = jnp.einsum("acd,ad->ac", coarse_inverse[0, 0], owned, precision=highest)
    spread = jnp.einsum("ea,ac->ec", chosen, gather_directly(update, "ty", 0), precision=highest)
    fine = jnp.einsum("cb,ec->eb", restriction, spread, precision=highest).reshape(residual.shape)
    return (field + fine, residual)


def solution(mesh):
    in_specs = (
        P("line", "tx", "ty", None),
        P("line", "tx", "ty", None),
        P("line", "tx", "ty", None, None),
        P("line", "tx", "ty"),
        P("line", "tx", "ty"),
        P(),
        P(),
        P(),
        P(None, "line", "tx", "ty"),
        P(None, "line", "tx", "ty"),
        P("line", "tx", "ty"),
        P(),
        P("line", "tx", "ty", None, None),
    )
    out_specs = (P("line", "tx", "ty", None), P("line", "tx", "ty", None))
    return jax.shard_map(body, mesh=mesh, in_specs=in_specs, out_specs=out_specs, check_vma=False)
```

profile of v0, /device:TPU:1, one launch (start us, length us, event | category | flops | bytes accessed | tf_op | source)
XLA Modules:
  0.0 238.3 jit_solution(14356176647562546191)
XLA Ops:
  1.4 10.2 %collective-permute-start = (f32[4,1,4,128]{3,2,1,0:T(4,128)S(1)}, f32[4,1,4,128]{3,2,1,0:T(4,128)S(1)}, u32[]{:S(2)}, u32[]{:S(2)}) collective-permute-start(f32[4,1,4,128]{3,2,1,0:T(4,128)S(1)} %get-tuple-element.1753), channel_id=1, source_target_pairs={{0,16},{16,32},{32,48},{48,64},{64,80},{80,96},{96,112},{1,17},{17... | collective-permute-start | bytes 24584 | tf_op jit(solution)/shard_map/ppermute | solution.py:20
  11.6 1.9 collective-permute-start.1
  14.4 1.3 collective-permute-start.3
  15.7 4.0 %collective-permute-start.2 = (f32[4,4,1,128]{3,2,1,0:T(1,128)S(1)}, f32[4,4,1,128]{3,2,1,0:T(1,128)S(1)}, u32[]{:S(2)}, u32[]{:S(2)}) collective-permute-start(f32[4,4,1,128]{3,2,1,0:T(1,128)S(1)} %get-tuple-element.1750), channel_id=1, source_target_pairs={{0,1},{1,2},{2,3},{3,4},{4,5},{5,6},{6,7},{7,8},{8,9},{9,10},{10,1... | collective-permute-start | bytes 24584 | tf_op jit(solution)/shard_map/ppermute | solution.py:20
  21.3 1.3 fusion.119
  25.7 4.7 %while.226 = (s32[]{:T(128)}, f32[4,4,128]{2,1,0:T(4,128)S(1)}, f32[4,4,4,128]{3,2,1,0:T(4,128)S(1)}, bf16[4,4,4,128,128]{4,3,2,1,0:T(8,128)(2,1)S(1)}, f32[4,4,...) while((s32[]{:T(128)}, f32[4,4,128]{2,1,0:T(4,128)S(1)}, ...), condition=%wide.region_5.6_spmd, body=%wide.region_4.5_spmd.sunk | while | flops 6295554 | bytes 647461 | solution.py:90
  30.5 3.5 %collective-permute-start.4 = (f32[4,4,128]{2,1,0:T(4,128)S(1)}, f32[4,4,128]{2,1,0:T(4,128)S(1)}, u32[]{:S(2)}, u32[]{:S(2)}) collective-permute-start(f32[4,4,128]{2,1,0:T(4,128)S(1)} %slice_bitcast_fusion.11), channel_id=1, source_target_pairs={{0,128},{128,256},{256,384},{1,129},{129,257},{257,385},{2,130},{1... | collective-permute-start | bytes 24584 | tf_op jit(solution)/shard_map/ppermute | solution.py:35
  34.8 4.7 %while.227 = (s32[]{:T(128)}, f32[4,4,128]{2,1,0:T(4,128)S(1)}, f32[4,4,4,128]{3,2,1,0:T(4,128)S(1)}, bf16[4,4,4,128,128]{4,3,2,1,0:T(8,128)(2,1)S(1)}, f32[4,4,...) while((s32[]{:T(128)}, f32[4,4,128]{2,1,0:T(4,128)S(1)}, ...), condition=%wide.region_7.8_spmd, body=%wide.region_6.7_spmd.sunk | while | flops 6295554 | bytes 647461 | solution.py:90
  39.5 3.6 %collective-permute-start.5 = (f32[4,4,128]{2,1,0:T(4,128)S(1)}, f32[4,4,128]{2,1,0:T(4,128)S(1)}, u32[]{:S(2)}, u32[]{:S(2)}) collective-permute-start(f32[4,4,128]{2,1,0:T(4,128)S(1)} %slice_bitcast_fusion.10), channel_id=1, source_target_pairs={{0,128},{128,256},{256,384},{1,129},{129,257},{257,385},{2,130},{1... | collective-permute-start | bytes 24584 | tf_op jit(solution)/shard_map/ppermute | solution.py:35
  43.9 4.7 %while.228 = (s32[]{:T(128)}, f32[4,4,128]{2,1,0:T(4,128)S(1)}, f32[4,4,4,128]{3,2,1,0:T(4,128)S(1)}, bf16[4,4,4,128,128]{4,3,2,1,0:T(8,128)(2,1)S(1)}, f32[4,4,...) while((s32[]{:T(128)}, f32[4,4,128]{2,1,0:T(4,128)S(1)}, ...), condition=%wide.region_9.10_spmd, body=%wide.region_8.9_spmd.sunk | while | flops 6295554 | bytes 647461 | solution.py:90
  48.7 3.8 %collective-permute-start.6 = (f32[4,4,128]{2,1,0:T(4,128)S(1)}, f32[4,4,128]{2,1,0:T(4,128)S(1)}, u32[]{:S(2)}, u32[]{:S(2)}) collective-permute-start(f32[4,4,128]{2,1,0:T(4,128)S(1)} %slice_bitcast_fusion.9), channel_id=1, source_target_pairs={{0,128},{128,256},{256,384},{1,129},{129,257},{257,385},{2,130},{1... | collective-permute-start | bytes 24584 | tf_op jit(solution)/shard_map/ppermute | solution.py:35
  53.2 4.7 %while.229 = (s32[]{:T(128)}, f32[4,4,128]{2,1,0:T(4,128)S(1)}, f32[4,4,4,128]{3,2,1,0:T(4,128)S(1)}, bf16[4,4,4,128,128]{4,3,2,1,0:T(8,128)(2,1)S(1)}, f32[4,4,...) while((s32[]{:T(128)}, f32[4,4,128]{2,1,0:T(4,128)S(1)}, ...), condition=%wide.region_11.12_spmd, body=%wide.region_10.11_spmd.sunk | while | flops 6295554 | bytes 647461 | solution.py:90
  58.0 4.9 %while.240 = (s32[]{:T(128)}, f32[4,4,128]{2,1,0:T(4,128)S(1)}, f32[4,4,4,128]{3,2,1,0:T(4,128)S(1)}, f32[4,4,4,128]{3,2,1,0:T(4,128)S(1)}, bf16[4,4,4,128,128]{...) while((s32[]{:T(128)}, f32[4,4,128]{2,1,0:T(4,128)S(1)}, ...), condition=%wide.region_13.14_spmd.clone, body=%wide.region_12.13_spmd.clone.sunk | while | flops 6297604 | bytes 655687 | solution.py:104
  62.8 1.3 collective-permute-start.7
  64.1 3.4 %collective-permute-done.7 = f32[4,4,128]{2,1,0:T(4,128)S(1)} collective-permute-done((f32[4,4,128]{2,1,0:T(4,128)S(1)}, f32[4,4,128]{2,1,0:T(4,128)S(1)}, u32[]{:S(2)}, u32[]{:S(2)}) %collective-permute-start.7) | collective-permute-done | bytes 8224 | tf_op jit(solution)/shard_map/ppermute | solution.py:35
  67.5 4.8 %while.230 = (s32[]{:T(128)}, f32[4,4,128]{2,1,0:T(4,128)S(1)}, f32[4,4,4,128]{3,2,1,0:T(4,128)S(1)}, f32[4,4,4,128]{3,2,1,0:T(4,128)S(1)}, bf16[4,4,4,128,128]{...) while((s32[]{:T(128)}, f32[4,4,128]{2,1,0:T(4,128)S(1)}, ...), condition=%wide.region_15.16_spmd, body=%wide.region_14.15_spmd.sunk | while | flops 6295555 | bytes 655669 | solution.py:104
  72.3 1.3 collective-permute-start.8
  73.6 3.5 %collective-permute-done.8 = f32[4,4,128]{2,1,0:T(4,128)S(1)} collective-permute-done((f32[4,4,128]{2,1,0:T(4,128)S(1)}, f32[4,4,128]{2,1,0:T(4,128)S(1)}, u32[]{:S(2)}, u32[]{:S(2)}) %collective-permute-start.8) | collective-permute-done | bytes 8224 | tf_op jit(solution)/shard_map/ppermute | solution.py:35
  77.2 4.8 %while.231 = (s32[]{:T(128)}, f32[4,4,128]{2,1,0:T(4,128)S(1)}, f32[4,4,4,128]{3,2,1,0:T(4,128)S(1)}, f32[4,4,4,128]{3,2,1,0:T(4,128)S(1)}, bf16[4,4,4,128,128]{...) while((s32[]{:T(128)}, f32[4,4,128]{2,1,0:T(4,128)S(1)}, ...), condition=%wide.region_17.18_spmd, body=%wide.region_16.17_spmd.sunk | while | flops 6295555 | bytes 655669 | solution.py:104
  82.0 1.3 collective-permute-start.9
  83.3 3.1 %collective-permute-done.9 = f32[4,4,128]{2,1,0:T(4,128)S(1)} collective-permute-done((f32[4,4,128]{2,1,0:T(4,128)S(1)}, f32[4,4,128]{2,1,0:T(4,128)S(1)}, u32[]{:S(2)}, u32[]{:S(2)}) %collective-permute-start.9) | collective-permute-done | bytes 8224 | tf_op jit(solution)/shard_map/ppermute | solution.py:35
  86.4 4.8 %while.232 = (s32[]{:T(128)}, f32[4,4,128]{2,1,0:T(4,128)S(1)}, f32[4,4,4,128]{3,2,1,0:T(4,128)S(1)}, f32[4,4,4,128]{3,2,1,0:T(4,128)S(1)}, bf16[4,4,4,128,128]{...) while((s32[]{:T(128)}, f32[4,4,128]{2,1,0:T(4,128)S(1)}, ...), condition=%wide.region_19.20_spmd, body=%wide.region_18.19_spmd.sunk | while | flops 6295555 | bytes 655669 | solution.py:104
  91.2 14.3 %collective-permute-start.10 = (f32[4,1,4,128]{3,2,1,0:T(4,128)S(1)}, f32[4,1,4,128]{3,2,1,0:T(4,128)S(1)}, u32[]{:S(2)}, u32[]{:S(2)}) collective-permute-start(f32[4,1,4,128]{3,2,1,0:T(4,128)S(1)} %get-tuple-element.1745), channel_id=1, source_target_pairs={{0,16},{16,32},{32,48},{48,64},{64,80},{80,96},{96,112},{1,17},{17... | collective-permute-start | bytes 24584 | tf_op jit(solution)/shard_map/ppermute | solution.py:20
  105.6 1.9 collective-permute-start.11
  107.5 3.1 %collective-permute-start.12 = (f32[4,4,1,128]{3,2,1,0:T(1,128)S(1)}, f32[4,4,1,128]{3,2,1,0:T(1,128)S(1)}, u32[]{:S(2)}, u32[]{:S(2)}) collective-permute-start(f32[4,4,1,128]{3,2,1,0:T(1,128)S(1)} %get-tuple-element.1742), channel_id=1, source_target_pairs={{0,1},{1,2},{2,3},{3,4},{4,5},{5,6},{6,7},{7,8},{8,9},{9,10},{10,1... | collective-permute-start | bytes 24584 | tf_op jit(solution)/shard_map/ppermute | solution.py:20
  112.4 2.0 collective-permute-done.11
  116.0 4.7 %while.233 = (s32[]{:T(128)}, f32[4,4,128]{2,1,0:T(4,128)S(1)}, f32[4,4,4,128]{3,2,1,0:T(4,128)S(1)}, bf16[4,4,4,128,128]{4,3,2,1,0:T(8,128)(2,1)S(1)}, f32[4,4,...) while((s32[]{:T(128)}, f32[4,4,128]{2,1,0:T(4,128)S(1)}, ...), condition=%wide.region_25.26_spmd, body=%wide.region_24.25_spmd.sunk | while | flops 6295554 | bytes 647461 | solution.py:90
  120.7 3.6 %collective-permute-start.14 = (f32[4,4,128]{2,1,0:T(4,128)S(1)}, f32[4,4,128]{2,1,0:T(4,128)S(1)}, u32[]{:S(2)}, u32[]{:S(2)}) collective-permute-start(f32[4,4,128]{2,1,0:T(4,128)S(1)} %slice_bitcast_fusion.5), channel_id=1, source_target_pairs={{0,128},{128,256},{256,384},{1,129},{129,257},{257,385},{2,130},{1... | collective-permute-start | bytes 24584 | tf_op jit(solution)/shard_map/ppermute | solution.py:35
  125.2 4.7 %while.234 = (s32[]{:T(128)}, f32[4,4,128]{2,1,0:T(4,128)S(1)}, f32[4,4,4,128]{3,2,1,0:T(4,128)S(1)}, bf16[4,4,4,128,128]{4,3,2,1,0:T(8,128)(2,1)S(1)}, f32[4,4,...) while((s32[]{:T(128)}, f32[4,4,128]{2,1,0:T(4,128)S(1)}, ...), condition=%wide.region_27.28_spmd, body=%wide.region_26.27_spmd.sunk | while | flops 6295554 | bytes 647461 | solution.py:90
  129.9 3.6 %collective-permute-start.15 = (f32[4,4,128]{2,1,0:T(4,128)S(1)}, f32[4,4,128]{2,1,0:T(4,128)S(1)}, u32[]{:S(2)}, u32[]{:S(2)}) collective-permute-start(f32[4,4,128]{2,1,0:T(4,128)S(1)} %slice_bitcast_fusion.4), channel_id=1, source_target_pairs={{0,128},{128,256},{256,384},{1,129},{129,257},{257,385},{2,130},{1... | collective-permute-start | bytes 24584 | tf_op jit(solution)/shard_map/ppermute | solution.py:35
  134.3 4.7 %while.235 = (s32[]{:T(128)}, f32[4,4,128]{2,1,0:T(4,128)S(1)}, f32[4,4,4,128]{3,2,1,0:T(4,128)S(1)}, bf16[4,4,4,128,128]{4,3,2,1,0:T(8,128)(2,1)S(1)}, f32[4,4,...) while((s32[]{:T(128)}, f32[4,4,128]{2,1,0:T(4,128)S(1)}, ...), condition=%wide.region_29.30_spmd, body=%wide.region_28.29_spmd.sunk | while | flops 6295554 | bytes 647461 | solution.py:90
  139.0 3.6 %collective-permute-start.16 = (f32[4,4,128]{2,1,0:T(4,128)S(1)}, f32[4,4,128]{2,1,0:T(4,128)S(1)}, u32[]{:S(2)}, u32[]{:S(2)}) collective-permute-start(f32[4,4,128]{2,1,0:T(4,128)S(1)} %slice_bitcast_fusion.3), channel_id=1, source_target_pairs={{0,128},{128,256},{256,384},{1,129},{129,257},{257,385},{2,130},{1... | collective-permute-start | bytes 24584 | tf_op jit(solution)/shard_map/ppermute | solution.py:35
  143.4 4.7 %while.236 = (s32[]{:T(128)}, f32[4,4,128]{2,1,0:T(4,128)S(1)}, f32[4,4,4,128]{3,2,1,0:T(4,128)S(1)}, bf16[4,4,4,128,128]{4,3,2,1,0:T(8,128)(2,1)S(1)}, f32[4,4,...) while((s32[]{:T(128)}, f32[4,4,128]{2,1,0:T(4,128)S(1)}, ...), condition=%wide.region_31.32_spmd, body=%wide.region_30.31_spmd.sunk | while | flops 6295554 | bytes 647461 | solution.py:90
  148.1 4.9 %while.241 = (s32[]{:T(128)}, f32[4,4,128]{2,1,0:T(4,128)S(1)}, f32[4,4,4,128]{3,2,1,0:T(4,128)S(1)}, f32[4,4,4,128]{3,2,1,0:T(4,128)S(1)}, bf16[4,4,4,128,128]{...) while((s32[]{:T(128)}, f32[4,4,128]{2,1,0:T(4,128)S(1)}, ...), condition=%wide.region_33.34_spmd.clone, body=%wide.region_32.33_spmd.clone.sunk | while | flops 6297604 | bytes 655687 | solution.py:104
  153.0 1.5 collective-permute-start.17
  154.5 3.2 %collective-permute-done.17 = f32[4,4,128]{2,1,0:T(4,128)S(1)} collective-permute-done((f32[4,4,128]{2,1,0:T(4,128)S(1)}, f32[4,4,128]{2,1,0:T(4,128)S(1)}, u32[]{:S(2)}, u32[]{:S(2)}) %collective-permute-start.17) | collective-permute-done | bytes 8224 | tf_op jit(solution)/shard_map/ppermute | solution.py:35
  157.7 4.8 %while.237 = (s32[]{:T(128)}, f32[4,4,128]{2,1,0:T(4,128)S(1)}, f32[4,4,4,128]{3,2,1,0:T(4,128)S(1)}, f32[4,4,4,128]{3,2,1,0:T(4,128)S(1)}, bf16[4,4,4,128,128]{...) while((s32[]{:T(128)}, f32[4,4,128]{2,1,0:T(4,128)S(1)}, ...), condition=%wide.region_35.36_spmd, body=%wide.region_34.35_spmd.sunk | while | flops 6295555 | bytes 655669 | solution.py:104
  163.8 3.3 %collective-permute-done.18 = f32[4,4,128]{2,1,0:T(4,128)S(1)} collective-permute-done((f32[4,4,128]{2,1,0:T(4,128)S(1)}, f32[4,4,128]{2,1,0:T(4,128)S(1)}, u32[]{:S(2)}, u32[]{:S(2)}) %collective-permute-start.18) | collective-permute-done | bytes 8224 | tf_op jit(solution)/shard_map/ppermute | solution.py:35
  167.1 4.8 %while.238 = (s32[]{:T(128)}, f32[4,4,128]{2,1,0:T(4,128)S(1)}, f32[4,4,4,128]{3,2,1,0:T(4,128)S(1)}, f32[4,4,4,128]{3,2,1,0:T(4,128)S(1)}, bf16[4,4,4,128,128]{...) while((s32[]{:T(128)}, f32[4,4,128]{2,1,0:T(4,128)S(1)}, ...), condition=%wide.region_37.38_spmd, body=%wide.region_36.37_spmd.sunk | while | flops 6295555 | bytes 655669 | solution.py:104
  173.7 2.9 %collective-permute-done.19 = f32[4,4,128]{2,1,0:T(4,128)S(1)} collective-permute-done((f32[4,4,128]{2,1,0:T(4,128)S(1)}, f32[4,4,128]{2,1,0:T(4,128)S(1)}, u32[]{:S(2)}, u32[]{:S(2)}) %collective-permute-start.19) | collective-permute-done | bytes 8224 | tf_op jit(solution)/shard_map/ppermute | solution.py:35
  176.6 4.8 %while.239 = (s32[]{:T(128)}, f32[4,4,128]{2,1,0:T(4,128)S(1)}, f32[4,4,4,128]{3,2,1,0:T(4,128)S(1)}, f32[4,4,4,128]{3,2,1,0:T(4,128)S(1)}, bf16[4,4,4,128,128]{...) while((s32[]{:T(128)}, f32[4,4,128]{2,1,0:T(4,128)S(1)}, ...), condition=%wide.region_39.40_spmd, body=%wide.region_38.39_spmd.sunk | while | flops 6295555 | bytes 655669 | solution.py:104
  181.5 14.8 %collective-permute-start.20 = (f32[4,1,4,128]{3,2,1,0:T(4,128)S(1)}, f32[4,1,4,128]{3,2,1,0:T(4,128)S(1)}, u32[]{:S(2)}, u32[]{:S(2)}) collective-permute-start(f32[4,1,4,128]{3,2,1,0:T(4,128)S(1)} %get-tuple-element.1740), channel_id=1, source_target_pairs={{0,16},{16,32},{32,48},{48,64},{64,80},{80,96},{96,112},{1,17},{17... | collective-permute-start | bytes 24584 | tf_op jit(solution)/shard_map/ppermute | solution.py:20
  196.3 1.9 collective-permute-start.21
  198.3 4.4 %collective-permute-start.22 = (f32[4,4,1,128]{3,2,1,0:T(1,128)S(1)}, f32[4,4,1,128]{3,2,1,0:T(1,128)S(1)}, u32[]{:S(2)}, u32[]{:S(2)}) collective-permute-start(f32[4,4,1,128]{3,2,1,0:T(1,128)S(1)} %get-tuple-element.1738), channel_id=1, source_target_pairs={{0,1},{1,2},{2,3},{3,4},{4,5},{5,6},{6,7},{7,8},{8,9},{9,10},{10,1... | collective-permute-start | bytes 24584 | tf_op jit(solution)/shard_map/ppermute | solution.py:20
  202.7 1.3 collective-permute-start.23
  208.6 15.1 %all_to_all.10 = f32[16,1,512]{2,1,0:T(1,128)S(1)} all-to-all(f32[16,1,512]{2,1,0:T(1,128)S(1)} %reshape.146), channel_id=1, replica_groups=mesh['line'=4,'tx'=8,'ty'=16] {'ty'}, dimensions={0} | all-to-all | bytes 65536 | tf_op jit(solution)/shard_map/all_to_all | solution.py:45
  226.5 3.5 %all-to-all-start.1 = ((f32[16,1,512]{2,1,0:T(1,128)}), f32[16,1,512]{2,1,0:T(1,128)S(1)}, u32[]{:S(2)}, u32[]{:S(2)}) async-start(f32[16,1,512]{2,1,0:T(1,128)} %reshape.148), calls=%async_computation.1 | async-start | bytes 65536 | tf_op jit(solution)/shard_map/all_to_all | solution.py:51
  230.7 5.6 %all-to-all-done.1 = f32[16,1,512]{2,1,0:T(1,128)S(1)} async-done(((f32[16,1,512]{2,1,0:T(1,128)}), f32[16,1,512]{2,1,0:T(1,128)S(1)}, u32[]{:S(2)}, u32[]{:S(2)}) %all-to-all-start.1) | async-done | bytes 32800 | tf_op jit(solution)/shard_map/all_to_all | solution.py:51
  (379 shorter events, 102.0 us)
Async XLA Ops:
  0.6 20.6 %copy-start = (f32[4,128,128]{2,1,0:T(8,128)S(1)}, f32[4,128,128]{2,1,0:T(8,128)}, u32[]{:S(2)}) copy-start(f32[4,128,128]{2,1,0:T(8,128)} %param.52) | copy-start | bytes 786436
  1.4 19.8 %collective-permute-start = (f32[4,1,4,128]{3,2,1,0:T(4,128)S(1)}, f32[4,1,4,128]{3,2,1,0:T(4,128)S(1)}, u32[]{:S(2)}, u32[]{:S(2)}) collective-permute-start(f32[4,1,4,128]{3,2,1,0:T(4,128)S(1)} %get-tuple-element.1753), channel_id=1, source_target_pairs={{0,16},{16,32},{32,48},{48,64},{64,80},{80,96},{96,112},{1,17},{17... | collective-permute-start | bytes 24584 | tf_op jit(solution)/shard_map/ppermute | solution.py:20
  11.6 11.8 %collective-permute-start.1 = (f32[4,1,4,128]{3,2,1,0:T(4,128)S(1)}, f32[4,1,4,128]{3,2,1,0:T(4,128)S(1)}, u32[]{:S(2)}, u32[]{:S(2)}) collective-permute-start(f32[4,1,4,128]{3,2,1,0:T(4,128)S(1)} %get-tuple-element.1752), channel_id=1, source_target_pairs={{16,0},{32,16},{48,32},{64,48},{80,64},{96,80},{112,96},{17,1},{33... | collective-permute-start | bytes 24584 | tf_op jit(solution)/shard_map/ppermute | solution.py:21
  14.4 10.2 %collective-permute-start.3 = (f32[4,4,1,128]{3,2,1,0:T(1,128)S(1)}, f32[4,4,1,128]{3,2,1,0:T(1,128)S(1)}, u32[]{:S(2)}, u32[]{:S(2)}) collective-permute-start(f32[4,4,1,128]{3,2,1,0:T(1,128)S(1)} %get-tuple-element.1751), channel_id=1, source_target_pairs={{1,0},{2,1},{3,2},{4,3},{5,4},{6,5},{7,6},{8,7},{9,8},{10,9},{11,1... | collective-permute-start | bytes 24584 | tf_op jit(solution)/shard_map/ppermute | solution.py:21
  15.7 9.4 %collective-permute-start.2 = (f32[4,4,1,128]{3,2,1,0:T(1,128)S(1)}, f32[4,4,1,128]{3,2,1,0:T(1,128)S(1)}, u32[]{:S(2)}, u32[]{:S(2)}) collective-permute-start(f32[4,4,1,128]{3,2,1,0:T(1,128)S(1)} %get-tuple-element.1750), channel_id=1, source_target_pairs={{0,1},{1,2},{2,3},{3,4},{4,5},{5,6},{6,7},{7,8},{8,9},{9,10},{10,1... | collective-permute-start | bytes 24584 | tf_op jit(solution)/shard_map/ppermute | solution.py:20
  20.5 5.0 %copy-start.7 = (f32[4,4,4,128]{3,2,1,0:T(4,128)S(1)}, f32[4,4,4,128]{3,2,1,0:T(4,128)}, u32[]{:S(2)}) copy-start(f32[4,4,4,128]{3,2,1,0:T(4,128)} %param.45) | copy-start | bytes 98308
  21.3 4.4 %copy-start.1 = (bf16[4,4,4,128,128]{4,3,2,1,0:T(8,128)(2,1)S(1)}, bf16[4,4,4,128,128]{4,3,2,1,0:T(8,128)(2,1)}, u32[]{:S(2)}) copy-start(bf16[4,4,4,128,128]{4,3,2,1,0:T(8,128)(2,1)} %param.47) | copy-start | bytes 6291460
  21.3 4.4 %copy-start.2 = (f32[128,128]{1,0:T(8,128)S(1)}, f32[128,128]{1,0:T(8,128)}, u32[]{:S(2)}) copy-start(f32[128,128]{1,0:T(8,128)} %param.50) | copy-start | bytes 196612
  21.3 4.4 %copy-start.4 = (f32[4,4,4]{2,1,0:T(4,128)S(1)}, f32[4,4,4]{2,1,0:T(4,128)}, u32[]{:S(2)}) copy-start(f32[4,4,4]{2,1,0:T(4,128)} %param.48) | copy-start | bytes 772
  30.5 4.3 %collective-permute-start.4 = (f32[4,4,128]{2,1,0:T(4,128)S(1)}, f32[4,4,128]{2,1,0:T(4,128)S(1)}, u32[]{:S(2)}, u32[]{:S(2)}) collective-permute-start(f32[4,4,128]{2,1,0:T(4,128)S(1)} %slice_bitcast_fusion.11), channel_id=1, source_target_pairs={{0,128},{128,256},{256,384},{1,129},{129,257},{257,385},{2,130},{1... | collective-permute-start | bytes 24584 | tf_op jit(solution)/shard_map/ppermute | solution.py:35
  39.5 4.4 %collective-permute-start.5 = (f32[4,4,128]{2,1,0:T(4,128)S(1)}, f32[4,4,128]{2,1,0:T(4,128)S(1)}, u32[]{:S(2)}, u32[]{:S(2)}) collective-permute-start(f32[4,4,128]{2,1,0:T(4,128)S(1)} %slice_bitcast_fusion.10), channel_id=1, source_target_pairs={{0,128},{128,256},{256,384},{1,129},{129,257},{257,385},{2,130},{1... | collective-permute-start | bytes 24584 | tf_op jit(solution)/shard_map/ppermute | solution.py:35
  48.6 9.3 %copy-start.3 = (f32[128,128]{1,0:T(8,128)S(1)}, f32[128,128]{1,0:T(8,128)}, u32[]{:S(2)}) copy-start(f32[128,128]{1,0:T(8,128)} %param.51) | copy-start | bytes 196612
  48.6 9.3 %copy-start.5 = (f32[4,4,4]{2,1,0:T(4,128)S(1)}, f32[4,4,4]{2,1,0:T(4,128)}, u32[]{:S(2)}) copy-start(f32[4,4,4]{2,1,0:T(4,128)} %param.49) | copy-start | bytes 772
  48.7 4.5 %collective-permute-start.6 = (f32[4,4,128]{2,1,0:T(4,128)S(1)}, f32[4,4,128]{2,1,0:T(4,128)S(1)}, u32[]{:S(2)}, u32[]{:S(2)}) collective-permute-start(f32[4,4,128]{2,1,0:T(4,128)S(1)} %slice_bitcast_fusion.9), channel_id=1, source_target_pairs={{0,128},{128,256},{256,384},{1,129},{129,257},{257,385},{2,130},{1... | collective-permute-start | bytes 24584 | tf_op jit(solution)/shard_map/ppermute | solution.py:35
  62.8 4.7 %collective-permute-start.7 = (f32[4,4,128]{2,1,0:T(4,128)S(1)}, f32[4,4,128]{2,1,0:T(4,128)S(1)}, u32[]{:S(2)}, u32[]{:S(2)}) collective-permute-start(f32[4,4,128]{2,1,0:T(4,128)S(1)} %slice_bitcast_fusion.8), channel_id=1, source_target_pairs={{128,0},{256,128},{384,256},{129,1},{257,129},{385,257},{130,2},{2... | collective-permute-start | bytes 24584 | tf_op jit(solution)/shard_map/ppermute | solution.py:35
  72.3 4.8 %collective-permute-start.8 = (f32[4,4,128]{2,1,0:T(4,128)S(1)}, f32[4,4,128]{2,1,0:T(4,128)S(1)}, u32[]{:S(2)}, u32[]{:S(2)}) collective-permute-start(f32[4,4,128]{2,1,0:T(4,128)S(1)} %slice_bitcast_fusion.7), channel_id=1, source_target_pairs={{128,0},{256,128},{384,256},{129,1},{257,129},{385,257},{130,2},{2... | collective-permute-start | bytes 24584 | tf_op jit(solution)/shard_map/ppermute | solution.py:35
  82.0 4.4 %collective-permute-start.9 = (f32[4,4,128]{2,1,0:T(4,128)S(1)}, f32[4,4,128]{2,1,0:T(4,128)S(1)}, u32[]{:S(2)}, u32[]{:S(2)}) collective-permute-start(f32[4,4,128]{2,1,0:T(4,128)S(1)} %slice_bitcast_fusion.6), channel_id=1, source_target_pairs={{128,0},{256,128},{384,256},{129,1},{257,129},{385,257},{130,2},{2... | collective-permute-start | bytes 24584 | tf_op jit(solution)/shard_map/ppermute | solution.py:35
  91.2 20.7 %collective-permute-start.10 = (f32[4,1,4,128]{3,2,1,0:T(4,128)S(1)}, f32[4,1,4,128]{3,2,1,0:T(4,128)S(1)}, u32[]{:S(2)}, u32[]{:S(2)}) collective-permute-start(f32[4,1,4,128]{3,2,1,0:T(4,128)S(1)} %get-tuple-element.1745), channel_id=1, source_target_pairs={{0,16},{16,32},{32,48},{48,64},{64,80},{80,96},{96,112},{1,17},{17... | collective-permute-start | bytes 24584 | tf_op jit(solution)/shard_map/ppermute | solution.py:20
  105.6 8.9 %collective-permute-start.11 = (f32[4,1,4,128]{3,2,1,0:T(4,128)S(1)}, f32[4,1,4,128]{3,2,1,0:T(4,128)S(1)}, u32[]{:S(2)}, u32[]{:S(2)}) collective-permute-start(f32[4,1,4,128]{3,2,1,0:T(4,128)S(1)} %get-tuple-element.1744), channel_id=1, source_target_pairs={{16,0},{32,16},{48,32},{64,48},{80,64},{96,80},{112,96},{17,1},{33... | collective-permute-start | bytes 24584 | tf_op jit(solution)/shard_map/ppermute | solution.py:21
  107.5 7.4 %collective-permute-start.12 = (f32[4,4,1,128]{3,2,1,0:T(1,128)S(1)}, f32[4,4,1,128]{3,2,1,0:T(1,128)S(1)}, u32[]{:S(2)}, u32[]{:S(2)}) collective-permute-start(f32[4,4,1,128]{3,2,1,0:T(1,128)S(1)} %get-tuple-element.1742), channel_id=1, source_target_pairs={{0,1},{1,2},{2,3},{3,4},{4,5},{5,6},{6,7},{7,8},{8,9},{9,10},{10,1... | collective-permute-start | bytes 24584 | tf_op jit(solution)/shard_map/ppermute | solution.py:20
  110.6 4.7 %collective-permute-start.13 = (f32[4,4,1,128]{3,2,1,0:T(1,128)S(1)}, f32[4,4,1,128]{3,2,1,0:T(1,128)S(1)}, u32[]{:S(2)}, u32[]{:S(2)}) collective-permute-start(f32[4,4,1,128]{3,2,1,0:T(1,128)S(1)} %get-tuple-element.1743), channel_id=1, source_target_pairs={{1,0},{2,1},{3,2},{4,3},{5,4},{6,5},{7,6},{8,7},{9,8},{10,9},{11,1... | collective-permute-start | bytes 24584 | tf_op jit(solution)/shard_map/ppermute | solution.py:21
  120.7 4.4 %collective-permute-start.14 = (f32[4,4,128]{2,1,0:T(4,128)S(1)}, f32[4,4,128]{2,1,0:T(4,128)S(1)}, u32[]{:S(2)}, u32[]{:S(2)}) collective-permute-start(f32[4,4,128]{2,1,0:T(4,128)S(1)} %slice_bitcast_fusion.5), channel_id=1, source_target_pairs={{0,128},{128,256},{256,384},{1,129},{129,257},{257,385},{2,130},{1... | collective-permute-start | bytes 24584 | tf_op jit(solution)/shard_map/ppermute | solution.py:35
  129.9 4.4 %collective-permute-start.15 = (f32[4,4,128]{2,1,0:T(4,128)S(1)}, f32[4,4,128]{2,1,0:T(4,128)S(1)}, u32[]{:S(2)}, u32[]{:S(2)}) collective-permute-start(f32[4,4,128]{2,1,0:T(4,128)S(1)} %slice_bitcast_fusion.4), channel_id=1, source_target_pairs={{0,128},{128,256},{256,384},{1,129},{129,257},{257,385},{2,130},{1... | collective-permute-start | bytes 24584 | tf_op jit(solution)/shard_map/ppermute | solution.py:35
  139.0 4.4 %collective-permute-start.16 = (f32[4,4,128]{2,1,0:T(4,128)S(1)}, f32[4,4,128]{2,1,0:T(4,128)S(1)}, u32[]{:S(2)}, u32[]{:S(2)}) collective-permute-start(f32[4,4,128]{2,1,0:T(4,128)S(1)} %slice_bitcast_fusion.3), channel_id=1, source_target_pairs={{0,128},{128,256},{256,384},{1,129},{129,257},{257,385},{2,130},{1... | collective-permute-start | bytes 24584 | tf_op jit(solution)/shard_map/ppermute | solution.py:35
  153.0 4.7 %collective-permute-start.17 = (f32[4,4,128]{2,1,0:T(4,128)S(1)}, f32[4,4,128]{2,1,0:T(4,128)S(1)}, u32[]{:S(2)}, u32[]{:S(2)}) collective-permute-start(f32[4,4,128]{2,1,0:T(4,128)S(1)} %slice_bitcast_fusion.2), channel_id=1, source_target_pairs={{128,0},{256,128},{384,256},{129,1},{257,129},{385,257},{130,2},{2... | collective-permute-start | bytes 24584 | tf_op jit(solution)/shard_map/ppermute | solution.py:35
  162.5 11.1 %copy-start.9 = (s32[4,4,4]{2,1,0:T(4,128)S(1)}, s32[4,4,4]{2,1,0:T(4,128)}, u32[]{:S(2)}) copy-start(s32[4,4,4]{2,1,0:T(4,128)} %param.55) | copy-start | bytes 772
  162.5 4.6 %collective-permute-start.18 = (f32[4,4,128]{2,1,0:T(4,128)S(1)}, f32[4,4,128]{2,1,0:T(4,128)S(1)}, u32[]{:S(2)}, u32[]{:S(2)}) collective-permute-start(f32[4,4,128]{2,1,0:T(4,128)S(1)} %slice_bitcast_fusion.1), channel_id=1, source_target_pairs={{128,0},{256,128},{384,256},{129,1},{257,129},{385,257},{130,2},{2... | collective-permute-start | bytes 24584 | tf_op jit(solution)/shard_map/ppermute | solution.py:35
  171.9 4.7 %collective-permute-start.19 = (f32[4,4,128]{2,1,0:T(4,128)S(1)}, f32[4,4,128]{2,1,0:T(4,128)S(1)}, u32[]{:S(2)}, u32[]{:S(2)}) collective-permute-start(f32[4,4,128]{2,1,0:T(4,128)S(1)} %slice_bitcast_fusion), channel_id=1, source_target_pairs={{128,0},{256,128},{384,256},{129,1},{257,129},{385,257},{130,2},{2... | collective-permute-start | bytes 24584 | tf_op jit(solution)/shard_map/ppermute | solution.py:35
  181.4 26.4 %copy-start.8 = (f32[32,128]{1,0:T(8,128)S(1)}, f32[32,128]{1,0:T(8,128)}, u32[]{:S(2)}) copy-start(f32[32,128]{1,0:T(8,128)} %param.56) | copy-start | bytes 49156
  181.5 22.5 %collective-permute-start.20 = (f32[4,1,4,128]{3,2,1,0:T(4,128)S(1)}, f32[4,1,4,128]{3,2,1,0:T(4,128)S(1)}, u32[]{:S(2)}, u32[]{:S(2)}) collective-permute-start(f32[4,1,4,128]{3,2,1,0:T(4,128)S(1)} %get-tuple-element.1740), channel_id=1, source_target_pairs={{0,16},{16,32},{32,48},{48,64},{64,80},{80,96},{96,112},{1,17},{17... | collective-permute-start | bytes 24584 | tf_op jit(solution)/shard_map/ppermute | solution.py:20
  196.3 8.9 %collective-permute-start.21 = (f32[4,1,4,128]{3,2,1,0:T(4,128)S(1)}, f32[4,1,4,128]{3,2,1,0:T(4,128)S(1)}, u32[]{:S(2)}, u32[]{:S(2)}) collective-permute-start(f32[4,1,4,128]{3,2,1,0:T(4,128)S(1)} %get-tuple-element.1741), channel_id=1, source_target_pairs={{16,0},{32,16},{48,32},{64,48},{80,64},{96,80},{112,96},{17,1},{33... | collective-permute-start | bytes 24584 | tf_op jit(solution)/shard_map/ppermute | solution.py:21
  198.3 7.4 %collective-permute-start.22 = (f32[4,4,1,128]{3,2,1,0:T(1,128)S(1)}, f32[4,4,1,128]{3,2,1,0:T(1,128)S(1)}, u32[]{:S(2)}, u32[]{:S(2)}) collective-permute-start(f32[4,4,1,128]{3,2,1,0:T(1,128)S(1)} %get-tuple-element.1738), channel_id=1, source_target_pairs={{0,1},{1,2},{2,3},{3,4},{4,5},{5,6},{6,7},{7,8},{8,9},{9,10},{10,1... | collective-permute-start | bytes 24584 | tf_op jit(solution)/shard_map/ppermute | solution.py:20
  202.7 4.7 %collective-permute-start.23 = (f32[4,4,1,128]{3,2,1,0:T(1,128)S(1)}, f32[4,4,1,128]{3,2,1,0:T(1,128)S(1)}, u32[]{:S(2)}, u32[]{:S(2)}) collective-permute-start(f32[4,4,1,128]{3,2,1,0:T(1,128)S(1)} %get-tuple-element.1739), channel_id=1, source_target_pairs={{1,0},{2,1},{3,2},{4,3},{5,4},{6,5},{7,6},{8,7},{9,8},{10,9},{11,1... | collective-permute-start | bytes 24584 | tf_op jit(solution)/shard_map/ppermute | solution.py:21
  204.4 20.8 %copy-start.6 = (f32[1,1,16,32,32]{4,3,2,1,0:T(8,128)S(1)}, f32[1,1,16,32,32]{4,3,2,1,0:T(8,128)}, u32[]{:S(2)}) copy-start(f32[1,1,16,32,32]{4,3,2,1,0:T(8,128)} %param.57) | copy-start | bytes 196612
  226.5 9.9 %all-to-all-start.1 = ((f32[16,1,512]{2,1,0:T(1,128)}), f32[16,1,512]{2,1,0:T(1,128)S(1)}, u32[]{:S(2)}, u32[]{:S(2)}) async-start(f32[16,1,512]{2,1,0:T(1,128)} %reshape.148), calls=%async_computation.1 | async-start | bytes 65536 | tf_op jit(solution)/shard_map/all_to_all | solution.py:51
where the time goes:
time: 241 us; the launch traced here: 238 us
  starting transfers between devices  93.7 us (39%)
  matrix products  82 us (34%)
  waiting for transfers between devices  33.7 us (14%)
  blocking collectives  15.1 us (6%)
  local copies, waits for them, and re-layouts  6.9 us (3%)
  other arithmetic  3.91 us (2%)
    ppermute x6, starting transfers between devices, with_halo(): lax.ppermute(last, axis, up)  50.8 us
    ppermute x12, starting transfers between devices, from_behind(): lax.ppermute(value, axis, [(source, source + steps) for source in range(l...  29.7 us
    dot_general x32, matrix products, backward_step(): jnp.einsum('xycb,xyb->xyc', inverse.astype(jnp.float32), inner, precision...  29.3 us
    dot_general x32, matrix products, forward_step(): jnp.einsum('xycb,xyb->xyc', inverse.astype(jnp.float32), inner, precision...  29.3 us
    ppermute x12, waiting for transfers between devices, from_behind(): lax.ppermute(value, axis, [(source, source + steps) for source in range(l...  23.9 us
    all_to_all x1, blocking collectives, summed_on_arrival(): parts = lax.all_to_all(split_up(array, dim, count), axis, 0, 0, tiled=True)  15.1 us
    ppermute x6, starting transfers between devices, with_halo(): lax.ppermute(leading, axis, [(b, a) for a, b in up])  9.64 us
    dot_general x32, matrix products, forward_step(): jnp.einsum('cb,xyb->xyc', lower_block, carry, precision=highest)  7.73 us
  transfers between devices with their start and end apart: 25, of which 16 were waited for; matrix products, arithmetic and copies ran while one was open for 4% of the time, Pallas kernels for 0%

commit v1 on v0

v1 whole, which is shorter than its diff:
```python
import functools

import jax
import jax.numpy as jnp
from jax import lax
from jax.experimental import pallas as pl
from jax.experimental.pallas import tpu as pltpu
from jax.sharding import PartitionSpec as P

SWEEPS = 2
F32 = jnp.float32
BF16 = jnp.bfloat16
SPEC = pl.BlockSpec(memory_space=pltpu.VMEM)


def call(kernel, outs, *args, scratch=()):
    return pl.pallas_call(
        kernel,
        in_specs=[SPEC] * len(args),
        out_specs=[SPEC] * len(outs),
        out_shape=[pltpu.VMEM(s, d) for s, d in outs],
        scratch_shapes=list(scratch),
    )(*[pltpu.with_memory_space_constraint(a, pltpu.VMEM) for a in args])


def halves(v):
    hi = v.astype(BF16)
    return hi, (v - hi.astype(F32)).astype(BF16)


def nt(a, b):
    return lax.dot_general(a, b, (((1,), (1,)), ((), ())), preferred_element_type=F32)


def nn(a, b):
    return lax.dot_general(a, b, (((1,), (0,)), ((), ())), preferred_element_type=F32)


def times(v, m, dot=nt):
    n = v.shape[0]
    hi, lo = halves(v)
    both = dot(jnp.concatenate([hi, lo], 0), m[0])
    return both[:n] + both[n:] + dot(hi, m[1])


def each_line(v, weights, lines):
    hi, lo = halves(v)
    out = nt(jnp.concatenate([hi, lo], 0), weights)
    row = lax.broadcasted_iota(jnp.int32, (2 * lines, 128), 0)
    row = jnp.where(row >= lines, row - lines, row)
    acc = jnp.zeros((2 * lines, 128), F32)
    for l in range(lines):
        acc = acc + jnp.where(row == l, out[:, l * 128 : (l + 1) * 128], 0.0)
    return acc[:lines] + acc[lines:]


def forward(g, inc, w_ref, low, cols, n, lines):
    carry, ys = inc, []
    for i in range(n):
        at = slice(i * lines, (i + 1) * lines)
        inner = g[at] - cols[at, 16:17] * times(carry, low)
        carry = each_line(inner, w_ref[i * lines * 128 : (i + 1) * lines * 128, :], lines)
        ys.append(carry)
    return ys


def backward(y, arr, w_ref, upp, cols, n, lines):
    carry, xs = arr, [None] * n
    for i in reversed(range(n)):
        at = slice(i * lines, (i + 1) * lines)
        inner = cols[at, 17:18] * times(carry, upp)
        carry = y[at] - each_line(inner, w_ref[i * lines * 128 : (i + 1) * lines * 128, :], lines)
        xs[i] = carry
    return xs


def put_edges(x_ref, par_ref, outs, n, lx, ly):
    a_ref, b_ref, c_ref, d_ref = outs
    lines = lx * ly
    first = jnp.concatenate([x_ref[i * lines : i * lines + ly, :] for i in range(n)], 0)
    last = jnp.concatenate([x_ref[(i + 1) * lines - ly : (i + 1) * lines, :] for i in range(n)], 0)
    even = par_ref[0:1, :] < 0.5
    a_ref[...] = jnp.where(even, last, first)
    b_ref[...] = jnp.where(even, first, last)
    first = x_ref[pl.ds(0, n * lx, stride=ly), :]
    last = x_ref[pl.ds(ly - 1, n * lx, stride=ly), :]
    even = par_ref[1:2, :] < 0.5
    c_ref[...] = jnp.where(even, last, first)
    d_ref[...] = jnp.where(even, first, last)


def tangential(x_ref, got, par_ref, cols, blocks, near, n, lx, ly):
    lines = lx * ly
    x = x_ref[...]
    even = par_ref[0:1, :] < 0.5
    a, b, c, d = (r[...] for r in got)
    below, above = jnp.where(even, b, a), jnp.where(even, a, b)
    near[0] = pltpu.roll(x, ly, 0)
    near[1] = pltpu.roll(x, n * lines - ly, 0)
    for i in range(n):
        near[0, i * lines : i * lines + ly, :] = below[i * ly : (i + 1) * ly]
        near[1, (i + 1) * lines - ly : (i + 1) * lines, :] = above[i * ly : (i + 1) * ly]
    even = par_ref[1:2, :] < 0.5
    below, above = jnp.where(even, d, c), jnp.where(even, c, d)
    row = lax.broadcasted_iota(jnp.int32, x.shape, 0) % ly
    near[2] = pltpu.roll(x, 1, 0)
    near[3] = pltpu.roll(x, n * lines - 1, 0)
    for q in range(n * lx):
        near[2, q * ly : q * ly + 1, :] = below[q : q + 1]
        near[3, q * ly + ly - 1 : q * ly + ly, :] = above[q : q + 1]
    total = jnp.zeros(x.shape, F32)
    beside = [near[s] for s in range(4)]
    for k in range(4):
        mixed = sum(cols[:, 4 * s + k : 4 * s + k + 1] * beside[s] for s in range(4))
        total = total + times(mixed, (blocks[0][k], blocks[1][k]))
    return total


def swaps(count, start):
    return [
        pair
        for i in range(start, count - 1, 2)
        for pair in ((i, i + 1), (i + 1, i))
    ]


def exchange(sends):
    nx, ny = lax.axis_size("tx"), lax.axis_size("ty")
    a, b, c, d = sends
    return (
        lax.ppermute(a, "tx", swaps(nx, 0)),
        lax.ppermute(b, "tx", swaps(nx, 1)),
        lax.ppermute(c, "ty", swaps(ny, 0)),
        lax.ppermute(d, "ty", swaps(ny, 1)),
    )


def body(
    right_side,
    start_field,
    line_inverse,
    lower_scale,
    upper_scale,
    lower_block,
    upper_block,
    face_blocks,
    face_kind,
    face_scale,
    agglomerate,
    restriction,
    coarse_inverse,
):
    n, lx, ly, width = right_side.shape
    lines, rows, cb = lx * ly, n * lx * ly, restriction.shape[0]
    quarter = width // cb
    segments, owners = lax.axis_size("line"), lax.axis_size("ty")
    owned_rows = coarse_inverse.shape[2] // quarter
    agg_rows = owned_rows * owners
    rhs = right_side.reshape(rows, width)
    start = start_field.reshape(rows, width)
    w = line_inverse.reshape(rows * width, width)

    kinds = jnp.arange(4, dtype=jnp.int32)
    face = jnp.where(face_kind[:, None] == kinds[None, :, None, None, None], face_scale[:, None], 0.0)
    agg = agglomerate.reshape(rows)
    agg_row, agg_part = agg // quarter, agg % quarter
    cols = jnp.concatenate(
        [
            face.reshape(16, rows),
            lower_scale.reshape(1, rows),
            upper_scale.reshape(1, rows),
            agg_row.astype(F32)[None],
            agg_part.astype(F32)[None],
            jnp.zeros((12, rows), F32),
        ],
        0,
    ).T
    agg_lane = jnp.broadcast_to(agg_row.astype(F32)[None], (8, rows))
    par = jnp.stack([lax.axis_index("tx") % 2, lax.axis_index("ty") % 2]).astype(F32)
    par = jnp.broadcast_to(jnp.pad(par, (0, 6))[:, None], (8, width))
    eye = jnp.eye(quarter, dtype=F32)
    ci = coarse_inverse.reshape(owned_rows, quarter, cb, 1, cb) * eye[None, :, None, :, None]
    ci = ci.reshape(owned_rows * width, width)
    spread_op = jnp.tile(restriction, (quarter, 1))

    block, edge = ((rows, width), F32), ((lines, width), F32)
    half, half4 = ((width, width), BF16), ((4, width, width), BF16)
    edges4 = [((n * ly, width), F32)] * 2 + [((n * lx, width), F32)] * 2

    def prepare(x_ref, par_ref, l_ref, u_ref, f_ref, r_ref, c_ref, *outs):
        put_edges(x_ref, par_ref, outs[:4], n, lx, ly)
        for src, k in ((l_ref, 4), (u_ref, 6), (f_ref, 8), (r_ref, 10), (c_ref, 12)):
            outs[k][...], outs[k + 1][...] = halves(src[...])

    made = call(
        prepare,
        edges4
        + [half, half, half, half, half4, half4, half, half]
        + [((owned_rows * width, width), BF16)] * 2,
        start,
        par,
        lower_block,
        upper_block,
        face_blocks,
        spread_op,
        ci,
    )
    sends, lh, ll, uh, ul, fh, fl, rh, rl, ch, cl = made[:4], *made[4:]

    def open_forward(x_ref, a, b, c, d, par_ref, cols_ref, fh_ref, fl_ref, rhs_ref, lh_ref, ll_ref, w_ref, g_ref, y_ref, f_ref, near):
        cols = cols_ref[...]
        total = tangential(x_ref, (a, b, c, d), par_ref, cols, (fh_ref, fl_ref), near, n, lx, ly)
        g = rhs_ref[...] - total
        g_ref[...] = g
        zero = jnp.zeros((lines, width), F32)
        ys = forward(g, zero, w_ref, (lh_ref[...], ll_ref[...]), cols, n, lines)
        y_ref[...] = jnp.concatenate(ys, 0)
        f_ref[...] = ys[-1]

    def next_forward(g_ref, inc_ref, got_ref, cols_ref, lh_ref, ll_ref, w_ref, sum_ref, f_ref):
        inc = inc_ref[...] + got_ref[...]
        sum_ref[...] = inc
        ys = forward(g_ref[...], inc, w_ref, (lh_ref[...], ll_ref[...]), cols_ref[...], n, lines)
        f_ref[...] = ys[-1]

    def turn(g_ref, inc_ref, got_ref, cols_ref, lh_ref, ll_ref, uh_ref, ul_ref, w_ref, y_ref, x_ref):
        cols = cols_ref[...]
        inc = inc_ref[...] + got_ref[...]
        ys = forward(g_ref[...], inc, w_ref, (lh_ref[...], ll_ref[...]), cols, n, lines)
        y = jnp.concatenate(ys, 0)
        y_ref[...] = y
        zero = jnp.zeros((lines, width), F32)
        xs = backward(y, zero, w_ref, (uh_ref[...], ul_ref[...]), cols, n, lines)
        x_ref[...] = xs[0]

    def next_backward(y_ref, arr_ref, got_ref, cols_ref, uh_ref, ul_ref, w_ref, sum_ref, x_ref):
        arr = arr_ref[...] + got_ref[...]
        sum_ref[...] = arr
        xs = backward(y_ref[...], arr, w_ref, (uh_ref[...], ul_ref[...]), cols_ref[...], n, lines)
        x_ref[...] = xs[0]

    def close_backward(last, y_ref, arr_ref, got_ref, prev_ref, par_ref, cols_ref, uh_ref, ul_ref, w_ref, x_ref, d_ref, *outs):
        arr = arr_ref[...] + got_ref[...]
        xs = backward(y_ref[...], arr, w_ref, (uh_ref[...], ul_ref[...]), cols_ref[...], n, lines)
        x = jnp.concatenate(xs, 0)
        x_ref[...] = x
        d_ref[...] = prev_ref[...] - x
        put_edges(d_ref if last else x_ref, par_ref, outs, n, lx, ly)

    field = start
    change = None
    for sweep in range(SWEEPS):
        got = exchange(sends)
        g, y, ahead = call(
            open_forward,
            [block, block, edge],
            field, *got, par, cols, fh, fl, rhs, lh, ll, w,
            scratch=[pltpu.VMEM((4, rows, width), F32)],
        )
        inc = jnp.zeros((lines, width), F32)
        for k in range(segments - 2):
            recv = lax.ppermute(ahead, "line", [(k, k + 1)])
            inc, ahead = call(next_forward, [edge, edge], g, inc, recv, cols, lh, ll, w)
        recv = lax.ppermute(ahead, "line", [(segments - 2, segments - 1)])
        y, behind = call(turn, [block, edge], g, inc, recv, cols, lh, ll, uh, ul, w)
        arr = jnp.zeros((lines, width), F32)
        for k in range(segments - 2):
            recv = lax.ppermute(behind, "line", [(segments - 1 - k, segments - 2 - k)])
            arr, behind = call(next_backward, [edge, edge], y, arr, recv, cols, uh, ul, w)
        recv = lax.ppermute(behind, "line", [(1, 0)])
        out = call(
            functools.partial(close_backward, sweep == SWEEPS - 1),
            [block, block] + edges4,
            y, arr, recv, field, par, cols, uh, ul, w,
        )
        field, change, sends = out[0], out[1], out[2:]

    got = exchange(sends)

    def restrict(x_ref, a, b, c, d, par_ref, cols_ref, fh_ref, fl_ref, rh_ref, rl_ref, lane_ref, res_ref, part_ref, near):
        cols = cols_ref[...]
        res = tangential(x_ref, (a, b, c, d), par_ref, cols, (fh_ref, fl_ref), near, n, lx, ly)
        res_ref[...] = res
        proj = times(res, (rh_ref[...], rl_ref[...]))
        part = lax.broadcasted_iota(jnp.int32, (rows, width), 1) // cb
        proj = jnp.where(part.astype(F32) == cols[:, 19:20], proj, 0.0)
        hit = lax.broadcasted_iota(jnp.int32, (agg_rows, rows), 0).astype(F32)
        hit = jnp.where(hit == lane_ref[0:1, :], 1.0, 0.0).astype(BF16)
        hi, lo = halves(proj)
        part_ref[...] = nn(hit, hi) + nn(hit, lo)

    residual, partial = call(
        restrict,
        [block, ((agg_rows, width), F32)],
        change, *got, par, cols, fh, fl, rh, rl, agg_lane,
        scratch=[pltpu.VMEM((4, rows, width), F32)],
    )
    parts = lax.all_to_all(partial.reshape(owners, owned_rows, width), "ty", 0, 0, tiled=True)

    def solve_coarse(parts_ref, ch_ref, cl_ref, up_ref):
        sums = parts_ref[0]
        for k in range(1, owners):
            sums = sums + parts_ref[k]
        hi, lo = halves(sums)
        zero = jnp.zeros((8 - owned_rows, width), BF16)
        hi, lo = jnp.concatenate([hi, zero], 0), jnp.concatenate([lo, zero], 0)
        both = jnp.concatenate([hi, lo], 0)
        out = nt(both, ch_ref[...])
        out = out[:8] + out[8:] + nt(both, cl_ref[...])[:8]
        row = lax.broadcasted_iota(jnp.int32, (8, width), 0)
        acc = jnp.zeros((8, width), F32)
        for k in range(owned_rows):
            acc = acc + jnp.where(row == k, out[:, k * width : (k + 1) * width], 0.0)
        for k in range(owners):
            up_ref[k] = acc[:owned_rows]

    (copies,) = call(solve_coarse, [((owners, owned_rows, width), F32)], parts, ch, cl)
    update = lax.all_to_all(copies, "ty", 0, 0, tiled=True)

    def correct(up_ref, x_ref, cols_ref, rh_ref, rl_ref, out_ref):
        cols = cols_ref[...]
        hit = lax.broadcasted_iota(jnp.int32, (rows, agg_rows), 1).astype(F32)
        hit = jnp.where(hit == cols[:, 18:19], 1.0, 0.0).astype(BF16)
        hi, lo = halves(up_ref[...])
        picked = nn(hit, hi) + nn(hit, lo)
        part = lax.broadcasted_iota(jnp.int32, (rows, width), 1) // cb
        picked = jnp.where(part.astype(F32) == cols[:, 19:20], picked, 0.0)
        out_ref[...] = x_ref[...] + times(picked, (rh_ref[...], rl_ref[...]), nn)

    (corrected,) = call(correct, [block], update.reshape(agg_rows, width), field, cols, rh, rl)
    return corrected.reshape(right_side.shape), residual.reshape(right_side.shape)


def solution(mesh):
    in_specs = (
        P("line", "tx", "ty", None),
        P("line", "tx", "ty", None),
        P("line", "tx", "ty", None, None),
        P("line", "tx", "ty"),
        P("line", "tx", "ty"),
        P(),
        P(),
        P(),
        P(None, "line", "tx", "ty"),
        P(None, "line", "tx", "ty"),
        P("line", "tx", "ty"),
        P(),
        P("line", "tx", "ty", None, None),
    )
    out_specs = (P("line", "tx", "ty", None), P("line", "tx", "ty", None))
    return jax.shard_map(body, mesh=mesh, in_specs=in_specs, out_specs=out_specs, check_vma=False)
```

time: 241 us -> 171 us (0.71)
  matrix products: 82 us -> 0 us
  Pallas kernels: 0 us -> 28.4 us
  starting transfers between devices: 93.7 us -> 67.5 us
  local copies, waits for them, and re-layouts: 6.9 us -> 18.8 us
  blocking collectives: 15.1 us -> 18.5 us
  other arithmetic: 3.91 us -> 1.5 us
    dot_general x145 -> x0, matrix products: 82 us -> none  [the longest x32 29.3 us: backward_step(): jnp.einsum('xycb,xyb->xyc', inverse.astype(jnp.float32), inner, precision...]
    pallas_call x0 -> x18, Pallas kernels: none -> 28.4 us  [call(): pl.pallas_call(kernel, in_specs=[SPEC] * len(args), out_specs=[SPEC] * le...]
    ppermute x24, starting transfers between devices: 90.2 us -> 64 us  [the longest x3 20.4 us: exchange(): lax.ppermute(b, 'tx', swaps(nx, 1))]
    unnamed x28 -> x44, local copies, waits for them, and re-layouts: 1.88 us -> 17.2 us
    all_to_all x1, blocking collectives: 15.1 us -> 18.5 us  [body(): lax.all_to_all(partial.reshape(owners, owned_rows, width), 'ty', 0, 0, ti...]
    slice x7 -> x0, local copies, waits for them, and re-layouts: 2.41 us -> none  [the longest x4 0.89 us: with_halo(): last = lax.slice_in_dim(array, length - width, length, axis=dim)]
  transfers between devices with their start and end apart: 25 -> 25, of which waited for: 16 -> 8; matrix products, arithmetic and copies ran while one was open for 4% -> 1% of each run, Pallas kernels for 0% -> 0%
where the time goes in v1:
time: 171 us; the launch traced here: 170 us
  starting transfers between devices  67.5 us (39%)
  waiting for transfers between devices  33.7 us (20%)
  Pallas kernels  28.4 us (17%)
  local copies, waits for them, and re-layouts  18.8 us (11%)
  blocking collectives  18.5 us (11%)
    pallas_call x18, Pallas kernels, call(): pl.pallas_call(kernel, in_specs=[SPEC] * len(args), out_specs=[SPEC] * le...  28.4 us
    ppermute x2, waiting for transfers between devices, body(): recv = lax.ppermute(behind, 'line', [(1, 0)])  25 us
    ppermute x3, starting transfers between devices, exchange(): lax.ppermute(b, 'tx', swaps(nx, 1))  20.4 us
    all_to_all x1, blocking collectives, body(): lax.all_to_all(partial.reshape(owners, owned_rows, width), 'ty', 0, 0, ti...  18.5 us
    unnamed x44, local copies, waits for them, and re-layouts  17.2 us
    ppermute x3, starting transfers between devices, exchange(): lax.ppermute(c, 'ty', swaps(ny, 0))  15.8 us
    ppermute x3, starting transfers between devices, exchange(): lax.ppermute(a, 'tx', swaps(nx, 0))  13.4 us
    all_to_all x1, waiting for transfers between devices, body(): update = lax.all_to_all(copies, 'ty', 0, 0, tiled=True)  5.77 us
  transfers between devices with their start and end apart: 25, of which 8 were waited for; matrix products, arithmetic and copies ran while one was open for 1% of the time, Pallas kernels for 0%

profile of v1, /device:TPU:1, one launch (start us, length us, event | category | flops | bytes accessed | tf_op | source)
XLA Modules:
  0.0 169.6 jit_solution(4234197778332172106)
XLA Ops:
  0.8 1.4 broadcast_multiply_fusion
  2.9 8.7 %collective-permute-start = (f32[16,128]{1,0:T(8,128)S(1)}, f32[16,128]{1,0:T(8,128)S(1)}, u32[]{:S(2)}, u32[]{:S(2)}) collective-permute-start(f32[16,128]{1,0:T(8,128)S(1)} %get-tuple-element.53), channel_id=1, source_target_pairs={{0,16},{16,0},{32,48},{48,32},{64,80},{80,64},{96,112},{112,96},{1... | collective-permute-start | bytes 24584 | tf_op jit(solution)/shard_map/ppermute | solution.py:131
  11.7 3.4 %collective-permute-start.1 = (f32[16,128]{1,0:T(8,128)S(1)}, f32[16,128]{1,0:T(8,128)S(1)}, u32[]{:S(2)}, u32[]{:S(2)}) collective-permute-start(f32[16,128]{1,0:T(8,128)S(1)} %get-tuple-element.54), channel_id=1, source_target_pairs={{16,32},{32,16},{48,64},{64,48},{80,96},{96,80},{17,33},{33,17},{4... | collective-permute-start | bytes 24584 | tf_op jit(solution)/shard_map/ppermute | solution.py:132
  15.1 3.1 %collective-permute-start.2 = (f32[16,128]{1,0:T(8,128)S(1)}, f32[16,128]{1,0:T(8,128)S(1)}, u32[]{:S(2)}, u32[]{:S(2)}) collective-permute-start(f32[16,128]{1,0:T(8,128)S(1)} %get-tuple-element.55), channel_id=1, source_target_pairs={{0,1},{1,0},{2,3},{3,2},{4,5},{5,4},{6,7},{7,6},{8,9},{9,8},{10,11... | collective-permute-start | bytes 24584 | tf_op jit(solution)/shard_map/ppermute | solution.py:133
  20.6 1.6 copy-done
  22.2 2.5 %shard_map.141 = (f32[64,128]{1,0:T(8,128)S(1)}, f32[64,128]{1,0:T(8,128)}, f32[16,128]{1,0:T(8,128)S(1)}) custom-call(f32[64,128]{1,0:T(8,128)S(1)} %bitcast.45, f32[16,128]{1,0:T(8,128)S(1)} %collective-permute-done.a, f32[16,128]{1,0:T(8,128)S(1)} %collective-permute-done.1.b, f32[16,128]{1,0:T(8,128)S(1)} %collective-permute-done.2.c, ...), custom_call_target="tpu_custom_call" | custom-call | tf_op jit(solution)/shard_map/pallas_call | solution.py:17
  24.7 2.9 %collective-permute-start.4 = (f32[16,128]{1,0:T(8,128)S(1)}, f32[16,128]{1,0:T(8,128)S(1)}, u32[]{:S(2)}, u32[]{:S(2)}) collective-permute-start(f32[16,128]{1,0:T(8,128)S(1)} %get-tuple-element.62), channel_id=1, source_target_pairs={{0,128},{1,129},{2,130},{3,131},{4,132},{5,133},{6,134},{7,135},{8... | collective-permute-start | bytes 24584 | tf_op jit(solution)/shard_map/ppermute | solution.py:262
  27.7 0.8 collective-permute-done.4.got_ref
  28.4 1.6 copy-done.1
  30.0 1.5 shard_map.142
  31.5 0.7 collective-permute-start.5
  32.2 1.5 shard_map.143
  34.4 1.6 copy-done.2
  36.0 2.9 %shard_map.144 = (f32[64,128]{1,0:T(8,128)S(1)}, f32[16,128]{1,0:T(8,128)S(1)}) custom-call(f32[64,128]{1,0:T(8,128)S(1)} %get-tuple-element.61.g_ref, f32[16,128]{1,0:T(8,128)S(1)} %get-tuple-element.65.inc_ref, f32[16,128]{1,0:T(8,128)S(1)} %collective-permute-done.6.got_ref, f32[64,32]{1,0:T(8,128)S(1)} %bitcast.31, ...), custom_call_target="tpu_custom_call" | custom-call | tf_op jit(solution)/shard_map/pallas_call | solution.py:17
  39.6 1.6 copy-done.3
  41.2 1.5 shard_map.145
  43.4 1.5 shard_map.146
  44.9 1.3 collective-permute-start.9
  46.2 12.6 %collective-permute-done.9.got_ref = f32[16,128]{1,0:T(8,128)S(1)} collective-permute-done((f32[16,128]{1,0:T(8,128)S(1)}, f32[16,128]{1,0:T(8,128)S(1)}, u32[]{:S(2)}, u32[]{:S(2)}) %collective-permute-start.9) | collective-permute-done | bytes 8224 | tf_op jit(solution)/shard_map/ppermute | solution.py:270
  58.8 1.6 copy-done.4
  60.4 2.1 %shard_map.147 = (f32[64,128]{1,0:T(8,128)S(1)}, f32[64,128]{1,0:T(8,128)}, f32[16,128]{1,0:T(8,128)S(1)}, f32[16,128]{1,0:T(8,128)S(1)}, f32[16,128]{1,0:T(8,128)S(1)}, /*index=5*/f32[16,128]{1,0:T(8,128)S(1)}) custom-call(f32[64,128]{1,0:T(8,128)S(1)} %get-tuple-element.69.y_ref, f32[16,128]{1,0:T(8,128)S(1)} %get-tuple-element.73.arr_ref, ...), custom_call_target="tpu_custom_call" | custom-call | tf_op jit(solution)/shard_map/pallas_call | solution.py:17
  62.5 2.8 %collective-permute-start.10 = (f32[16,128]{1,0:T(8,128)S(1)}, f32[16,128]{1,0:T(8,128)S(1)}, u32[]{:S(2)}, u32[]{:S(2)}) collective-permute-start(f32[16,128]{1,0:T(8,128)S(1)} %get-tuple-element.76), channel_id=1, source_target_pairs={{0,16},{16,0},{32,48},{48,32},{64,80},{80,64},{96,112},{112,96},{1... | collective-permute-start | bytes 24584 | tf_op jit(solution)/shard_map/ppermute | solution.py:131
  65.3 8.8 %collective-permute-start.11 = (f32[16,128]{1,0:T(8,128)S(1)}, f32[16,128]{1,0:T(8,128)S(1)}, u32[]{:S(2)}, u32[]{:S(2)}) collective-permute-start(f32[16,128]{1,0:T(8,128)S(1)} %get-tuple-element.77), channel_id=1, source_target_pairs={{16,32},{32,16},{48,64},{64,48},{80,96},{96,80},{17,33},{33,17},{4... | collective-permute-start | bytes 24584 | tf_op jit(solution)/shard_map/ppermute | solution.py:132
  74.1 5.6 %collective-permute-start.12 = (f32[16,128]{1,0:T(8,128)S(1)}, f32[16,128]{1,0:T(8,128)S(1)}, u32[]{:S(2)}, u32[]{:S(2)}) collective-permute-start(f32[16,128]{1,0:T(8,128)S(1)} %get-tuple-element.78), channel_id=1, source_target_pairs={{0,1},{1,0},{2,3},{3,2},{4,5},{5,4},{6,7},{7,6},{8,9},{9,8},{10,11... | collective-permute-start | bytes 24584 | tf_op jit(solution)/shard_map/ppermute | solution.py:133
  80.7 1.6 copy-done.5
  82.3 2.5 %shard_map.148 = (f32[64,128]{1,0:T(8,128)S(1)}, f32[64,128]{1,0:T(8,128)}, f32[16,128]{1,0:T(8,128)S(1)}) custom-call(f32[64,128]{1,0:T(8,128)S(1)} %get-tuple-element.75.x_ref.prev_ref, f32[16,128]{1,0:T(8,128)S(1)} %collective-permute-done.10.a, f32[16,128]{1,0:T(8,128)S(1)} %collective-permute-done.11.b, f32[16,128]{1,0:T(8,128)S(1)} %collective-permute-done.12.c, ...), custom_call_target="tpu_custom_call" | custom-call | tf_op jit(solution)/shard_map/pallas_call | solution.py:17
  84.9 1.4 collective-permute-start.14
  86.2 0.8 collective-permute-done.14.got_ref
  87.0 1.6 copy-done.6
  88.6 1.5 shard_map.149
  90.8 1.5 shard_map.150
  93.0 1.6 copy-done.7
  94.6 2.9 %shard_map.151 = (f32[64,128]{1,0:T(8,128)S(1)}, f32[16,128]{1,0:T(8,128)S(1)}) custom-call(f32[64,128]{1,0:T(8,128)S(1)} %get-tuple-element.80.g_ref, f32[16,128]{1,0:T(8,128)S(1)} %get-tuple-element.84.inc_ref, f32[16,128]{1,0:T(8,128)S(1)} %collective-permute-done.16.got_ref, f32[64,32]{1,0:T(8,128)S(1)} %bitcast.38, ...), custom_call_target="tpu_custom_call" | custom-call | tf_op jit(solution)/shard_map/pallas_call | solution.py:17
  98.2 1.6 copy-done.8
  99.8 1.5 shard_map.152
  102.0 1.5 shard_map.153
  103.5 1.3 collective-permute-start.19
  104.9 12.5 %collective-permute-done.19.got_ref = f32[16,128]{1,0:T(8,128)S(1)} collective-permute-done((f32[16,128]{1,0:T(8,128)S(1)}, f32[16,128]{1,0:T(8,128)S(1)}, u32[]{:S(2)}, u32[]{:S(2)}) %collective-permute-start.19) | collective-permute-done | bytes 8224 | tf_op jit(solution)/shard_map/ppermute | solution.py:270
  117.4 1.6 copy-done.9
  118.9 1.5 shard_map.154
  120.5 1.9 %collective-permute-start.20 = (f32[16,128]{1,0:T(8,128)S(1)}, f32[16,128]{1,0:T(8,128)S(1)}, u32[]{:S(2)}, u32[]{:S(2)}) collective-permute-start(f32[16,128]{1,0:T(8,128)S(1)} %get-tuple-element.93), channel_id=1, source_target_pairs={{0,16},{16,0},{32,48},{48,32},{64,80},{80,64},{96,112},{112,96},{1... | collective-permute-start | bytes 24584 | tf_op jit(solution)/shard_map/ppermute | solution.py:131
  122.4 8.3 %collective-permute-start.21 = (f32[16,128]{1,0:T(8,128)S(1)}, f32[16,128]{1,0:T(8,128)S(1)}, u32[]{:S(2)}, u32[]{:S(2)}) collective-permute-start(f32[16,128]{1,0:T(8,128)S(1)} %get-tuple-element.94), channel_id=1, source_target_pairs={{16,32},{32,16},{48,64},{64,48},{80,96},{96,80},{17,33},{33,17},{4... | collective-permute-start | bytes 24584 | tf_op jit(solution)/shard_map/ppermute | solution.py:132
  130.7 7.1 %collective-permute-start.22 = (f32[16,128]{1,0:T(8,128)S(1)}, f32[16,128]{1,0:T(8,128)S(1)}, u32[]{:S(2)}, u32[]{:S(2)}) collective-permute-start(f32[16,128]{1,0:T(8,128)S(1)} %get-tuple-element.95), channel_id=1, source_target_pairs={{0,1},{1,0},{2,3},{3,2},{4,5},{5,4},{6,7},{7,6},{8,9},{9,8},{10,11... | collective-permute-start | bytes 24584 | tf_op jit(solution)/shard_map/ppermute | solution.py:133
  138.8 0.7 shard_map.155
  139.5 18.5 %all_to_all.10.parts_ref = f32[16,4,128]{2,1,0:T(4,128)S(1)} all-to-all(f32[16,4,128]{2,1,0:T(4,128)S(1)} %bitcast.51), channel_id=1, replica_groups=mesh['line'=4,'tx'=8,'ty'=16] {'ty'}, dimensions={0} | all-to-all | bytes 65536 | tf_op jit(solution)/shard_map/all_to_all | solution.py:298
  157.9 0.8 shard_map.156
  158.8 3.5 %all-to-all-start.1 = ((f32[16,4,128]{2,1,0:T(4,128)}), f32[16,4,128]{2,1,0:T(4,128)S(1)}, u32[]{:S(2)}, u32[]{:S(2)}) async-start(f32[16,4,128]{2,1,0:T(4,128)} %shard_map.156), calls=%async_computation.1 | async-start | bytes 65536 | tf_op jit(solution)/shard_map/all_to_all | solution.py:318
  162.9 5.8 %all-to-all-done.1 = f32[16,4,128]{2,1,0:T(4,128)S(1)} async-done(((f32[16,4,128]{2,1,0:T(4,128)}), f32[16,4,128]{2,1,0:T(4,128)S(1)}, u32[]{:S(2)}, u32[]{:S(2)}) %all-to-all-start.1) | async-done | bytes 32800 | tf_op jit(solution)/shard_map/all_to_all | solution.py:318
  (91 shorter events, 11.6 us)
Async XLA Ops:
  0.6 2.2 %copy-start.10 = (f32[4,4,4,128]{3,2,1,0:T(4,128)S(1)}, f32[4,4,4,128]{3,2,1,0:T(4,128)}, u32[]{:S(2)}) copy-start(f32[4,4,4,128]{3,2,1,0:T(4,128)} %param.14) | copy-start | bytes 98308
  0.6 2.1 %copy-start.18 = (f32[32,128]{1,0:T(8,128)S(1)}, f32[32,128]{1,0:T(8,128)}, u32[]{:S(2)}) copy-start(f32[32,128]{1,0:T(8,128)} %param.24) | copy-start | bytes 49156
  0.7 2.2 %copy-start.13 = (f32[128,128]{1,0:T(8,128)S(1)}, f32[128,128]{1,0:T(8,128)}, u32[]{:S(2)}) copy-start(f32[128,128]{1,0:T(8,128)} %l_ref.1) | copy-start | bytes 196612
  0.7 2.2 %copy-start.14 = (f32[128,128]{1,0:T(8,128)S(1)}, f32[128,128]{1,0:T(8,128)}, u32[]{:S(2)}) copy-start(f32[128,128]{1,0:T(8,128)} %u_ref.1) | copy-start | bytes 196612
  0.7 2.2 %copy-start.11 = (f32[4,128,128]{2,1,0:T(8,128)S(1)}, f32[4,128,128]{2,1,0:T(8,128)}, u32[]{:S(2)}) copy-start(f32[4,128,128]{2,1,0:T(8,128)} %f_ref.1) | copy-start | bytes 786436
  0.7 18.2 %copy-start.17 = (s32[4,4,4]{2,1,0:T(4,128)S(1)}, s32[4,4,4]{2,1,0:T(4,128)}, u32[]{:S(2)}) copy-start(s32[4,4,4]{2,1,0:T(4,128)} %param.23) | copy-start | bytes 772
  0.7 18.3 %copy-start.15 = (s32[4,4,4,4]{3,2,1,0:T(4,128)S(1)}, s32[4,4,4,4]{3,2,1,0:T(4,128)}, u32[]{:S(2)}) copy-start(s32[4,4,4,4]{3,2,1,0:T(4,128)} %param.21) | copy-start | bytes 3076
  0.7 18.5 %copy-start.16 = (f32[4,4,4,4]{3,2,1,0:T(4,128)S(1)}, f32[4,4,4,4]{3,2,1,0:T(4,128)}, u32[]{:S(2)}) copy-start(f32[4,4,4,4]{3,2,1,0:T(4,128)} %param.22) | copy-start | bytes 3076
  0.7 18.9 %copy-start.19 = (f32[4,4,4]{2,1,0:T(4,128)S(1)}, f32[4,4,4]{2,1,0:T(4,128)}, u32[]{:S(2)}) copy-start(f32[4,4,4]{2,1,0:T(4,128)} %param.16) | copy-start | bytes 772
  0.7 19.0 %copy-start.20 = (f32[4,4,4]{2,1,0:T(4,128)S(1)}, f32[4,4,4]{2,1,0:T(4,128)}, u32[]{:S(2)}) copy-start(f32[4,4,4]{2,1,0:T(4,128)} %param.17) | copy-start | bytes 772
  0.8 19.8 %copy-start.12 = (f32[4,4,4,128]{3,2,1,0:T(4,128)S(1)}, f32[4,4,4,128]{3,2,1,0:T(4,128)}, u32[]{:S(2)}) copy-start(f32[4,4,4,128]{3,2,1,0:T(4,128)} %param.13) | copy-start | bytes 98308
  2.9 17.0 %collective-permute-start = (f32[16,128]{1,0:T(8,128)S(1)}, f32[16,128]{1,0:T(8,128)S(1)}, u32[]{:S(2)}, u32[]{:S(2)}) collective-permute-start(f32[16,128]{1,0:T(8,128)S(1)} %get-tuple-element.53), channel_id=1, source_target_pairs={{0,16},{16,0},{32,48},{48,32},{64,80},{80,64},{96,112},{112,96},{1... | collective-permute-start | bytes 24584 | tf_op jit(solution)/shard_map/ppermute | solution.py:131
  11.7 8.9 %collective-permute-start.1 = (f32[16,128]{1,0:T(8,128)S(1)}, f32[16,128]{1,0:T(8,128)S(1)}, u32[]{:S(2)}, u32[]{:S(2)}) collective-permute-start(f32[16,128]{1,0:T(8,128)S(1)} %get-tuple-element.54), channel_id=1, source_target_pairs={{16,32},{32,16},{48,64},{64,48},{80,96},{96,80},{17,33},{33,17},{4... | collective-permute-start | bytes 24584 | tf_op jit(solution)/shard_map/ppermute | solution.py:132
  15.1 5.5 %collective-permute-start.2 = (f32[16,128]{1,0:T(8,128)S(1)}, f32[16,128]{1,0:T(8,128)S(1)}, u32[]{:S(2)}, u32[]{:S(2)}) collective-permute-start(f32[16,128]{1,0:T(8,128)S(1)} %get-tuple-element.55), channel_id=1, source_target_pairs={{0,1},{1,0},{2,3},{3,2},{4,5},{5,4},{6,7},{7,6},{8,9},{9,8},{10,11... | collective-permute-start | bytes 24584 | tf_op jit(solution)/shard_map/ppermute | solution.py:133
  18.2 2.4 %collective-permute-start.3 = (f32[16,128]{1,0:T(8,128)S(1)}, f32[16,128]{1,0:T(8,128)S(1)}, u32[]{:S(2)}, u32[]{:S(2)}) collective-permute-start(f32[16,128]{1,0:T(8,128)S(1)} %get-tuple-element.56), channel_id=1, source_target_pairs={{1,2},{2,1},{3,4},{4,3},{5,6},{6,5},{7,8},{8,7},{9,10},{10,9},{11,... | collective-permute-start | bytes 24584 | tf_op jit(solution)/shard_map/ppermute | solution.py:134
  20.6 1.6 copy-start
  24.7 3.7 %collective-permute-start.4 = (f32[16,128]{1,0:T(8,128)S(1)}, f32[16,128]{1,0:T(8,128)S(1)}, u32[]{:S(2)}, u32[]{:S(2)}) collective-permute-start(f32[16,128]{1,0:T(8,128)S(1)} %get-tuple-element.62), channel_id=1, source_target_pairs={{0,128},{1,129},{2,130},{3,131},{4,132},{5,133},{6,134},{7,135},{8... | collective-permute-start | bytes 24584 | tf_op jit(solution)/shard_map/ppermute | solution.py:262
  28.4 1.6 copy-start.1
  31.5 0.7 collective-permute-start.5
  33.7 0.7 collective-permute-start.6
  34.4 1.6 copy-start.2
  38.9 0.7 collective-permute-start.7
  39.6 1.6 copy-start.3
  42.7 0.7 collective-permute-start.8
  44.9 13.9 %collective-permute-start.9 = (f32[16,128]{1,0:T(8,128)S(1)}, f32[16,128]{1,0:T(8,128)S(1)}, u32[]{:S(2)}, u32[]{:S(2)}) collective-permute-start(f32[16,128]{1,0:T(8,128)S(1)} %get-tuple-element.74), channel_id=1, source_target_pairs={{128,0},{129,1},{130,2},{131,3},{132,4},{133,5},{134,6},{135,7},{1... | collective-permute-start | bytes 24584 | tf_op jit(solution)/shard_map/ppermute | solution.py:270
  58.8 1.6 copy-start.4
  62.5 17.9 %collective-permute-start.10 = (f32[16,128]{1,0:T(8,128)S(1)}, f32[16,128]{1,0:T(8,128)S(1)}, u32[]{:S(2)}, u32[]{:S(2)}) collective-permute-start(f32[16,128]{1,0:T(8,128)S(1)} %get-tuple-element.76), channel_id=1, source_target_pairs={{0,16},{16,0},{32,48},{48,32},{64,80},{80,64},{96,112},{112,96},{1... | collective-permute-start | bytes 24584 | tf_op jit(solution)/shard_map/ppermute | solution.py:131
  65.3 15.1 %collective-permute-start.11 = (f32[16,128]{1,0:T(8,128)S(1)}, f32[16,128]{1,0:T(8,128)S(1)}, u32[]{:S(2)}, u32[]{:S(2)}) collective-permute-start(f32[16,128]{1,0:T(8,128)S(1)} %get-tuple-element.77), channel_id=1, source_target_pairs={{16,32},{32,16},{48,64},{64,48},{80,96},{96,80},{17,33},{33,17},{4... | collective-permute-start | bytes 24584 | tf_op jit(solution)/shard_map/ppermute | solution.py:132
  74.1 6.6 %collective-permute-start.12 = (f32[16,128]{1,0:T(8,128)S(1)}, f32[16,128]{1,0:T(8,128)S(1)}, u32[]{:S(2)}, u32[]{:S(2)}) collective-permute-start(f32[16,128]{1,0:T(8,128)S(1)} %get-tuple-element.78), channel_id=1, source_target_pairs={{0,1},{1,0},{2,3},{3,2},{4,5},{5,4},{6,7},{7,6},{8,9},{9,8},{10,11... | collective-permute-start | bytes 24584 | tf_op jit(solution)/shard_map/ppermute | solution.py:133
  79.7 1.0 collective-permute-start.13
  80.7 1.6 copy-start.5
  84.9 2.1 %collective-permute-start.14 = (f32[16,128]{1,0:T(8,128)S(1)}, f32[16,128]{1,0:T(8,128)S(1)}, u32[]{:S(2)}, u32[]{:S(2)}) collective-permute-start(f32[16,128]{1,0:T(8,128)S(1)} %get-tuple-element.81), channel_id=1, source_target_pairs={{0,128},{1,129},{2,130},{3,131},{4,132},{5,133},{6,134},{7,135},{8... | collective-permute-start | bytes 24584 | tf_op jit(solution)/shard_map/ppermute | solution.py:262
  87.0 1.6 copy-start.6
  90.1 0.7 collective-permute-start.15
  92.3 0.7 collective-permute-start.16
  93.0 1.6 copy-start.7
  97.5 0.7 collective-permute-start.17
  98.2 1.6 copy-start.8
  101.3 0.7 collective-permute-start.18
  103.5 13.9 %collective-permute-start.19 = (f32[16,128]{1,0:T(8,128)S(1)}, f32[16,128]{1,0:T(8,128)S(1)}, u32[]{:S(2)}, u32[]{:S(2)}) collective-permute-start(f32[16,128]{1,0:T(8,128)S(1)} %get-tuple-element.91), channel_id=1, source_target_pairs={{128,0},{129,1},{130,2},{131,3},{132,4},{133,5},{134,6},{135,7},{1... | collective-permute-start | bytes 24584 | tf_op jit(solution)/shard_map/ppermute | solution.py:270
  117.3 1.6 copy-start.9
  120.5 18.0 %collective-permute-start.20 = (f32[16,128]{1,0:T(8,128)S(1)}, f32[16,128]{1,0:T(8,128)S(1)}, u32[]{:S(2)}, u32[]{:S(2)}) collective-permute-start(f32[16,128]{1,0:T(8,128)S(1)} %get-tuple-element.93), channel_id=1, source_target_pairs={{0,16},{16,0},{32,48},{48,32},{64,80},{80,64},{96,112},{112,96},{1... | collective-permute-start | bytes 24584 | tf_op jit(solution)/shard_map/ppermute | solution.py:131
  122.4 16.0 %collective-permute-start.21 = (f32[16,128]{1,0:T(8,128)S(1)}, f32[16,128]{1,0:T(8,128)S(1)}, u32[]{:S(2)}, u32[]{:S(2)}) collective-permute-start(f32[16,128]{1,0:T(8,128)S(1)} %get-tuple-element.94), channel_id=1, source_target_pairs={{16,32},{32,16},{48,64},{64,48},{80,96},{96,80},{17,33},{33,17},{4... | collective-permute-start | bytes 24584 | tf_op jit(solution)/shard_map/ppermute | solution.py:132
  130.7 8.1 %collective-permute-start.22 = (f32[16,128]{1,0:T(8,128)S(1)}, f32[16,128]{1,0:T(8,128)S(1)}, u32[]{:S(2)}, u32[]{:S(2)}) collective-permute-start(f32[16,128]{1,0:T(8,128)S(1)} %get-tuple-element.95), channel_id=1, source_target_pairs={{0,1},{1,0},{2,3},{3,2},{4,5},{5,4},{6,7},{7,6},{8,9},{9,8},{10,11... | collective-permute-start | bytes 24584 | tf_op jit(solution)/shard_map/ppermute | solution.py:133
  137.7 1.0 collective-permute-start.23
  158.8 9.9 %all-to-all-start.1 = ((f32[16,4,128]{2,1,0:T(4,128)}), f32[16,4,128]{2,1,0:T(4,128)S(1)}, u32[]{:S(2)}, u32[]{:S(2)}) async-start(f32[16,4,128]{2,1,0:T(4,128)} %shard_map.156), calls=%async_computation.1 | async-start | bytes 65536 | tf_op jit(solution)/shard_map/all_to_all | solution.py:318

commit v2 on v1

--- a/solution.py
+++ b/solution.py
@@ -13,14 +13,15 @@
 SPEC = pl.BlockSpec(memory_space=pltpu.VMEM)
 
 
-def call(kernel, outs, *args, scratch=()):
+def call(kernel, outs, *args, scratch=(), whole=0):
     return pl.pallas_call(
         kernel,
-        in_specs=[SPEC] * len(args),
+        in_specs=[pl.BlockSpec(memory_space=pl.ANY)] * whole + [SPEC] * (len(args) - whole),
         out_specs=[SPEC] * len(outs),
         out_shape=[pltpu.VMEM(s, d) for s, d in outs],
         scratch_shapes=list(scratch),
-    )(*[pltpu.with_memory_space_constraint(a, pltpu.VMEM) for a in args])
+        compiler_params=pltpu.CompilerParams(vmem_limit_bytes=24 << 20),
+    )(*args[:whole], *[pltpu.with_memory_space_constraint(a, pltpu.VMEM) for a in args[whole:]])
 
 
 def halves(v):
@@ -93,7 +94,7 @@
     lines = lx * ly
     x = x_ref[...]
     even = par_ref[0:1, :] < 0.5
-    a, b, c, d = (r[...] for r in got)
+    b, c, d, a = (r[...] for r in got)
     below, above = jnp.where(even, b, a), jnp.where(even, a, b)
     near[0] = pltpu.roll(x, ly, 0)
     near[1] = pltpu.roll(x, n * lines - ly, 0)
@@ -127,12 +128,11 @@
 def exchange(sends):
     nx, ny = lax.axis_size("tx"), lax.axis_size("ty")
     a, b, c, d = sends
-    return (
-        lax.ppermute(a, "tx", swaps(nx, 0)),
-        lax.ppermute(b, "tx", swaps(nx, 1)),
-        lax.ppermute(c, "ty", swaps(ny, 0)),
-        lax.ppermute(d, "ty", swaps(ny, 1)),
-    )
+    b = lax.ppermute(b, "tx", swaps(nx, 1))
+    c = lax.ppermute(c, "ty", swaps(ny, 0))
+    d = lax.ppermute(d, "ty", swaps(ny, 1))
+    a = lax.ppermute(a, "tx", swaps(nx, 0))
+    return b, c, d, a
 
 
 def body(
@@ -187,25 +187,32 @@
     half, half4 = ((width, width), BF16), ((4, width, width), BF16)
     edges4 = [((n * ly, width), F32)] * 2 + [((n * lx, width), F32)] * 2
 
-    def prepare(x_ref, par_ref, l_ref, u_ref, f_ref, r_ref, c_ref, *outs):
-        put_edges(x_ref, par_ref, outs[:4], n, lx, ly)
-        for src, k in ((l_ref, 4), (u_ref, 6), (f_ref, 8), (r_ref, 10), (c_ref, 12)):
-            outs[k][...], outs[k + 1][...] = halves(src[...])
-
-    made = call(
+    def first_edges(x_ref, par_ref, *outs):
+        put_edges(x_ref, par_ref, outs, n, lx, ly)
+
+    sends = call(first_edges, edges4, start, par)
+
+    def prepare(w_ref, l_ref, u_ref, f_ref, r_ref, c_ref, *outs):
+        copy = pltpu.make_async_copy(w_ref, outs[10], outs[11])
+        copy.start()
+        for k, src in enumerate((l_ref, u_ref, f_ref, r_ref, c_ref)):
+            outs[2 * k][...], outs[2 * k + 1][...] = halves(src[...])
+        copy.wait()
+
+    lh, ll, uh, ul, fh, fl, rh, rl, ch, cl, w = call(
         prepare,
-        edges4
-        + [half, half, half, half, half4, half4, half, half]
-        + [((owned_rows * width, width), BF16)] * 2,
-        start,
-        par,
+        [half, half, half, half, half4, half4, half, half]
+        + [((owned_rows * width, width), BF16)] * 2
+        + [((rows * width, width), BF16)],
+        w,
         lower_block,
         upper_block,
         face_blocks,
         spread_op,
         ci,
+        scratch=[pltpu.SemaphoreType.DMA],
+        whole=1,
     )
-    sends, lh, ll, uh, ul, fh, fl, rh, rl, ch, cl = made[:4], *made[4:]
 
     def open_forward(x_ref, a, b, c, d, par_ref, cols_ref, fh_ref, fl_ref, rhs_ref, lh_ref, ll_ref, w_ref, g_ref, y_ref, f_ref, near):
         cols = cols_ref[...]

time: 171 us -> 165 us (0.965)
  local copies, waits for them, and re-layouts: 18.8 us -> 10.3 us
  blocking collectives: 18.5 us -> 14 us
  starting transfers between devices: 67.5 us -> 71.7 us
    unnamed x44 -> x24, local copies, waits for them, and re-layouts: 17.2 us -> 4.46 us
    all_to_all x1, blocking collectives: 18.5 us -> 14 us  [body(): lax.all_to_all(partial.reshape(owners, owned_rows, width), 'ty', 0, 0, ti...]
    ppermute x12, starting transfers between devices: 51.6 us -> 55.2 us  [the longest x3 33.5 us: exchange(): b = lax.ppermute(b, 'tx', swaps(nx, 1))]
    pallas_call x18 -> x19, Pallas kernels: 28.4 us -> 29 us  [call(): pl.pallas_call(kernel, in_specs=[pl.BlockSpec(memory_space=pl.ANY)] * who...]
  transfers between devices with their start and end apart: 25 -> 25, of which waited for: 8 -> 7; matrix products, arithmetic and copies ran while one was open for 1% -> 5% of each run, Pallas kernels for 0% -> 0%
where the time goes in v2:
time: 165 us; the launch traced here: 163 us
  starting transfers between devices  71.7 us (43%)
  waiting for transfers between devices  34.6 us (21%)
  Pallas kernels  29 us (18%)
  blocking collectives  14 us (8%)
  local copies, waits for them, and re-layouts  10.3 us (6%)
  other arithmetic  2.62 us (2%)
    ppermute x3, starting transfers between devices, exchange(): b = lax.ppermute(b, 'tx', swaps(nx, 1))  33.5 us
    pallas_call x19, Pallas kernels, call(): pl.pallas_call(kernel, in_specs=[pl.BlockSpec(memory_space=pl.ANY)] * who...  29 us
    ppermute x2, waiting for transfers between devices, body(): recv = lax.ppermute(behind, 'line', [(1, 0)])  25 us
    all_to_all x1, blocking collectives, body(): lax.all_to_all(partial.reshape(owners, owned_rows, width), 'ty', 0, 0, ti...  14 us
    ppermute x3, starting transfers between devices, exchange(): c = lax.ppermute(c, 'ty', swaps(ny, 0))  14 us
    ppermute x4, starting transfers between devices, body(): recv = lax.ppermute(ahead, 'line', [(k, k + 1)])  6.25 us
    all_to_all x1, waiting for transfers between devices, body(): update = lax.all_to_all(copies, 'ty', 0, 0, tiled=True)  5.77 us
    ppermute x3, starting transfers between devices, exchange(): a = lax.ppermute(a, 'tx', swaps(nx, 0))  5.76 us
  transfers between devices with their start and end apart: 25, of which 7 were waited for; matrix products, arithmetic and copies ran while one was open for 5% of the time, Pallas kernels for 0%

profile of v2, /device:TPU:1, one launch (start us, length us, event | category | flops | bytes accessed | tf_op | source)
XLA Modules:
  0.0 163.5 jit_solution(6004930504372852393)
XLA Ops:
  0.8 0.8 copy-done.1
  2.2 10.2 %collective-permute-start = (f32[16,128]{1,0:T(8,128)}, f32[16,128]{1,0:T(8,128)S(1)}, u32[]{:S(2)}, u32[]{:S(2)}) collective-permute-start(f32[16,128]{1,0:T(8,128)} %get-tuple-element.54), channel_id=1, source_target_pairs={{16,32},{32,16},{48,64},{64,48},{80,96},{96,80},{17,33},{33,17},{4... | collective-permute-start | bytes 24584 | tf_op jit(solution)/shard_map/ppermute | solution.py:131
  12.4 3.1 %collective-permute-start.1 = (f32[16,128]{1,0:T(8,128)}, f32[16,128]{1,0:T(8,128)S(1)}, u32[]{:S(2)}, u32[]{:S(2)}) collective-permute-start(f32[16,128]{1,0:T(8,128)} %get-tuple-element.55), channel_id=1, source_target_pairs={{0,1},{1,0},{2,3},{3,2},{4,5},{5,4},{6,7},{7,6},{8,9},{9,8},{10,11... | collective-permute-start | bytes 24584 | tf_op jit(solution)/shard_map/ppermute | solution.py:132
  16.2 1.9 %collective-permute-start.3 = (f32[16,128]{1,0:T(8,128)S(1)}, f32[16,128]{1,0:T(8,128)S(1)}, u32[]{:S(2)}, u32[]{:S(2)}) collective-permute-start(f32[16,128]{1,0:T(8,128)S(1)} %get-tuple-element.57), channel_id=1, source_target_pairs={{0,16},{16,0},{32,48},{48,32},{64,80},{80,64},{96,112},{112,96},{1... | collective-permute-start | bytes 24584 | tf_op jit(solution)/shard_map/ppermute | solution.py:134
  18.1 0.8 reshape.186
  18.9 0.8 eq.32
  19.9 0.8 broadcast_in_dim.21
  21.0 1.2 broadcast_multiply_fusion
  24.1 0.7 reshape.184
  24.8 0.7 reshape.185
  25.5 1.6 copy-done
  27.1 0.8 copy-done.6
  28.2 0.9 concatenate.3
  29.2 2.5 %shard_map.142 = (f32[64,128]{1,0:T(8,128)S(1)}, f32[64,128]{1,0:T(8,128)}, f32[16,128]{1,0:T(8,128)S(1)}) custom-call(f32[64,128]{1,0:T(8,128)S(1)} %bitcast.32, f32[16,128]{1,0:T(8,128)S(1)} %collective-permute-done.a, f32[16,128]{1,0:T(8,128)S(1)} %collective-permute-done.1.b, f32[16,128]{1,0:T(8,128)S(1)} %collective-permute-done.2.c, ...), custom_call_target="tpu_custom_call" | custom-call | tf_op jit(solution)/shard_map/pallas_call | solution.py:17
  31.7 3.5 %collective-permute-start.4 = (f32[16,128]{1,0:T(8,128)S(1)}, f32[16,128]{1,0:T(8,128)S(1)}, u32[]{:S(2)}, u32[]{:S(2)}) collective-permute-start(f32[16,128]{1,0:T(8,128)S(1)} %get-tuple-element.64), channel_id=1, source_target_pairs={{0,128},{1,129},{2,130},{3,131},{4,132},{5,133},{6,134},{7,135},{8... | collective-permute-start | bytes 24584 | tf_op jit(solution)/shard_map/ppermute | solution.py:269
  35.3 0.8 collective-permute-done.4.got_ref
  36.0 1.5 shard_map.143
  38.2 1.5 shard_map.144
  40.4 2.9 %shard_map.145 = (f32[64,128]{1,0:T(8,128)S(1)}, f32[16,128]{1,0:T(8,128)S(1)}) custom-call(f32[64,128]{1,0:T(8,128)S(1)} %get-tuple-element.63.g_ref, f32[16,128]{1,0:T(8,128)S(1)} %get-tuple-element.67.inc_ref, f32[16,128]{1,0:T(8,128)S(1)} %collective-permute-done.6.got_ref, f32[64,32]{1,0:T(8,128)S(1)} %bitcast.17, ...), custom_call_target="tpu_custom_call" | custom-call | tf_op jit(solution)/shard_map/pallas_call | solution.py:17
  44.0 1.5 shard_map.146
  46.2 1.5 shard_map.147
  47.7 1.3 collective-permute-start.9
  49.0 12.6 %collective-permute-done.9.got_ref = f32[16,128]{1,0:T(8,128)S(1)} collective-permute-done((f32[16,128]{1,0:T(8,128)S(1)}, f32[16,128]{1,0:T(8,128)S(1)}, u32[]{:S(2)}, u32[]{:S(2)}) %collective-permute-start.9) | collective-permute-done | bytes 8224 | tf_op jit(solution)/shard_map/ppermute | solution.py:277
  61.6 2.1 %shard_map.148 = (f32[64,128]{1,0:T(8,128)S(1)}, f32[64,128]{1,0:T(8,128)}, f32[16,128]{1,0:T(8,128)S(1)}, f32[16,128]{1,0:T(8,128)S(1)}, f32[16,128]{1,0:T(8,128)S(1)}, /*index=5*/f32[16,128]{1,0:T(8,128)S(1)}) custom-call(f32[64,128]{1,0:T(8,128)S(1)} %get-tuple-element.71.y_ref, f32[16,128]{1,0:T(8,128)S(1)} %get-tuple-element.75.arr_ref, ...), custom_call_target="tpu_custom_call" | custom-call | tf_op jit(solution)/shard_map/pallas_call | solution.py:17
  63.7 13.8 %collective-permute-start.10 = (f32[16,128]{1,0:T(8,128)S(1)}, f32[16,128]{1,0:T(8,128)S(1)}, u32[]{:S(2)}, u32[]{:S(2)}) collective-permute-start(f32[16,128]{1,0:T(8,128)S(1)} %get-tuple-element.78), channel_id=1, source_target_pairs={{16,32},{32,16},{48,64},{64,48},{80,96},{96,80},{17,33},{33,17},{4... | collective-permute-start | bytes 24584 | tf_op jit(solution)/shard_map/ppermute | solution.py:131
  77.5 5.3 %collective-permute-start.11 = (f32[16,128]{1,0:T(8,128)S(1)}, f32[16,128]{1,0:T(8,128)S(1)}, u32[]{:S(2)}, u32[]{:S(2)}) collective-permute-start(f32[16,128]{1,0:T(8,128)S(1)} %get-tuple-element.79), channel_id=1, source_target_pairs={{0,1},{1,0},{2,3},{3,2},{4,5},{5,4},{6,7},{7,6},{8,9},{9,8},{10,11... | collective-permute-start | bytes 24584 | tf_op jit(solution)/shard_map/ppermute | solution.py:132
  83.4 1.9 %collective-permute-start.13 = (f32[16,128]{1,0:T(8,128)S(1)}, f32[16,128]{1,0:T(8,128)S(1)}, u32[]{:S(2)}, u32[]{:S(2)}) collective-permute-start(f32[16,128]{1,0:T(8,128)S(1)} %get-tuple-element.81), channel_id=1, source_target_pairs={{0,16},{16,0},{32,48},{48,32},{64,80},{80,64},{96,112},{112,96},{1... | collective-permute-start | bytes 24584 | tf_op jit(solution)/shard_map/ppermute | solution.py:134
  85.4 1.1 collective-permute-done.13.d
  86.5 2.5 %shard_map.149 = (f32[64,128]{1,0:T(8,128)S(1)}, f32[64,128]{1,0:T(8,128)}, f32[16,128]{1,0:T(8,128)S(1)}) custom-call(f32[64,128]{1,0:T(8,128)S(1)} %get-tuple-element.77.x_ref.prev_ref, f32[16,128]{1,0:T(8,128)S(1)} %collective-permute-done.10.a, f32[16,128]{1,0:T(8,128)S(1)} %collective-permute-done.11.b, f32[16,128]{1,0:T(8,128)S(1)} %collective-permute-done.12.c, ...), custom_call_target="tpu_custom_call" | custom-call | tf_op jit(solution)/shard_map/pallas_call | solution.py:17
  89.0 1.4 collective-permute-start.14
  90.4 0.8 collective-permute-done.14.got_ref
  91.2 1.5 shard_map.150
  93.4 1.5 shard_map.151
  95.6 2.9 %shard_map.152 = (f32[64,128]{1,0:T(8,128)S(1)}, f32[16,128]{1,0:T(8,128)S(1)}) custom-call(f32[64,128]{1,0:T(8,128)S(1)} %get-tuple-element.82.g_ref, f32[16,128]{1,0:T(8,128)S(1)} %get-tuple-element.86.inc_ref, f32[16,128]{1,0:T(8,128)S(1)} %collective-permute-done.16.got_ref, f32[64,32]{1,0:T(8,128)S(1)} %bitcast.24, ...), custom_call_target="tpu_custom_call" | custom-call | tf_op jit(solution)/shard_map/pallas_call | solution.py:17
  99.2 1.5 shard_map.153
  101.3 1.5 shard_map.154
  102.8 1.3 collective-permute-start.19
  104.3 12.4 %collective-permute-done.19.got_ref = f32[16,128]{1,0:T(8,128)S(1)} collective-permute-done((f32[16,128]{1,0:T(8,128)S(1)}, f32[16,128]{1,0:T(8,128)S(1)}, u32[]{:S(2)}, u32[]{:S(2)}) %collective-permute-start.19) | collective-permute-done | bytes 8224 | tf_op jit(solution)/shard_map/ppermute | solution.py:277
  116.7 1.5 shard_map.155
  118.2 9.5 %collective-permute-start.20 = (f32[16,128]{1,0:T(8,128)S(1)}, f32[16,128]{1,0:T(8,128)S(1)}, u32[]{:S(2)}, u32[]{:S(2)}) collective-permute-start(f32[16,128]{1,0:T(8,128)S(1)} %get-tuple-element.95), channel_id=1, source_target_pairs={{16,32},{32,16},{48,64},{64,48},{80,96},{96,80},{17,33},{33,17},{4... | collective-permute-start | bytes 24584 | tf_op jit(solution)/shard_map/ppermute | solution.py:131
  127.8 5.6 %collective-permute-start.21 = (f32[16,128]{1,0:T(8,128)S(1)}, f32[16,128]{1,0:T(8,128)S(1)}, u32[]{:S(2)}, u32[]{:S(2)}) collective-permute-start(f32[16,128]{1,0:T(8,128)S(1)} %get-tuple-element.96), channel_id=1, source_target_pairs={{0,1},{1,0},{2,3},{3,2},{4,5},{5,4},{6,7},{7,6},{8,9},{9,8},{10,11... | collective-permute-start | bytes 24584 | tf_op jit(solution)/shard_map/ppermute | solution.py:132
  134.0 1.9 %collective-permute-start.23 = (f32[16,128]{1,0:T(8,128)S(1)}, f32[16,128]{1,0:T(8,128)S(1)}, u32[]{:S(2)}, u32[]{:S(2)}) collective-permute-start(f32[16,128]{1,0:T(8,128)S(1)} %get-tuple-element.98), channel_id=1, source_target_pairs={{0,16},{16,0},{32,48},{48,32},{64,80},{80,64},{96,112},{112,96},{1... | collective-permute-start | bytes 24584 | tf_op jit(solution)/shard_map/ppermute | solution.py:134
  136.0 1.1 collective-permute-done.23.d
  137.1 0.7 shard_map.156
  137.8 14.0 %all_to_all.10.parts_ref = f32[16,4,128]{2,1,0:T(4,128)S(1)} all-to-all(f32[16,4,128]{2,1,0:T(4,128)S(1)} %bitcast.38), channel_id=1, replica_groups=mesh['line'=4,'tx'=8,'ty'=16] {'ty'}, dimensions={0} | all-to-all | bytes 65536 | tf_op jit(solution)/shard_map/all_to_all | solution.py:305
  151.8 0.8 shard_map.157
  152.6 3.5 %all-to-all-start.1 = ((f32[16,4,128]{2,1,0:T(4,128)}), f32[16,4,128]{2,1,0:T(4,128)S(1)}, u32[]{:S(2)}, u32[]{:S(2)}) async-start(f32[16,4,128]{2,1,0:T(4,128)} %shard_map.157), calls=%async_computation.1 | async-start | bytes 65536 | tf_op jit(solution)/shard_map/all_to_all | solution.py:325
  156.7 5.8 %all-to-all-done.1 = f32[16,4,128]{2,1,0:T(4,128)S(1)} async-done(((f32[16,4,128]{2,1,0:T(4,128)}), f32[16,4,128]{2,1,0:T(4,128)S(1)}, u32[]{:S(2)}, u32[]{:S(2)}) %all-to-all-start.1) | async-done | bytes 32800 | tf_op jit(solution)/shard_map/all_to_all | solution.py:325
  (72 shorter events, 12.5 us)
Async XLA Ops:
  0.6 24.8 %copy-start.5 = (f32[128,128]{1,0:T(8,128)S(1)}, f32[128,128]{1,0:T(8,128)}, u32[]{:S(2)}) copy-start(f32[128,128]{1,0:T(8,128)} %l_ref.1) | copy-start | bytes 196612
  0.8 0.8 copy-start.1
  1.6 22.5 %copy-start.9 = (f32[4,4,4]{2,1,0:T(4,128)S(1)}, f32[4,4,4]{2,1,0:T(4,128)}, u32[]{:S(2)}) copy-start(f32[4,4,4]{2,1,0:T(4,128)} %param.16) | copy-start | bytes 772
  1.6 23.2 %copy-start.10 = (f32[4,4,4]{2,1,0:T(4,128)S(1)}, f32[4,4,4]{2,1,0:T(4,128)}, u32[]{:S(2)}) copy-start(f32[4,4,4]{2,1,0:T(4,128)} %param.17) | copy-start | bytes 772
  1.6 23.9 %copy-start.8 = (f32[32,128]{1,0:T(8,128)S(1)}, f32[32,128]{1,0:T(8,128)}, u32[]{:S(2)}) copy-start(f32[32,128]{1,0:T(8,128)} %param.24) | copy-start | bytes 49156
  1.6 23.9 %copy-start.3 = (f32[4,128,128]{2,1,0:T(8,128)S(1)}, f32[4,128,128]{2,1,0:T(8,128)}, u32[]{:S(2)}) copy-start(f32[4,128,128]{2,1,0:T(8,128)} %f_ref.1) | copy-start | bytes 786436
  2.2 26.9 %collective-permute-start = (f32[16,128]{1,0:T(8,128)}, f32[16,128]{1,0:T(8,128)S(1)}, u32[]{:S(2)}, u32[]{:S(2)}) collective-permute-start(f32[16,128]{1,0:T(8,128)} %get-tuple-element.54), channel_id=1, source_target_pairs={{16,32},{32,16},{48,64},{64,48},{80,96},{96,80},{17,33},{33,17},{4... | collective-permute-start | bytes 24584 | tf_op jit(solution)/shard_map/ppermute | solution.py:131
  12.4 16.7 %collective-permute-start.1 = (f32[16,128]{1,0:T(8,128)}, f32[16,128]{1,0:T(8,128)S(1)}, u32[]{:S(2)}, u32[]{:S(2)}) collective-permute-start(f32[16,128]{1,0:T(8,128)} %get-tuple-element.55), channel_id=1, source_target_pairs={{0,1},{1,0},{2,3},{3,2},{4,5},{5,4},{6,7},{7,6},{8,9},{9,8},{10,11... | collective-permute-start | bytes 24584 | tf_op jit(solution)/shard_map/ppermute | solution.py:132
  15.5 13.6 %collective-permute-start.2 = (f32[16,128]{1,0:T(8,128)}, f32[16,128]{1,0:T(8,128)S(1)}, u32[]{:S(2)}, u32[]{:S(2)}) collective-permute-start(f32[16,128]{1,0:T(8,128)} %get-tuple-element.56), channel_id=1, source_target_pairs={{1,2},{2,1},{3,4},{4,3},{5,6},{6,5},{7,8},{8,7},{9,10},{10,9},{11,... | collective-permute-start | bytes 24584 | tf_op jit(solution)/shard_map/ppermute | solution.py:133
  16.2 13.0 %collective-permute-start.3 = (f32[16,128]{1,0:T(8,128)S(1)}, f32[16,128]{1,0:T(8,128)S(1)}, u32[]{:S(2)}, u32[]{:S(2)}) collective-permute-start(f32[16,128]{1,0:T(8,128)S(1)} %get-tuple-element.57), channel_id=1, source_target_pairs={{0,16},{16,0},{32,48},{48,32},{64,80},{80,64},{96,112},{112,96},{1... | collective-permute-start | bytes 24584 | tf_op jit(solution)/shard_map/ppermute | solution.py:134
  23.6 5.6 %copy-start.2 = (f32[4,4,4,128]{3,2,1,0:T(4,128)S(1)}, f32[4,4,4,128]{3,2,1,0:T(4,128)}, u32[]{:S(2)}) copy-start(f32[4,4,4,128]{3,2,1,0:T(4,128)} %param.14) | copy-start | bytes 98308
  23.6 5.6 %copy-start.4 = (f32[4,4,4,128]{3,2,1,0:T(4,128)S(1)}, f32[4,4,4,128]{3,2,1,0:T(4,128)}, u32[]{:S(2)}) copy-start(f32[4,4,4,128]{3,2,1,0:T(4,128)} %param.13) | copy-start | bytes 98308
  25.5 1.6 copy-start
  27.1 0.8 copy-start.6
  31.7 4.3 %collective-permute-start.4 = (f32[16,128]{1,0:T(8,128)S(1)}, f32[16,128]{1,0:T(8,128)S(1)}, u32[]{:S(2)}, u32[]{:S(2)}) collective-permute-start(f32[16,128]{1,0:T(8,128)S(1)} %get-tuple-element.64), channel_id=1, source_target_pairs={{0,128},{1,129},{2,130},{3,131},{4,132},{5,133},{6,134},{7,135},{8... | collective-permute-start | bytes 24584 | tf_op jit(solution)/shard_map/ppermute | solution.py:269
  37.5 0.7 collective-permute-start.5
  39.7 0.7 collective-permute-start.6
  43.3 0.7 collective-permute-start.7
  45.5 0.7 collective-permute-start.8
  47.7 13.9 %collective-permute-start.9 = (f32[16,128]{1,0:T(8,128)S(1)}, f32[16,128]{1,0:T(8,128)S(1)}, u32[]{:S(2)}, u32[]{:S(2)}) collective-permute-start(f32[16,128]{1,0:T(8,128)S(1)} %get-tuple-element.76), channel_id=1, source_target_pairs={{128,0},{129,1},{130,2},{131,3},{132,4},{133,5},{134,6},{135,7},{1... | collective-permute-start | bytes 24584 | tf_op jit(solution)/shard_map/ppermute | solution.py:277
  63.7 21.7 %collective-permute-start.10 = (f32[16,128]{1,0:T(8,128)S(1)}, f32[16,128]{1,0:T(8,128)S(1)}, u32[]{:S(2)}, u32[]{:S(2)}) collective-permute-start(f32[16,128]{1,0:T(8,128)S(1)} %get-tuple-element.78), channel_id=1, source_target_pairs={{16,32},{32,16},{48,64},{64,48},{80,96},{96,80},{17,33},{33,17},{4... | collective-permute-start | bytes 24584 | tf_op jit(solution)/shard_map/ppermute | solution.py:131
  77.5 7.9 %collective-permute-start.11 = (f32[16,128]{1,0:T(8,128)S(1)}, f32[16,128]{1,0:T(8,128)S(1)}, u32[]{:S(2)}, u32[]{:S(2)}) collective-permute-start(f32[16,128]{1,0:T(8,128)S(1)} %get-tuple-element.79), channel_id=1, source_target_pairs={{0,1},{1,0},{2,3},{3,2},{4,5},{5,4},{6,7},{7,6},{8,9},{9,8},{10,11... | collective-permute-start | bytes 24584 | tf_op jit(solution)/shard_map/ppermute | solution.py:132
  82.8 2.6 %collective-permute-start.12 = (f32[16,128]{1,0:T(8,128)S(1)}, f32[16,128]{1,0:T(8,128)S(1)}, u32[]{:S(2)}, u32[]{:S(2)}) collective-permute-start(f32[16,128]{1,0:T(8,128)S(1)} %get-tuple-element.80), channel_id=1, source_target_pairs={{1,2},{2,1},{3,4},{4,3},{5,6},{6,5},{7,8},{8,7},{9,10},{10,9},{11,... | collective-permute-start | bytes 24584 | tf_op jit(solution)/shard_map/ppermute | solution.py:133
  83.4 3.1 %collective-permute-start.13 = (f32[16,128]{1,0:T(8,128)S(1)}, f32[16,128]{1,0:T(8,128)S(1)}, u32[]{:S(2)}, u32[]{:S(2)}) collective-permute-start(f32[16,128]{1,0:T(8,128)S(1)} %get-tuple-element.81), channel_id=1, source_target_pairs={{0,16},{16,0},{32,48},{48,32},{64,80},{80,64},{96,112},{112,96},{1... | collective-permute-start | bytes 24584 | tf_op jit(solution)/shard_map/ppermute | solution.py:134
  89.0 2.1 %collective-permute-start.14 = (f32[16,128]{1,0:T(8,128)S(1)}, f32[16,128]{1,0:T(8,128)S(1)}, u32[]{:S(2)}, u32[]{:S(2)}) collective-permute-start(f32[16,128]{1,0:T(8,128)S(1)} %get-tuple-element.83), channel_id=1, source_target_pairs={{0,128},{1,129},{2,130},{3,131},{4,132},{5,133},{6,134},{7,135},{8... | collective-permute-start | bytes 24584 | tf_op jit(solution)/shard_map/ppermute | solution.py:269
  92.7 0.7 collective-permute-start.15
  94.9 0.7 collective-permute-start.16
  98.4 0.7 collective-permute-start.17
  99.1 5.0 %copy-start.7 = (s32[4,4,4]{2,1,0:T(4,128)S(1)}, s32[4,4,4]{2,1,0:T(4,128)}, u32[]{:S(2)}) copy-start(s32[4,4,4]{2,1,0:T(4,128)} %param.23) | copy-start | bytes 772
  100.6 0.7 collective-permute-start.18
  102.8 13.9 %collective-permute-start.19 = (f32[16,128]{1,0:T(8,128)S(1)}, f32[16,128]{1,0:T(8,128)S(1)}, u32[]{:S(2)}, u32[]{:S(2)}) collective-permute-start(f32[16,128]{1,0:T(8,128)S(1)} %get-tuple-element.93), channel_id=1, source_target_pairs={{128,0},{129,1},{130,2},{131,3},{132,4},{133,5},{134,6},{135,7},{1... | collective-permute-start | bytes 24584 | tf_op jit(solution)/shard_map/ppermute | solution.py:277
  118.2 17.7 %collective-permute-start.20 = (f32[16,128]{1,0:T(8,128)S(1)}, f32[16,128]{1,0:T(8,128)S(1)}, u32[]{:S(2)}, u32[]{:S(2)}) collective-permute-start(f32[16,128]{1,0:T(8,128)S(1)} %get-tuple-element.95), channel_id=1, source_target_pairs={{16,32},{32,16},{48,64},{64,48},{80,96},{96,80},{17,33},{33,17},{4... | collective-permute-start | bytes 24584 | tf_op jit(solution)/shard_map/ppermute | solution.py:131
  127.8 8.2 %collective-permute-start.21 = (f32[16,128]{1,0:T(8,128)S(1)}, f32[16,128]{1,0:T(8,128)S(1)}, u32[]{:S(2)}, u32[]{:S(2)}) collective-permute-start(f32[16,128]{1,0:T(8,128)S(1)} %get-tuple-element.96), channel_id=1, source_target_pairs={{0,1},{1,0},{2,3},{3,2},{4,5},{5,4},{6,7},{7,6},{8,9},{9,8},{10,11... | collective-permute-start | bytes 24584 | tf_op jit(solution)/shard_map/ppermute | solution.py:132
  133.4 2.6 %collective-permute-start.22 = (f32[16,128]{1,0:T(8,128)S(1)}, f32[16,128]{1,0:T(8,128)S(1)}, u32[]{:S(2)}, u32[]{:S(2)}) collective-permute-start(f32[16,128]{1,0:T(8,128)S(1)} %get-tuple-element.97), channel_id=1, source_target_pairs={{1,2},{2,1},{3,4},{4,3},{5,6},{6,5},{7,8},{8,7},{9,10},{10,9},{11,... | collective-permute-start | bytes 24584 | tf_op jit(solution)/shard_map/ppermute | solution.py:133
  134.0 3.1 %collective-permute-start.23 = (f32[16,128]{1,0:T(8,128)S(1)}, f32[16,128]{1,0:T(8,128)S(1)}, u32[]{:S(2)}, u32[]{:S(2)}) collective-permute-start(f32[16,128]{1,0:T(8,128)S(1)} %get-tuple-element.98), channel_id=1, source_target_pairs={{0,16},{16,0},{32,48},{48,32},{64,80},{80,64},{96,112},{112,96},{1... | collective-permute-start | bytes 24584 | tf_op jit(solution)/shard_map/ppermute | solution.py:134
  152.6 9.9 %all-to-all-start.1 = ((f32[16,4,128]{2,1,0:T(4,128)}), f32[16,4,128]{2,1,0:T(4,128)S(1)}, u32[]{:S(2)}, u32[]{:S(2)}) async-start(f32[16,4,128]{2,1,0:T(4,128)} %shard_map.157), calls=%async_computation.1 | async-start | bytes 65536 | tf_op jit(solution)/shard_map/all_to_all | solution.py:325

commit v3 on v2

--- a/solution.py
+++ b/solution.py
@@ -16,12 +16,15 @@
 def call(kernel, outs, *args, scratch=(), whole=0):
     return pl.pallas_call(
         kernel,
-        in_specs=[pl.BlockSpec(memory_space=pl.ANY)] * whole + [SPEC] * (len(args) - whole),
+        in_specs=[pl.BlockSpec(memory_space=pltpu.HBM)] * whole + [SPEC] * (len(args) - whole),
         out_specs=[SPEC] * len(outs),
         out_shape=[pltpu.VMEM(s, d) for s, d in outs],
         scratch_shapes=list(scratch),
         compiler_params=pltpu.CompilerParams(vmem_limit_bytes=24 << 20),
-    )(*args[:whole], *[pltpu.with_memory_space_constraint(a, pltpu.VMEM) for a in args[whole:]])
+    )(
+        *[pltpu.with_memory_space_constraint(a, pltpu.HBM) for a in args[:whole]],
+        *[pltpu.with_memory_space_constraint(a, pltpu.VMEM) for a in args[whole:]],
+    )
 
 
 def halves(v):
@@ -75,25 +78,29 @@
     return xs
 
 
-def put_edges(x_ref, par_ref, outs, n, lx, ly):
+def is_even(axis):
+    return lax.axis_index(axis) % 2 == 0
+
+
+def put_edges(x_ref, outs, n, lx, ly):
     a_ref, b_ref, c_ref, d_ref = outs
     lines = lx * ly
     first = jnp.concatenate([x_ref[i * lines : i * lines + ly, :] for i in range(n)], 0)
     last = jnp.concatenate([x_ref[(i + 1) * lines - ly : (i + 1) * lines, :] for i in range(n)], 0)
-    even = par_ref[0:1, :] < 0.5
+    even = is_even("tx")
     a_ref[...] = jnp.where(even, last, first)
     b_ref[...] = jnp.where(even, first, last)
     first = x_ref[pl.ds(0, n * lx, stride=ly), :]
     last = x_ref[pl.ds(ly - 1, n * lx, stride=ly), :]
-    even = par_ref[1:2, :] < 0.5
+    even = is_even("ty")
     c_ref[...] = jnp.where(even, last, first)
     d_ref[...] = jnp.where(even, first, last)
 
 
-def tangential(x_ref, got, par_ref, cols, blocks, near, n, lx, ly):
+def tangential(x_ref, got, cols, blocks, near, n, lx, ly):
     lines = lx * ly
     x = x_ref[...]
-    even = par_ref[0:1, :] < 0.5
+    even = is_even("tx")
     b, c, d, a = (r[...] for r in got)
     below, above = jnp.where(even, b, a), jnp.where(even, a, b)
     near[0] = pltpu.roll(x, ly, 0)
@@ -101,7 +108,7 @@
     for i in range(n):
         near[0, i * lines : i * lines + ly, :] = below[i * ly : (i + 1) * ly]
         near[1, (i + 1) * lines - ly : (i + 1) * lines, :] = above[i * ly : (i + 1) * ly]
-    even = par_ref[1:2, :] < 0.5
+    even = is_even("ty")
     below, above = jnp.where(even, d, c), jnp.where(even, c, d)
     row = lax.broadcasted_iota(jnp.int32, x.shape, 0) % ly
     near[2] = pltpu.roll(x, 1, 0)
@@ -160,63 +167,92 @@
     start = start_field.reshape(rows, width)
     w = line_inverse.reshape(rows * width, width)
 
-    kinds = jnp.arange(4, dtype=jnp.int32)
-    face = jnp.where(face_kind[:, None] == kinds[None, :, None, None, None], face_scale[:, None], 0.0)
-    agg = agglomerate.reshape(rows)
-    agg_row, agg_part = agg // quarter, agg % quarter
-    cols = jnp.concatenate(
-        [
-            face.reshape(16, rows),
-            lower_scale.reshape(1, rows),
-            upper_scale.reshape(1, rows),
-            agg_row.astype(F32)[None],
-            agg_part.astype(F32)[None],
-            jnp.zeros((12, rows), F32),
-        ],
-        0,
-    ).T
-    agg_lane = jnp.broadcast_to(agg_row.astype(F32)[None], (8, rows))
-    par = jnp.stack([lax.axis_index("tx") % 2, lax.axis_index("ty") % 2]).astype(F32)
-    par = jnp.broadcast_to(jnp.pad(par, (0, 6))[:, None], (8, width))
-    eye = jnp.eye(quarter, dtype=F32)
-    ci = coarse_inverse.reshape(owned_rows, quarter, cb, 1, cb) * eye[None, :, None, :, None]
-    ci = ci.reshape(owned_rows * width, width)
-    spread_op = jnp.tile(restriction, (quarter, 1))
-
     block, edge = ((rows, width), F32), ((lines, width), F32)
     half, half4 = ((width, width), BF16), ((4, width, width), BF16)
     edges4 = [((n * ly, width), F32)] * 2 + [((n * lx, width), F32)] * 2
 
-    def first_edges(x_ref, par_ref, *outs):
-        put_edges(x_ref, par_ref, outs, n, lx, ly)
-
-    sends = call(first_edges, edges4, start, par)
-
-    def prepare(w_ref, l_ref, u_ref, f_ref, r_ref, c_ref, *outs):
-        copy = pltpu.make_async_copy(w_ref, outs[10], outs[11])
-        copy.start()
-        for k, src in enumerate((l_ref, u_ref, f_ref, r_ref, c_ref)):
-            outs[2 * k][...], outs[2 * k + 1][...] = halves(src[...])
-        copy.wait()
-
-    lh, ll, uh, ul, fh, fl, rh, rl, ch, cl, w = call(
-        prepare,
-        [half, half, half, half, half4, half4, half, half]
-        + [((owned_rows * width, width), BF16)] * 2
-        + [((rows * width, width), BF16)],
+    def first_edges(x_ref, *outs):
+        put_edges(x_ref, outs, n, lx, ly)
+
+    sends = call(first_edges, edges4, start)
+
+    raw = (
         w,
         lower_block,
         upper_block,
         face_blocks,
-        spread_op,
-        ci,
-        scratch=[pltpu.SemaphoreType.DMA],
-        whole=1,
-    )
-
-    def open_forward(x_ref, a, b, c, d, par_ref, cols_ref, fh_ref, fl_ref, rhs_ref, lh_ref, ll_ref, w_ref, g_ref, y_ref, f_ref, near):
+        restriction,
+        coarse_inverse.reshape(owned_rows * width, cb),
+        face_kind,
+        face_scale,
+        lower_scale,
+        upper_scale,
+        agglomerate,
+    )
+
+    def prepare(*refs):
+        outs = refs[len(raw) : len(raw) + 13]
+        held, sems = refs[len(raw) + 13 : -1], refs[-1]
+        copies = [
+            pltpu.make_async_copy(src, dst, sems.at[k])
+            for k, (src, dst) in enumerate(zip(refs, (outs[10], *held)))
+        ]
+        for copy in copies:
+            copy.start()
+        for copy in copies[1:]:
+            copy.wait()
+        l_ref, u_ref, f_ref, r_ref, c_ref, kind_ref, face_ref, low_ref, up_ref, agg_ref = held
+        for k, src in enumerate((l_ref, u_ref, f_ref)):
+            outs[2 * k][...], outs[2 * k + 1][...] = halves(src[...])
+        outs[6][...], outs[7][...] = halves(jnp.concatenate([r_ref[...]] * quarter, 0))
+        lane = lax.broadcasted_iota(jnp.int32, (cb, width), 1) % cb
+        wide = (lane == lax.broadcasted_iota(jnp.int32, (cb, width), 0)).astype(F32).astype(BF16)
+        part = (lax.broadcasted_iota(jnp.int32, (owned_rows * width, width), 0) // cb) % quarter
+        mine = part == lax.broadcasted_iota(jnp.int32, (owned_rows * width, width), 1) // cb
+        for k, piece in enumerate(halves(c_ref[...])):
+            outs[8 + k][...] = jnp.where(mine, nn(piece, wide), 0.0).astype(BF16)
+        groups = rows // ly
+        row = lax.broadcasted_iota(jnp.int32, (rows, groups), 0)
+        up = (row // ly == lax.broadcasted_iota(jnp.int32, (rows, groups), 1)).astype(F32).astype(BF16)
+        row = lax.broadcasted_iota(jnp.int32, (rows, ly), 0)
+        own = row % ly == lax.broadcasted_iota(jnp.int32, (rows, ly), 1)
+
+        def column(ref, *at):
+            src = jnp.concatenate([ref[(*at, i)] for i in range(n)], 0).astype(F32)
+            hi, lo = halves(src)
+            return jnp.sum(jnp.where(own, nn(up, hi) + nn(up, lo), 0.0), axis=1, keepdims=True)
+
+        agg = column(agg_ref).astype(jnp.int32)
+        row_of = (agg // quarter).astype(F32)
+        listed = []
+        for side in range(4):
+            kind, face = column(kind_ref, side), column(face_ref, side)
+            listed += [jnp.where(kind == float(k), face, 0.0) for k in range(4)]
+        listed += [column(low_ref), column(up_ref), row_of, (agg % quarter).astype(F32)]
+        lane = lax.broadcasted_iota(jnp.int32, (rows, width), 1)
+        cols = jnp.zeros((rows, width), F32)
+        for k, value in enumerate(listed):
+            cols = jnp.where(lane == k, value, cols)
+        outs[11][...] = cols
+        square = lax.broadcasted_iota(jnp.int32, (rows, rows), 0) == lax.broadcasted_iota(jnp.int32, (rows, rows), 1)
+        across = jnp.sum(jnp.where(square, row_of, 0.0), axis=0, keepdims=True)
+        outs[12][...] = jnp.broadcast_to(across, (8, rows))
+        copies[0].wait()
+
+    lh, ll, uh, ul, fh, fl, rh, rl, ch, cl, w, cols, agg_lane = call(
+        prepare,
+        [half, half, half, half, half4, half4, half, half]
+        + [((owned_rows * width, width), BF16)] * 2
+        + [((rows * width, width), BF16), block, ((8, rows), F32)],
+        *raw,
+        scratch=[pltpu.VMEM(a.shape, a.dtype) for a in raw[1:]]
+        + [pltpu.SemaphoreType.DMA((len(raw),))],
+        whole=len(raw),
+    )
+
+    def open_forward(x_ref, a, b, c, d, cols_ref, fh_ref, fl_ref, rhs_ref, lh_ref, ll_ref, w_ref, g_ref, y_ref, f_ref, near):
         cols = cols_ref[...]
-        total = tangential(x_ref, (a, b, c, d), par_ref, cols, (fh_ref, fl_ref), near, n, lx, ly)
+        total = tangential(x_ref, (a, b, c, d), cols, (fh_ref, fl_ref), near, n, lx, ly)
         g = rhs_ref[...] - total
         g_ref[...] = g
         zero = jnp.zeros((lines, width), F32)
@@ -246,13 +282,13 @@
         xs = backward(y_ref[...], arr, w_ref, (uh_ref[...], ul_ref[...]), cols_ref[...], n, lines)
         x_ref[...] = xs[0]
 
-    def close_backward(last, y_ref, arr_ref, got_ref, prev_ref, par_ref, cols_ref, uh_ref, ul_ref, w_ref, x_ref, d_ref, *outs):
+    def close_backward(last, y_ref, arr_ref, got_ref, prev_ref, cols_ref, uh_ref, ul_ref, w_ref, x_ref, d_ref, *outs):
         arr = arr_ref[...] + got_ref[...]
         xs = backward(y_ref[...], arr, w_ref, (uh_ref[...], ul_ref[...]), cols_ref[...], n, lines)
         x = jnp.concatenate(xs, 0)
         x_ref[...] = x
         d_ref[...] = prev_ref[...] - x
-        put_edges(d_ref if last else x_ref, par_ref, outs, n, lx, ly)
+        put_edges(d_ref if last else x_ref, outs, n, lx, ly)
 
     field = start
     change = None
@@ -261,7 +297,7 @@
         g, y, ahead = call(
             open_forward,
             [block, block, edge],
-            field, *got, par, cols, fh, fl, rhs, lh, ll, w,
+            field, *got, cols, fh, fl, rhs, lh, ll, w,
             scratch=[pltpu.VMEM((4, rows, width), F32)],
         )
         inc = jnp.zeros((lines, width), F32)
@@ -278,15 +314,15 @@
         out = call(
             functools.partial(close_backward, sweep == SWEEPS - 1),
             [block, block] + edges4,
-            y, arr, recv, field, par, cols, uh, ul, w,
+            y, arr, recv, field, cols, uh, ul, w,
         )
         field, change, sends = out[0], out[1], out[2:]
 
     got = exchange(sends)
 
-    def restrict(x_ref, a, b, c, d, par_ref, cols_ref, fh_ref, fl_ref, rh_ref, rl_ref, lane_ref, res_ref, part_ref, near):
+    def restrict(x_ref, a, b, c, d, cols_ref, fh_ref, fl_ref, rh_ref, rl_ref, lane_ref, res_ref, part_ref, near):
         cols = cols_ref[...]
-        res = tangential(x_ref, (a, b, c, d), par_ref, cols, (fh_ref, fl_ref), near, n, lx, ly)
+        res = tangential(x_ref, (a, b, c, d), cols, (fh_ref, fl_ref), near, n, lx, ly)
         res_ref[...] = res
         proj = times(res, (rh_ref[...], rl_ref[...]))
         part = lax.broadcasted_iota(jnp.int32, (rows, width), 1) // cb
@@ -299,7 +335,7 @@
     residual, partial = call(
         restrict,
         [block, ((agg_rows, width), F32)],
-        change, *got, par, cols, fh, fl, rh, rl, agg_lane,
+        change, *got, cols, fh, fl, rh, rl, agg_lane,
         scratch=[pltpu.VMEM((4, rows, width), F32)],
     )
     parts = lax.all_to_all(partial.reshape(owners, owned_rows, width), "ty", 0, 0, tiled=True)

time: 165 us -> 155 us (0.939)
  local copies, waits for them, and re-layouts: 10.3 us -> 2 us
  other arithmetic: 2.62 us -> 0 us
    unnamed x24 -> x6, local copies, waits for them, and re-layouts: 4.46 us -> 2 us
    reshape x4 -> x0, local copies, waits for them, and re-layouts: 2.25 us -> none  [the longest x2 0.87 us: body(): agg = agglomerate.reshape(rows)]
  transfers between devices with their start and end apart: 25 -> 25, of which waited for: 7 -> 7; matrix products, arithmetic and copies ran while one was open for 5% -> 0% of each run, Pallas kernels for 0% -> 2%
where the time goes in v3:
time: 155 us; the launch traced here: 154 us
  starting transfers between devices  71.7 us (46%)
  waiting for transfers between devices  34.7 us (22%)
  Pallas kernels  30.6 us (20%)
  blocking collectives  14 us (9%)
  local copies, waits for them, and re-layouts  2 us (1%)
    ppermute x3, starting transfers between devices, exchange(): b = lax.ppermute(b, 'tx', swaps(nx, 1))  33.5 us
    pallas_call x19, Pallas kernels, call(): pl.pallas_call(kernel, in_specs=[pl.BlockSpec(memory_space=pltpu.HBM)] *...  30.6 us
    ppermute x2, waiting for transfers between devices, body(): recv = lax.ppermute(behind, 'line', [(1, 0)])  25.1 us
    all_to_all x1, blocking collectives, body(): lax.all_to_all(partial.reshape(owners, owned_rows, width), 'ty', 0, 0, ti...  14 us
    ppermute x3, starting transfers between devices, exchange(): c = lax.ppermute(c, 'ty', swaps(ny, 0))  14 us
    ppermute x4, starting transfers between devices, body(): recv = lax.ppermute(ahead, 'line', [(k, k + 1)])  6.24 us
    all_to_all x1, waiting for transfers between devices, body(): update = lax.all_to_all(copies, 'ty', 0, 0, tiled=True)  5.77 us
    ppermute x3, starting transfers between devices, exchange(): a = lax.ppermute(a, 'tx', swaps(nx, 0))  5.76 us
  transfers between devices with their start and end apart: 25, of which 7 were waited for; matrix products, arithmetic and copies ran while one was open for 0% of the time, Pallas kernels for 2%

profile of v3, /device:TPU:1, one launch (start us, length us, event | category | flops | bytes accessed | tf_op | source)
XLA Modules:
  0.0 154.0 jit_solution(7049782365621140871)
XLA Ops:
  0.6 0.7 copy-done
  1.4 10.2 %collective-permute-start = (f32[16,128]{1,0:T(8,128)S(1)}, f32[16,128]{1,0:T(8,128)S(1)}, u32[]{:S(2)}, u32[]{:S(2)}) collective-permute-start(f32[16,128]{1,0:T(8,128)S(1)} %get-tuple-element.56), channel_id=1, source_target_pairs={{16,32},{32,16},{48,64},{64,48},{80,96},{96,80},{17,33},{33,17},{4... | collective-permute-start | bytes 24584 | tf_op jit(solution)/shard_map/ppermute | solution.py:138
  11.6 3.1 %collective-permute-start.1 = (f32[16,128]{1,0:T(8,128)S(1)}, f32[16,128]{1,0:T(8,128)S(1)}, u32[]{:S(2)}, u32[]{:S(2)}) collective-permute-start(f32[16,128]{1,0:T(8,128)S(1)} %get-tuple-element.57), channel_id=1, source_target_pairs={{0,1},{1,0},{2,3},{3,2},{4,5},{5,4},{6,7},{7,6},{8,9},{9,8},{10,11... | collective-permute-start | bytes 24584 | tf_op jit(solution)/shard_map/ppermute | solution.py:139
  15.4 1.9 %collective-permute-start.3 = (f32[16,128]{1,0:T(8,128)S(1)}, f32[16,128]{1,0:T(8,128)S(1)}, u32[]{:S(2)}, u32[]{:S(2)}) collective-permute-start(f32[16,128]{1,0:T(8,128)S(1)} %get-tuple-element.59), channel_id=1, source_target_pairs={{0,16},{16,0},{32,48},{48,32},{64,80},{80,64},{96,112},{112,96},{1... | collective-permute-start | bytes 24584 | tf_op jit(solution)/shard_map/ppermute | solution.py:141
  17.3 2.3 %shard_map.141 = (bf16[128,128]{1,0:T(8,128)(2,1)S(1)}, bf16[128,128]{1,0:T(8,128)(2,1)S(1)}, bf16[128,128]{1,0:T(8,128)(2,1)S(1)}, bf16[128,128]{1,0:T(8,128)(2...) custom-call(bf16[8192,128]{1,0:T(8,128)(2,1)} %bitcast.17, ...), custom_call_target="tpu_custom_call" | custom-call | tf_op jit(solution)/shard_map/pallas_call | solution.py:17
  19.7 2.5 %shard_map.142 = (f32[64,128]{1,0:T(8,128)S(1)}, f32[64,128]{1,0:T(8,128)}, f32[16,128]{1,0:T(8,128)S(1)}) custom-call(f32[64,128]{1,0:T(8,128)S(1)} %bitcast.11, f32[16,128]{1,0:T(8,128)S(1)} %collective-permute-done.a, f32[16,128]{1,0:T(8,128)S(1)} %collective-permute-done.1.b, f32[16,128]{1,0:T(8,128)S(1)} %collective-permute-done.2.c, ...), custom_call_target="tpu_custom_call" | custom-call | tf_op jit(solution)/shard_map/pallas_call | solution.py:17
  22.2 3.5 %collective-permute-start.4 = (f32[16,128]{1,0:T(8,128)S(1)}, f32[16,128]{1,0:T(8,128)S(1)}, u32[]{:S(2)}, u32[]{:S(2)}) collective-permute-start(f32[16,128]{1,0:T(8,128)S(1)} %get-tuple-element.67), channel_id=1, source_target_pairs={{0,128},{1,129},{2,130},{3,131},{4,132},{5,133},{6,134},{7,135},{8... | collective-permute-start | bytes 24584 | tf_op jit(solution)/shard_map/ppermute | solution.py:305
  25.8 0.8 collective-permute-done.4.got_ref
  26.5 1.5 shard_map.143
  28.0 0.7 collective-permute-start.5
  28.7 1.5 shard_map.144
  30.2 0.7 collective-permute-start.6
  30.9 2.9 %shard_map.145 = (f32[64,128]{1,0:T(8,128)S(1)}, f32[16,128]{1,0:T(8,128)S(1)}) custom-call(f32[64,128]{1,0:T(8,128)S(1)} %get-tuple-element.66.g_ref, f32[16,128]{1,0:T(8,128)S(1)} %get-tuple-element.70.inc_ref, f32[16,128]{1,0:T(8,128)S(1)} %collective-permute-done.6.got_ref, f32[64,128]{1,0:T(8,128)S(1)} %get-tuple-element.60.cols_ref, ...), custom_call_target="tpu_custom_call" | custom-call | tf_op jit(solution)/shard_map/pallas_call | solution.py:17
  33.8 0.7 collective-permute-start.7
  34.5 1.5 shard_map.146
  36.0 0.7 collective-permute-start.8
  36.7 1.5 shard_map.147
  38.2 1.3 collective-permute-start.9
  39.5 12.6 %collective-permute-done.9.got_ref = f32[16,128]{1,0:T(8,128)S(1)} collective-permute-done((f32[16,128]{1,0:T(8,128)S(1)}, f32[16,128]{1,0:T(8,128)S(1)}, u32[]{:S(2)}, u32[]{:S(2)}) %collective-permute-start.9) | collective-permute-done | bytes 8224 | tf_op jit(solution)/shard_map/ppermute | solution.py:313
  52.1 2.1 %shard_map.148 = (f32[64,128]{1,0:T(8,128)S(1)}, f32[64,128]{1,0:T(8,128)}, f32[16,128]{1,0:T(8,128)S(1)}, f32[16,128]{1,0:T(8,128)S(1)}, f32[16,128]{1,0:T(8,128)S(1)}, /*index=5*/f32[16,128]{1,0:T(8,128)S(1)}) custom-call(f32[64,128]{1,0:T(8,128)S(1)} %get-tuple-element.74.y_ref, f32[16,128]{1,0:T(8,128)S(1)} %get-tuple-element.78.arr_ref, ...), custom_call_target="tpu_custom_call" | custom-call | tf_op jit(solution)/shard_map/pallas_call | solution.py:17
  54.2 13.8 %collective-permute-start.10 = (f32[16,128]{1,0:T(8,128)S(1)}, f32[16,128]{1,0:T(8,128)S(1)}, u32[]{:S(2)}, u32[]{:S(2)}) collective-permute-start(f32[16,128]{1,0:T(8,128)S(1)} %get-tuple-element.81), channel_id=1, source_target_pairs={{16,32},{32,16},{48,64},{64,48},{80,96},{96,80},{17,33},{33,17},{4... | collective-permute-start | bytes 24584 | tf_op jit(solution)/shard_map/ppermute | solution.py:138
  68.0 5.3 %collective-permute-start.11 = (f32[16,128]{1,0:T(8,128)S(1)}, f32[16,128]{1,0:T(8,128)S(1)}, u32[]{:S(2)}, u32[]{:S(2)}) collective-permute-start(f32[16,128]{1,0:T(8,128)S(1)} %get-tuple-element.82), channel_id=1, source_target_pairs={{0,1},{1,0},{2,3},{3,2},{4,5},{5,4},{6,7},{7,6},{8,9},{9,8},{10,11... | collective-permute-start | bytes 24584 | tf_op jit(solution)/shard_map/ppermute | solution.py:139
  74.0 1.9 %collective-permute-start.13 = (f32[16,128]{1,0:T(8,128)S(1)}, f32[16,128]{1,0:T(8,128)S(1)}, u32[]{:S(2)}, u32[]{:S(2)}) collective-permute-start(f32[16,128]{1,0:T(8,128)S(1)} %get-tuple-element.84), channel_id=1, source_target_pairs={{0,16},{16,0},{32,48},{48,32},{64,80},{80,64},{96,112},{112,96},{1... | collective-permute-start | bytes 24584 | tf_op jit(solution)/shard_map/ppermute | solution.py:141
  75.9 1.1 collective-permute-done.13.d
  77.0 2.5 %shard_map.149 = (f32[64,128]{1,0:T(8,128)S(1)}, f32[64,128]{1,0:T(8,128)}, f32[16,128]{1,0:T(8,128)S(1)}) custom-call(f32[64,128]{1,0:T(8,128)S(1)} %get-tuple-element.80.x_ref.prev_ref, f32[16,128]{1,0:T(8,128)S(1)} %collective-permute-done.10.a, f32[16,128]{1,0:T(8,128)S(1)} %collective-permute-done.11.b, f32[16,128]{1,0:T(8,128)S(1)} %collective-permute-done.12.c, ...), custom_call_target="tpu_custom_call" | custom-call | tf_op jit(solution)/shard_map/pallas_call | solution.py:17
  79.6 1.4 collective-permute-start.14
  80.9 0.8 collective-permute-done.14.got_ref
  81.7 1.5 shard_map.150
  83.2 0.7 collective-permute-start.15
  83.9 1.5 shard_map.151
  85.4 0.7 collective-permute-start.16
  86.1 2.9 %shard_map.152 = (f32[64,128]{1,0:T(8,128)S(1)}, f32[16,128]{1,0:T(8,128)S(1)}) custom-call(f32[64,128]{1,0:T(8,128)S(1)} %get-tuple-element.85.g_ref, f32[16,128]{1,0:T(8,128)S(1)} %get-tuple-element.89.inc_ref, f32[16,128]{1,0:T(8,128)S(1)} %collective-permute-done.16.got_ref, f32[64,128]{1,0:T(8,128)S(1)} %get-tuple-element.60.cols_ref, ...), custom_call_target="tpu_custom_call" | custom-call | tf_op jit(solution)/shard_map/pallas_call | solution.py:17
  89.0 0.7 collective-permute-start.17
  89.7 1.5 shard_map.153
  91.2 0.7 collective-permute-start.18
  91.9 1.5 shard_map.154
  93.4 1.3 collective-permute-start.19
  94.7 12.6 %collective-permute-done.19.got_ref = f32[16,128]{1,0:T(8,128)S(1)} collective-permute-done((f32[16,128]{1,0:T(8,128)S(1)}, f32[16,128]{1,0:T(8,128)S(1)}, u32[]{:S(2)}, u32[]{:S(2)}) %collective-permute-start.19) | collective-permute-done | bytes 8224 | tf_op jit(solution)/shard_map/ppermute | solution.py:313
  107.3 1.5 shard_map.155
  108.8 9.5 %collective-permute-start.20 = (f32[16,128]{1,0:T(8,128)S(1)}, f32[16,128]{1,0:T(8,128)S(1)}, u32[]{:S(2)}, u32[]{:S(2)}) collective-permute-start(f32[16,128]{1,0:T(8,128)S(1)} %get-tuple-element.98), channel_id=1, source_target_pairs={{16,32},{32,16},{48,64},{64,48},{80,96},{96,80},{17,33},{33,17},{4... | collective-permute-start | bytes 24584 | tf_op jit(solution)/shard_map/ppermute | solution.py:138
  118.4 5.6 %collective-permute-start.21 = (f32[16,128]{1,0:T(8,128)S(1)}, f32[16,128]{1,0:T(8,128)S(1)}, u32[]{:S(2)}, u32[]{:S(2)}) collective-permute-start(f32[16,128]{1,0:T(8,128)S(1)} %get-tuple-element.99), channel_id=1, source_target_pairs={{0,1},{1,0},{2,3},{3,2},{4,5},{5,4},{6,7},{7,6},{8,9},{9,8},{10,11... | collective-permute-start | bytes 24584 | tf_op jit(solution)/shard_map/ppermute | solution.py:139
  124.6 1.9 %collective-permute-start.23 = (f32[16,128]{1,0:T(8,128)S(1)}, f32[16,128]{1,0:T(8,128)S(1)}, u32[]{:S(2)}, u32[]{:S(2)}) collective-permute-start(f32[16,128]{1,0:T(8,128)S(1)} %get-tuple-element.101), channel_id=1, source_target_pairs={{0,16},{16,0},{32,48},{48,32},{64,80},{80,64},{96,112},{112,96},{1... | collective-permute-start | bytes 24584 | tf_op jit(solution)/shard_map/ppermute | solution.py:141
  126.6 1.1 collective-permute-done.23.d
  127.7 0.7 shard_map.156
  128.4 14.0 %all_to_all.10.parts_ref = f32[16,4,128]{2,1,0:T(4,128)S(1)} all-to-all(f32[16,4,128]{2,1,0:T(4,128)S(1)} %bitcast.16), channel_id=1, replica_groups=mesh['line'=4,'tx'=8,'ty'=16] {'ty'}, dimensions={0} | all-to-all | bytes 65536 | tf_op jit(solution)/shard_map/all_to_all | solution.py:341
  142.4 0.8 shard_map.157
  143.2 3.5 %all-to-all-start.1 = ((f32[16,4,128]{2,1,0:T(4,128)}), f32[16,4,128]{2,1,0:T(4,128)S(1)}, u32[]{:S(2)}, u32[]{:S(2)}) async-start(f32[16,4,128]{2,1,0:T(4,128)} %shard_map.157), calls=%async_computation.1 | async-start | bytes 65536 | tf_op jit(solution)/shard_map/all_to_all | solution.py:361
  147.3 5.8 %all-to-all-done.1 = f32[16,4,128]{2,1,0:T(4,128)S(1)} async-done(((f32[16,4,128]{2,1,0:T(4,128)}), f32[16,4,128]{2,1,0:T(4,128)S(1)}, u32[]{:S(2)}, u32[]{:S(2)}) %all-to-all-start.1) | async-done | bytes 32800 | tf_op jit(solution)/shard_map/all_to_all | solution.py:361
  (29 shorter events, 3.6 us)
Async XLA Ops:
  0.6 0.8 copy-start
  1.4 18.3 %copy-start.1 = (f32[4,4,4,128]{3,2,1,0:T(4,128)S(1)}, f32[4,4,4,128]{3,2,1,0:T(4,128)}, u32[]{:S(2)}) copy-start(f32[4,4,4,128]{3,2,1,0:T(4,128)} %param.13) | copy-start | bytes 98308
  1.4 18.3 %collective-permute-start = (f32[16,128]{1,0:T(8,128)S(1)}, f32[16,128]{1,0:T(8,128)S(1)}, u32[]{:S(2)}, u32[]{:S(2)}) collective-permute-start(f32[16,128]{1,0:T(8,128)S(1)} %get-tuple-element.56), channel_id=1, source_target_pairs={{16,32},{32,16},{48,64},{64,48},{80,96},{96,80},{17,33},{33,17},{4... | collective-permute-start | bytes 24584 | tf_op jit(solution)/shard_map/ppermute | solution.py:138
  11.6 8.1 %collective-permute-start.1 = (f32[16,128]{1,0:T(8,128)S(1)}, f32[16,128]{1,0:T(8,128)S(1)}, u32[]{:S(2)}, u32[]{:S(2)}) collective-permute-start(f32[16,128]{1,0:T(8,128)S(1)} %get-tuple-element.57), channel_id=1, source_target_pairs={{0,1},{1,0},{2,3},{3,2},{4,5},{5,4},{6,7},{7,6},{8,9},{9,8},{10,11... | collective-permute-start | bytes 24584 | tf_op jit(solution)/shard_map/ppermute | solution.py:139
  14.7 4.9 %collective-permute-start.2 = (f32[16,128]{1,0:T(8,128)S(1)}, f32[16,128]{1,0:T(8,128)S(1)}, u32[]{:S(2)}, u32[]{:S(2)}) collective-permute-start(f32[16,128]{1,0:T(8,128)S(1)} %get-tuple-element.58), channel_id=1, source_target_pairs={{1,2},{2,1},{3,4},{4,3},{5,6},{6,5},{7,8},{8,7},{9,10},{10,9},{11,... | collective-permute-start | bytes 24584 | tf_op jit(solution)/shard_map/ppermute | solution.py:140
  15.4 4.3 %collective-permute-start.3 = (f32[16,128]{1,0:T(8,128)S(1)}, f32[16,128]{1,0:T(8,128)S(1)}, u32[]{:S(2)}, u32[]{:S(2)}) collective-permute-start(f32[16,128]{1,0:T(8,128)S(1)} %get-tuple-element.59), channel_id=1, source_target_pairs={{0,16},{16,0},{32,48},{48,32},{64,80},{80,64},{96,112},{112,96},{1... | collective-permute-start | bytes 24584 | tf_op jit(solution)/shard_map/ppermute | solution.py:141
  22.2 4.3 %collective-permute-start.4 = (f32[16,128]{1,0:T(8,128)S(1)}, f32[16,128]{1,0:T(8,128)S(1)}, u32[]{:S(2)}, u32[]{:S(2)}) collective-permute-start(f32[16,128]{1,0:T(8,128)S(1)} %get-tuple-element.67), channel_id=1, source_target_pairs={{0,128},{1,129},{2,130},{3,131},{4,132},{5,133},{6,134},{7,135},{8... | collective-permute-start | bytes 24584 | tf_op jit(solution)/shard_map/ppermute | solution.py:305
  28.0 0.7 collective-permute-start.5
  30.2 0.7 collective-permute-start.6
  33.8 0.7 collective-permute-start.7
  36.0 0.7 collective-permute-start.8
  38.2 13.9 %collective-permute-start.9 = (f32[16,128]{1,0:T(8,128)S(1)}, f32[16,128]{1,0:T(8,128)S(1)}, u32[]{:S(2)}, u32[]{:S(2)}) collective-permute-start(f32[16,128]{1,0:T(8,128)S(1)} %get-tuple-element.79), channel_id=1, source_target_pairs={{128,0},{129,1},{130,2},{131,3},{132,4},{133,5},{134,6},{135,7},{1... | collective-permute-start | bytes 24584 | tf_op jit(solution)/shard_map/ppermute | solution.py:313
  54.2 21.7 %collective-permute-start.10 = (f32[16,128]{1,0:T(8,128)S(1)}, f32[16,128]{1,0:T(8,128)S(1)}, u32[]{:S(2)}, u32[]{:S(2)}) collective-permute-start(f32[16,128]{1,0:T(8,128)S(1)} %get-tuple-element.81), channel_id=1, source_target_pairs={{16,32},{32,16},{48,64},{64,48},{80,96},{96,80},{17,33},{33,17},{4... | collective-permute-start | bytes 24584 | tf_op jit(solution)/shard_map/ppermute | solution.py:138
  68.0 7.9 %collective-permute-start.11 = (f32[16,128]{1,0:T(8,128)S(1)}, f32[16,128]{1,0:T(8,128)S(1)}, u32[]{:S(2)}, u32[]{:S(2)}) collective-permute-start(f32[16,128]{1,0:T(8,128)S(1)} %get-tuple-element.82), channel_id=1, source_target_pairs={{0,1},{1,0},{2,3},{3,2},{4,5},{5,4},{6,7},{7,6},{8,9},{9,8},{10,11... | collective-permute-start | bytes 24584 | tf_op jit(solution)/shard_map/ppermute | solution.py:139
  73.3 2.6 %collective-permute-start.12 = (f32[16,128]{1,0:T(8,128)S(1)}, f32[16,128]{1,0:T(8,128)S(1)}, u32[]{:S(2)}, u32[]{:S(2)}) collective-permute-start(f32[16,128]{1,0:T(8,128)S(1)} %get-tuple-element.83), channel_id=1, source_target_pairs={{1,2},{2,1},{3,4},{4,3},{5,6},{6,5},{7,8},{8,7},{9,10},{10,9},{11,... | collective-permute-start | bytes 24584 | tf_op jit(solution)/shard_map/ppermute | solution.py:140
  74.0 3.1 %collective-permute-start.13 = (f32[16,128]{1,0:T(8,128)S(1)}, f32[16,128]{1,0:T(8,128)S(1)}, u32[]{:S(2)}, u32[]{:S(2)}) collective-permute-start(f32[16,128]{1,0:T(8,128)S(1)} %get-tuple-element.84), channel_id=1, source_target_pairs={{0,16},{16,0},{32,48},{48,32},{64,80},{80,64},{96,112},{112,96},{1... | collective-permute-start | bytes 24584 | tf_op jit(solution)/shard_map/ppermute | solution.py:141
  79.6 2.1 %collective-permute-start.14 = (f32[16,128]{1,0:T(8,128)S(1)}, f32[16,128]{1,0:T(8,128)S(1)}, u32[]{:S(2)}, u32[]{:S(2)}) collective-permute-start(f32[16,128]{1,0:T(8,128)S(1)} %get-tuple-element.86), channel_id=1, source_target_pairs={{0,128},{1,129},{2,130},{3,131},{4,132},{5,133},{6,134},{7,135},{8... | collective-permute-start | bytes 24584 | tf_op jit(solution)/shard_map/ppermute | solution.py:305
  83.2 0.7 collective-permute-start.15
  85.4 0.7 collective-permute-start.16
  89.0 0.7 collective-permute-start.17
  91.2 0.7 collective-permute-start.18
  93.4 13.9 %collective-permute-start.19 = (f32[16,128]{1,0:T(8,128)S(1)}, f32[16,128]{1,0:T(8,128)S(1)}, u32[]{:S(2)}, u32[]{:S(2)}) collective-permute-start(f32[16,128]{1,0:T(8,128)S(1)} %get-tuple-element.96), channel_id=1, source_target_pairs={{128,0},{129,1},{130,2},{131,3},{132,4},{133,5},{134,6},{135,7},{1... | collective-permute-start | bytes 24584 | tf_op jit(solution)/shard_map/ppermute | solution.py:313
  108.8 17.7 %collective-permute-start.20 = (f32[16,128]{1,0:T(8,128)S(1)}, f32[16,128]{1,0:T(8,128)S(1)}, u32[]{:S(2)}, u32[]{:S(2)}) collective-permute-start(f32[16,128]{1,0:T(8,128)S(1)} %get-tuple-element.98), channel_id=1, source_target_pairs={{16,32},{32,16},{48,64},{64,48},{80,96},{96,80},{17,33},{33,17},{4... | collective-permute-start | bytes 24584 | tf_op jit(solution)/shard_map/ppermute | solution.py:138
  118.4 8.2 %collective-permute-start.21 = (f32[16,128]{1,0:T(8,128)S(1)}, f32[16,128]{1,0:T(8,128)S(1)}, u32[]{:S(2)}, u32[]{:S(2)}) collective-permute-start(f32[16,128]{1,0:T(8,128)S(1)} %get-tuple-element.99), channel_id=1, source_target_pairs={{0,1},{1,0},{2,3},{3,2},{4,5},{5,4},{6,7},{7,6},{8,9},{9,8},{10,11... | collective-permute-start | bytes 24584 | tf_op jit(solution)/shard_map/ppermute | solution.py:139
  123.9 2.6 %collective-permute-start.22 = (f32[16,128]{1,0:T(8,128)S(1)}, f32[16,128]{1,0:T(8,128)S(1)}, u32[]{:S(2)}, u32[]{:S(2)}) collective-permute-start(f32[16,128]{1,0:T(8,128)S(1)} %get-tuple-element.100), channel_id=1, source_target_pairs={{1,2},{2,1},{3,4},{4,3},{5,6},{6,5},{7,8},{8,7},{9,10},{10,9},{11,... | collective-permute-start | bytes 24584 | tf_op jit(solution)/shard_map/ppermute | solution.py:140
  124.6 3.1 %collective-permute-start.23 = (f32[16,128]{1,0:T(8,128)S(1)}, f32[16,128]{1,0:T(8,128)S(1)}, u32[]{:S(2)}, u32[]{:S(2)}) collective-permute-start(f32[16,128]{1,0:T(8,128)S(1)} %get-tuple-element.101), channel_id=1, source_target_pairs={{0,16},{16,0},{32,48},{48,32},{64,80},{80,64},{96,112},{112,96},{1... | collective-permute-start | bytes 24584 | tf_op jit(solution)/shard_map/ppermute | solution.py:141
  143.2 9.9 %all-to-all-start.1 = ((f32[16,4,128]{2,1,0:T(4,128)}), f32[16,4,128]{2,1,0:T(4,128)S(1)}, u32[]{:S(2)}, u32[]{:S(2)}) async-start(f32[16,4,128]{2,1,0:T(4,128)} %shard_map.157), calls=%async_computation.1 | async-start | bytes 65536 | tf_op jit(solution)/shard_map/all_to_all | solution.py:361

commit v4 on v3

--- a/solution.py
+++ b/solution.py
@@ -122,6 +122,49 @@
         mixed = sum(cols[:, 4 * s + k : 4 * s + k + 1] * beside[s] for s in range(4))
         total = total + times(mixed, (blocks[0][k], blocks[1][k]))
     return total
+
+
+def each_line_pair(v, high, low, lines):
+    hi, lo = halves(v)
+    both = nt(jnp.concatenate([hi, lo], 0), high)
+    out = both[:lines] + both[lines:] + nt(hi, low)
+    row = lax.broadcasted_iota(jnp.int32, (lines, 128), 0)
+    acc = jnp.zeros((lines, 128), F32)
+    for l in range(lines):
+        acc = acc + jnp.where(row == l, out[:, l * 128 : (l + 1) * 128], 0.0)
+    return acc
+
+
+def advance(prev, out, mat, w_ref, cols_ref, col, i, lines, base=None):
+    group = lines // 2
+    stacked = jnp.concatenate([mat[0], mat[1]], 0)
+
+    def some(t, _):
+        for j in range(group):
+            l = t * group + j
+            if prev is None:
+                xh, xl = mat
+            else:
+                hi, lo = halves(prev[l])
+                both = nn(stacked, jnp.concatenate([hi, lo], 1))
+                xh, xl = halves(both[:128, :128] + both[:128, 128:] + both[128:, :128])
+            at = i * lines + l
+            w = w_ref[pl.ds(pl.multiple_of(at * 128, 128), 128), :]
+            y = nn(w, jnp.concatenate([xh, xl], 1))
+            y = (y[:, :128] + y[:, 128:]) * cols_ref[pl.ds(at, 1), col : col + 1]
+            out[l] = -y if base is None else base[l] - y
+        return 0
+
+    lax.fori_loop(0, lines // group, some, 0)
+
+
+def put_halves(src, high, low, lines):
+    def one(l, _):
+        at = pl.ds(pl.multiple_of(l * 128, 128), 128)
+        high[at, :], low[at, :] = halves(src[l])
+        return 0
+
+    lax.fori_loop(0, lines, one, 0)
 
 
 def swaps(count, start):
@@ -260,27 +303,70 @@
         y_ref[...] = jnp.concatenate(ys, 0)
         f_ref[...] = ys[-1]
 
-    def next_forward(g_ref, inc_ref, got_ref, cols_ref, lh_ref, ll_ref, w_ref, sum_ref, f_ref):
+    def forward_map(after_ref, cols_ref, lh_ref, ll_ref, w_ref, high, low, one, two):
+        pos = lax.axis_index("line")
+
+        @pl.when((pos > 0) & (pos < segments - 1))
+        def _():
+            mat, prev = (lh_ref[...], ll_ref[...]), None
+            for i in range(n):
+                now = (one, two)[i % 2]
+                advance(prev, now, mat, w_ref, cols_ref, 16, i, lines)
+                prev = now
+            put_halves(prev, high, low, lines)
+
+    def backward_map(after_ref, cols_ref, uh_ref, ul_ref, w_ref, high, low, one, two):
+        pos = lax.axis_index("line")
+
+        @pl.when((pos > 0) & (pos < segments - 1))
+        def _():
+            mat, prev = (uh_ref[...], ul_ref[...]), None
+            for i in reversed(range(n)):
+                now = (one, two)[i % 2]
+                advance(prev, now, mat, w_ref, cols_ref, 17, i, lines)
+                prev = now
+            put_halves(prev, high, low, lines)
+
+    def turn_map(after_ref, cols_ref, lh_ref, ll_ref, uh_ref, ul_ref, w_ref, high, low, steps, one, two):
+        @pl.when(lax.axis_index("line") == segments - 1)
+        def _():
+            mat, prev = (lh_ref[...], ll_ref[...]), None
+            for i in range(n):
+                advance(prev, steps.at[i], mat, w_ref, cols_ref, 16, i, lines)
+                prev = steps.at[i]
+            mat = (uh_ref[...], ul_ref[...])
+            for i in reversed(range(n - 1)):
+                now = (one, two)[i % 2]
+                advance(prev, now, mat, w_ref, cols_ref, 17, i, lines, steps.at[i])
+                prev = now
+            put_halves(prev, high, low, lines)
+
+    def next_forward(first_ref, inc_ref, got_ref, high, low, sum_ref, f_ref):
         inc = inc_ref[...] + got_ref[...]
         sum_ref[...] = inc
-        ys = forward(g_ref[...], inc, w_ref, (lh_ref[...], ll_ref[...]), cols_ref[...], n, lines)
-        f_ref[...] = ys[-1]
-
-    def turn(g_ref, inc_ref, got_ref, cols_ref, lh_ref, ll_ref, uh_ref, ul_ref, w_ref, y_ref, x_ref):
+        f_ref[...] = first_ref[...] + each_line_pair(inc, high[...], low[...], lines)
+
+    def local_back(after_ref, y_ref, cols_ref, uh_ref, ul_ref, w_ref, x_ref):
+        zero = jnp.zeros((lines, width), F32)
+        x_ref[...] = backward(y_ref[...], zero, w_ref, (uh_ref[...], ul_ref[...]), cols_ref[...], n, lines)[0]
+
+    def turn(local_ref, inc_ref, got_ref, high, low, sum_ref, x_ref):
+        inc = inc_ref[...] + got_ref[...]
+        sum_ref[...] = inc
+        x_ref[...] = local_ref[...] + each_line_pair(inc, high[...], low[...], lines)
+
+    def settle(after_ref, g_ref, inc_ref, cols_ref, lh_ref, ll_ref, uh_ref, ul_ref, w_ref, y_ref, x_ref):
         cols = cols_ref[...]
-        inc = inc_ref[...] + got_ref[...]
-        ys = forward(g_ref[...], inc, w_ref, (lh_ref[...], ll_ref[...]), cols, n, lines)
+        ys = forward(g_ref[...], inc_ref[...], w_ref, (lh_ref[...], ll_ref[...]), cols, n, lines)
         y = jnp.concatenate(ys, 0)
         y_ref[...] = y
         zero = jnp.zeros((lines, width), F32)
-        xs = backward(y, zero, w_ref, (uh_ref[...], ul_ref[...]), cols, n, lines)
-        x_ref[...] = xs[0]
-
-    def next_backward(y_ref, arr_ref, got_ref, cols_ref, uh_ref, ul_ref, w_ref, sum_ref, x_ref):
+        x_ref[...] = backward(y, zero, w_ref, (uh_ref[...], ul_ref[...]), cols, n, lines)[0]
+
+    def next_backward(first_ref, arr_ref, got_ref, high, low, sum_ref, x_ref):
         arr = arr_ref[...] + got_ref[...]
         sum_ref[...] = arr
-        xs = backward(y_ref[...], arr, w_ref, (uh_ref[...], ul_ref[...]), cols_ref[...], n, lines)
-        x_ref[...] = xs[0]
+        x_ref[...] = first_ref[...] + each_line_pair(arr, high[...], low[...], lines)
 
     def close_backward(last, y_ref, arr_ref, got_ref, prev_ref, cols_ref, uh_ref, ul_ref, w_ref, x_ref, d_ref, *outs):
         arr = arr_ref[...] + got_ref[...]
@@ -290,6 +376,8 @@
         d_ref[...] = prev_ref[...] - x
         put_edges(d_ref if last else x_ref, outs, n, lx, ly)
 
+    pair = [((lines * width, width), BF16)] * 2
+    two = [pltpu.VMEM((lines, width, width), F32)] * 2
     field = start
     change = None
     for sweep in range(SWEEPS):
@@ -300,16 +388,28 @@
             field, *got, cols, fh, fl, rhs, lh, ll, w,
             scratch=[pltpu.VMEM((4, rows, width), F32)],
         )
+        first = ahead
         inc = jnp.zeros((lines, width), F32)
         for k in range(segments - 2):
             recv = lax.ppermute(ahead, "line", [(k, k + 1)])
-            inc, ahead = call(next_forward, [edge, edge], g, inc, recv, cols, lh, ll, w)
+            if sweep == 0 and k == 0:
+                maps = [call(forward_map, pair, ahead, cols, lh, ll, w, scratch=two)]
+            inc, ahead = call(next_forward, [edge, edge], first, inc, recv, *maps[0])
+            if k == 0:
+                local = call(local_back, [edge], ahead, y, cols, uh, ul, w)[0]
+                if sweep == 0:
+                    steps = [pltpu.VMEM((n, lines, width, width), F32)]
+                    maps.append(call(turn_map, pair, ahead, cols, lh, ll, uh, ul, w, scratch=steps + two))
         recv = lax.ppermute(ahead, "line", [(segments - 2, segments - 1)])
-        y, behind = call(turn, [block, edge], g, inc, recv, cols, lh, ll, uh, ul, w)
+        if sweep == 0:
+            maps.append(call(backward_map, pair, ahead, cols, uh, ul, w, scratch=two))
+        inc, behind = call(turn, [edge, edge], local, inc, recv, *maps[1])
         arr = jnp.zeros((lines, width), F32)
         for k in range(segments - 2):
             recv = lax.ppermute(behind, "line", [(segments - 1 - k, segments - 2 - k)])
-            arr, behind = call(next_backward, [edge, edge], y, arr, recv, cols, uh, ul, w)
+            if k == 0:
+                y, first = call(settle, [block, edge], behind, g, inc, cols, lh, ll, uh, ul, w)
+            arr, behind = call(next_backward, [edge, edge], first, arr, recv, *maps[2])
         recv = lax.ppermute(behind, "line", [(1, 0)])
         out = call(
             functools.partial(close_backward, sweep == SWEEPS - 1),

time: 155 us -> 161 us (1.039)
  waiting for transfers between devices: 34.7 us -> 50.7 us
  Pallas kernels: 30.6 us -> 24.2 us
  starting transfers between devices: 71.7 us -> 67.9 us
    ppermute x2, waiting for transfers between devices: 25.1 us -> 41 us  [body(): recv = lax.ppermute(behind, 'line', [(1, 0)])]
    pallas_call x19 -> x26, Pallas kernels: 30.6 us -> 24.2 us  [call(): pl.pallas_call(kernel, in_specs=[pl.BlockSpec(memory_space=pltpu.HBM)] *...]
    ppermute x3, starting transfers between devices: 33.5 us -> 29.5 us  [exchange(): b = lax.ppermute(b, 'tx', swaps(nx, 1))]
  transfers between devices with their start and end apart: 25 -> 25, of which waited for: 7 -> 7; matrix products, arithmetic and copies ran while one was open for 0% -> 0% of each run, Pallas kernels for 2% -> 7%
where the time goes in v4:
time: 161 us; the launch traced here: 160 us
  starting transfers between devices  67.9 us (42%)
  waiting for transfers between devices  50.7 us (31%)
  Pallas kernels  24.2 us (15%)
  blocking collectives  14 us (9%)
  local copies, waits for them, and re-layouts  2.01 us (1%)
    ppermute x2, waiting for transfers between devices, body(): recv = lax.ppermute(behind, 'line', [(1, 0)])  41 us
    ppermute x3, starting transfers between devices, exchange(): b = lax.ppermute(b, 'tx', swaps(nx, 1))  29.5 us
    pallas_call x26, Pallas kernels, call(): pl.pallas_call(kernel, in_specs=[pl.BlockSpec(memory_space=pltpu.HBM)] *...  24.2 us
    all_to_all x1, blocking collectives, body(): lax.all_to_all(partial.reshape(owners, owned_rows, width), 'ty', 0, 0, ti...  14 us
    ppermute x3, starting transfers between devices, exchange(): c = lax.ppermute(c, 'ty', swaps(ny, 0))  14 us
    ppermute x4, starting transfers between devices, body(): recv = lax.ppermute(ahead, 'line', [(k, k + 1)])  6.31 us
    all_to_all x1, waiting for transfers between devices, body(): update = lax.all_to_all(copies, 'ty', 0, 0, tiled=True)  5.77 us
    ppermute x3, starting transfers between devices, exchange(): a = lax.ppermute(a, 'tx', swaps(nx, 0))  5.76 us
  transfers between devices with their start and end apart: 25, of which 7 were waited for; matrix products, arithmetic and copies ran while one was open for 0% of the time, Pallas kernels for 7%

profile of v4, /device:TPU:1, one launch (start us, length us, event | category | flops | bytes accessed | tf_op | source)
XLA Modules:
  0.0 159.9 jit_solution(3574240499911372966)
XLA Ops:
  0.6 0.7 copy-done
  1.4 10.2 %collective-permute-start = (f32[16,128]{1,0:T(8,128)S(1)}, f32[16,128]{1,0:T(8,128)S(1)}, u32[]{:S(2)}, u32[]{:S(2)}) collective-permute-start(f32[16,128]{1,0:T(8,128)S(1)} %get-tuple-element.68), channel_id=1, source_target_pairs={{16,32},{32,16},{48,64},{64,48},{80,96},{96,80},{17,33},{33,17},{4... | collective-permute-start | bytes 24584 | tf_op jit(solution)/shard_map/ppermute | solution.py:181
  11.6 3.1 %collective-permute-start.1 = (f32[16,128]{1,0:T(8,128)S(1)}, f32[16,128]{1,0:T(8,128)S(1)}, u32[]{:S(2)}, u32[]{:S(2)}) collective-permute-start(f32[16,128]{1,0:T(8,128)S(1)} %get-tuple-element.69), channel_id=1, source_target_pairs={{0,1},{1,0},{2,3},{3,2},{4,5},{5,4},{6,7},{7,6},{8,9},{9,8},{10,11... | collective-permute-start | bytes 24584 | tf_op jit(solution)/shard_map/ppermute | solution.py:182
  14.7 0.7 collective-permute-start.2
  15.4 1.9 %collective-permute-start.3 = (f32[16,128]{1,0:T(8,128)S(1)}, f32[16,128]{1,0:T(8,128)S(1)}, u32[]{:S(2)}, u32[]{:S(2)}) collective-permute-start(f32[16,128]{1,0:T(8,128)S(1)} %get-tuple-element.71), channel_id=1, source_target_pairs={{0,16},{16,0},{32,48},{48,32},{64,80},{80,64},{96,112},{112,96},{1... | collective-permute-start | bytes 24584 | tf_op jit(solution)/shard_map/ppermute | solution.py:184
  17.3 2.3 %shard_map.141 = (bf16[128,128]{1,0:T(8,128)(2,1)S(1)}, bf16[128,128]{1,0:T(8,128)(2,1)S(1)}, bf16[128,128]{1,0:T(8,128)(2,1)S(1)}, bf16[128,128]{1,0:T(8,128)(2...) custom-call(bf16[8192,128]{1,0:T(8,128)(2,1)} %bitcast.17, ...), custom_call_target="tpu_custom_call" | custom-call | tf_op jit(solution)/shard_map/pallas_call | solution.py:17
  19.7 1.9 %shard_map.142 = (f32[64,128]{1,0:T(8,128)S(1)}, f32[64,128]{1,0:T(8,128)S(1)}, f32[16,128]{1,0:T(8,128)S(1)}) custom-call(f32[64,128]{1,0:T(8,128)S(1)} %bitcast.11, f32[16,128]{1,0:T(8,128)S(1)} %collective-permute-done.a, f32[16,128]{1,0:T(8,128)S(1)} %collective-permute-done.1.b, f32[16,128]{1,0:T(8,128)S(1)} %collective-permute-done.2.c, ...), custom_call_target="tpu_custom_call" | custom-call | tf_op jit(solution)/shard_map/pallas_call | solution.py:17
  21.6 3.6 %collective-permute-start.4 = (f32[16,128]{1,0:T(8,128)S(1)}, f32[16,128]{1,0:T(8,128)S(1)}, u32[]{:S(2)}, u32[]{:S(2)}) collective-permute-start(f32[16,128]{1,0:T(8,128)S(1)} %get-tuple-element.78.after_ref.first_ref), channel_id=1, source_target_pairs={{0,128},{1,129},{2,130},{3,131},{4,132},{5,133},{6,134},{7,135},{8... | collective-permute-start | bytes 24584 | tf_op jit(solution)/shard_map/ppermute | solution.py:394
  25.2 0.7 collective-permute-done.4.got_ref
  26.3 0.7 collective-permute-start.5
  27.4 0.7 collective-permute-start.6
  28.1 1.5 shard_map.145.local_ref
  30.0 0.8 collective-permute-start.7
  30.9 2.9 %shard_map.149 = (f32[64,128]{1,0:T(8,128)S(1)}, f32[16,128]{1,0:T(8,128)S(1)}) custom-call(f32[16,128]{1,0:T(8,128)S(1)} %get-tuple-element.90.after_ref, f32[64,128]{1,0:T(8,128)S(1)} %get-tuple-element.91.g_ref, f32[16,128]{1,0:T(8,128)S(1)} %get-tuple-element.92.inc_ref, f32[64,128]{1,0:T(8,128)S(1)} %get-tuple-element.72.cols_ref, ...), custom_call_target="tpu_custom_call" | custom-call | tf_op jit(solution)/shard_map/pallas_call | solution.py:17
  34.3 0.7 collective-permute-start.8
  35.4 1.3 collective-permute-start.9
  36.7 32.2 %collective-permute-done.9.got_ref = f32[16,128]{1,0:T(8,128)S(1)} collective-permute-done((f32[16,128]{1,0:T(8,128)S(1)}, f32[16,128]{1,0:T(8,128)S(1)}, u32[]{:S(2)}, u32[]{:S(2)}) %collective-permute-start.9) | collective-permute-done | bytes 8224 | tf_op jit(solution)/shard_map/ppermute | solution.py:413
  68.8 2.1 %shard_map.153 = (f32[64,128]{1,0:T(8,128)S(1)}, f32[64,128]{1,0:T(8,128)}, f32[16,128]{1,0:T(8,128)S(1)}, f32[16,128]{1,0:T(8,128)S(1)}, f32[16,128]{1,0:T(8,128)S(1)}, /*index=5*/f32[16,128]{1,0:T(8,128)S(1)}) custom-call(f32[64,128]{1,0:T(8,128)S(1)} %get-tuple-element.93.y_ref, f32[16,128]{1,0:T(8,128)S(1)} %get-tuple-element.99.arr_ref, ...), custom_call_target="tpu_custom_call" | custom-call | tf_op jit(solution)/shard_map/pallas_call | solution.py:17
  71.0 10.3 %collective-permute-start.10 = (f32[16,128]{1,0:T(8,128)S(1)}, f32[16,128]{1,0:T(8,128)S(1)}, u32[]{:S(2)}, u32[]{:S(2)}) collective-permute-start(f32[16,128]{1,0:T(8,128)S(1)} %get-tuple-element.102), channel_id=1, source_target_pairs={{16,32},{32,16},{48,64},{64,48},{80,96},{96,80},{17,33},{33,17},{4... | collective-permute-start | bytes 24584 | tf_op jit(solution)/shard_map/ppermute | solution.py:181
  81.3 5.3 %collective-permute-start.11 = (f32[16,128]{1,0:T(8,128)S(1)}, f32[16,128]{1,0:T(8,128)S(1)}, u32[]{:S(2)}, u32[]{:S(2)}) collective-permute-start(f32[16,128]{1,0:T(8,128)S(1)} %get-tuple-element.103), channel_id=1, source_target_pairs={{0,1},{1,0},{2,3},{3,2},{4,5},{5,4},{6,7},{7,6},{8,9},{9,8},{10,11... | collective-permute-start | bytes 24584 | tf_op jit(solution)/shard_map/ppermute | solution.py:182
  86.6 0.7 collective-permute-start.12
  87.2 1.9 %collective-permute-start.13 = (f32[16,128]{1,0:T(8,128)S(1)}, f32[16,128]{1,0:T(8,128)S(1)}, u32[]{:S(2)}, u32[]{:S(2)}) collective-permute-start(f32[16,128]{1,0:T(8,128)S(1)} %get-tuple-element.105), channel_id=1, source_target_pairs={{0,16},{16,0},{32,48},{48,32},{64,80},{80,64},{96,112},{112,96},{1... | collective-permute-start | bytes 24584 | tf_op jit(solution)/shard_map/ppermute | solution.py:184
  89.2 1.1 collective-permute-done.13.d
  90.3 1.9 %shard_map.154 = (f32[64,128]{1,0:T(8,128)S(1)}, f32[64,128]{1,0:T(8,128)S(1)}, f32[16,128]{1,0:T(8,128)S(1)}) custom-call(f32[64,128]{1,0:T(8,128)S(1)} %get-tuple-element.101.x_ref.prev_ref, f32[16,128]{1,0:T(8,128)S(1)} %collective-permute-done.10.a, f32[16,128]{1,0:T(8,128)S(1)} %collective-permute-done.11.b, f32[16,128]{1,0:T(8,128)S(1)} %collective-permute-done.12.c, ...), custom_call_target="tpu_custom_call" | custom-call | tf_op jit(solution)/shard_map/pallas_call | solution.py:17
  92.2 1.4 collective-permute-start.14
  93.6 0.8 collective-permute-done.14.got_ref
  94.7 0.7 collective-permute-start.15
  95.8 0.7 collective-permute-start.16
  96.5 1.5 shard_map.156.local_ref
  98.4 0.7 collective-permute-start.17
  99.1 2.9 %shard_map.159 = (f32[64,128]{1,0:T(8,128)S(1)}, f32[16,128]{1,0:T(8,128)S(1)}) custom-call(f32[16,128]{1,0:T(8,128)S(1)} %get-tuple-element.112.after_ref, f32[64,128]{1,0:T(8,128)S(1)} %get-tuple-element.113.g_ref, f32[16,128]{1,0:T(8,128)S(1)} %get-tuple-element.114.inc_ref, f32[64,128]{1,0:T(8,128)S(1)} %get-tuple-element.72.cols_ref, ...), custom_call_target="tpu_custom_call" | custom-call | tf_op jit(solution)/shard_map/pallas_call | solution.py:17
  102.5 0.7 collective-permute-start.18
  103.2 0.4 shard_map.161
  103.5 1.3 collective-permute-start.19
  104.9 8.9 %collective-permute-done.19.got_ref = f32[16,128]{1,0:T(8,128)S(1)} collective-permute-done((f32[16,128]{1,0:T(8,128)S(1)}, f32[16,128]{1,0:T(8,128)S(1)}, u32[]{:S(2)}, u32[]{:S(2)}) %collective-permute-start.19) | collective-permute-done | bytes 8224 | tf_op jit(solution)/shard_map/ppermute | solution.py:413
  113.7 1.5 shard_map.162
  115.3 9.0 %collective-permute-start.20 = (f32[16,128]{1,0:T(8,128)S(1)}, f32[16,128]{1,0:T(8,128)S(1)}, u32[]{:S(2)}, u32[]{:S(2)}) collective-permute-start(f32[16,128]{1,0:T(8,128)S(1)} %get-tuple-element.122), channel_id=1, source_target_pairs={{16,32},{32,16},{48,64},{64,48},{80,96},{96,80},{17,33},{33,17},{4... | collective-permute-start | bytes 24584 | tf_op jit(solution)/shard_map/ppermute | solution.py:181
  124.2 5.6 %collective-permute-start.21 = (f32[16,128]{1,0:T(8,128)S(1)}, f32[16,128]{1,0:T(8,128)S(1)}, u32[]{:S(2)}, u32[]{:S(2)}) collective-permute-start(f32[16,128]{1,0:T(8,128)S(1)} %get-tuple-element.123), channel_id=1, source_target_pairs={{0,1},{1,0},{2,3},{3,2},{4,5},{5,4},{6,7},{7,6},{8,9},{9,8},{10,11... | collective-permute-start | bytes 24584 | tf_op jit(solution)/shard_map/ppermute | solution.py:182
  129.8 0.7 collective-permute-start.22
  130.5 1.9 %collective-permute-start.23 = (f32[16,128]{1,0:T(8,128)S(1)}, f32[16,128]{1,0:T(8,128)S(1)}, u32[]{:S(2)}, u32[]{:S(2)}) collective-permute-start(f32[16,128]{1,0:T(8,128)S(1)} %get-tuple-element.125), channel_id=1, source_target_pairs={{0,16},{16,0},{32,48},{48,32},{64,80},{80,64},{96,112},{112,96},{1... | collective-permute-start | bytes 24584 | tf_op jit(solution)/shard_map/ppermute | solution.py:184
  132.5 1.1 collective-permute-done.23.d
  133.6 0.7 shard_map.163
  134.3 14.0 %all_to_all.10.parts_ref = f32[16,4,128]{2,1,0:T(4,128)S(1)} all-to-all(f32[16,4,128]{2,1,0:T(4,128)S(1)} %bitcast.16), channel_id=1, replica_groups=mesh['line'=4,'tx'=8,'ty'=16] {'ty'}, dimensions={0} | all-to-all | bytes 65536 | tf_op jit(solution)/shard_map/all_to_all | solution.py:441
  148.3 0.8 shard_map.164
  149.1 3.5 %all-to-all-start.1 = ((f32[16,4,128]{2,1,0:T(4,128)}), f32[16,4,128]{2,1,0:T(4,128)S(1)}, u32[]{:S(2)}, u32[]{:S(2)}) async-start(f32[16,4,128]{2,1,0:T(4,128)} %shard_map.164), calls=%async_computation.1 | async-start | bytes 65536 | tf_op jit(solution)/shard_map/all_to_all | solution.py:461
  152.6 0.6 copy.16
  153.2 5.8 %all-to-all-done.1 = f32[16,4,128]{2,1,0:T(4,128)S(1)} async-done(((f32[16,4,128]{2,1,0:T(4,128)}), f32[16,4,128]{2,1,0:T(4,128)S(1)}, u32[]{:S(2)}, u32[]{:S(2)}) %all-to-all-start.1) | async-done | bytes 32800 | tf_op jit(solution)/shard_map/all_to_all | solution.py:461
  159.3 0.6 copy.15
  (38 shorter events, 4.0 us)
Async XLA Ops:
  0.6 0.8 copy-start
  1.4 18.3 %copy-start.2 = (f32[4,4,4,128]{3,2,1,0:T(4,128)S(1)}, f32[4,4,4,128]{3,2,1,0:T(4,128)}, u32[]{:S(2)}) copy-start(f32[4,4,4,128]{3,2,1,0:T(4,128)} %param.13) | copy-start | bytes 98308
  1.4 18.2 %collective-permute-start = (f32[16,128]{1,0:T(8,128)S(1)}, f32[16,128]{1,0:T(8,128)S(1)}, u32[]{:S(2)}, u32[]{:S(2)}) collective-permute-start(f32[16,128]{1,0:T(8,128)S(1)} %get-tuple-element.68), channel_id=1, source_target_pairs={{16,32},{32,16},{48,64},{64,48},{80,96},{96,80},{17,33},{33,17},{4... | collective-permute-start | bytes 24584 | tf_op jit(solution)/shard_map/ppermute | solution.py:181
  11.6 8.1 %collective-permute-start.1 = (f32[16,128]{1,0:T(8,128)S(1)}, f32[16,128]{1,0:T(8,128)S(1)}, u32[]{:S(2)}, u32[]{:S(2)}) collective-permute-start(f32[16,128]{1,0:T(8,128)S(1)} %get-tuple-element.69), channel_id=1, source_target_pairs={{0,1},{1,0},{2,3},{3,2},{4,5},{5,4},{6,7},{7,6},{8,9},{9,8},{10,11... | collective-permute-start | bytes 24584 | tf_op jit(solution)/shard_map/ppermute | solution.py:182
  14.7 4.9 %collective-permute-start.2 = (f32[16,128]{1,0:T(8,128)S(1)}, f32[16,128]{1,0:T(8,128)S(1)}, u32[]{:S(2)}, u32[]{:S(2)}) collective-permute-start(f32[16,128]{1,0:T(8,128)S(1)} %get-tuple-element.70), channel_id=1, source_target_pairs={{1,2},{2,1},{3,4},{4,3},{5,6},{6,5},{7,8},{8,7},{9,10},{10,9},{11,... | collective-permute-start | bytes 24584 | tf_op jit(solution)/shard_map/ppermute | solution.py:183
  15.4 4.3 %collective-permute-start.3 = (f32[16,128]{1,0:T(8,128)S(1)}, f32[16,128]{1,0:T(8,128)S(1)}, u32[]{:S(2)}, u32[]{:S(2)}) collective-permute-start(f32[16,128]{1,0:T(8,128)S(1)} %get-tuple-element.71), channel_id=1, source_target_pairs={{0,16},{16,0},{32,48},{48,32},{64,80},{80,64},{96,112},{112,96},{1... | collective-permute-start | bytes 24584 | tf_op jit(solution)/shard_map/ppermute | solution.py:184
  21.6 4.4 %collective-permute-start.4 = (f32[16,128]{1,0:T(8,128)S(1)}, f32[16,128]{1,0:T(8,128)S(1)}, u32[]{:S(2)}, u32[]{:S(2)}) collective-permute-start(f32[16,128]{1,0:T(8,128)S(1)} %get-tuple-element.78.after_ref.first_ref), channel_id=1, source_target_pairs={{0,128},{1,129},{2,130},{3,131},{4,132},{5,133},{6,134},{7,135},{8... | collective-permute-start | bytes 24584 | tf_op jit(solution)/shard_map/ppermute | solution.py:394
  26.3 0.7 collective-permute-start.5
  27.4 2.2 %collective-permute-start.6 = (f32[16,128]{1,0:T(8,128)S(1)}, f32[16,128]{1,0:T(8,128)S(1)}, u32[]{:S(2)}, u32[]{:S(2)}) collective-permute-start(f32[16,128]{1,0:T(8,128)S(1)} %get-tuple-element.87.after_ref), channel_id=1, source_target_pairs={{256,384},{257,385},{258,386},{259,387},{260,388},{261,389},{262,3... | collective-permute-start | bytes 24584 | tf_op jit(solution)/shard_map/ppermute | solution.py:403
  30.0 3.8 %collective-permute-start.7 = (f32[16,128]{1,0:T(8,128)S(1)}, f32[16,128]{1,0:T(8,128)S(1)}, u32[]{:S(2)}, u32[]{:S(2)}) collective-permute-start(f32[16,128]{1,0:T(8,128)S(1)} %get-tuple-element.90.after_ref), channel_id=1, source_target_pairs={{384,256},{385,257},{386,258},{387,259},{388,260},{389,261},{390,2... | collective-permute-start | bytes 24584 | tf_op jit(solution)/shard_map/ppermute | solution.py:409
  30.9 37.9 %copy-start.1 = (f32[4,4,4,128]{3,2,1,0:T(4,128)S(1)}, f32[4,4,4,128]{3,2,1,0:T(4,128)}, u32[]{:S(2)}) copy-start(f32[4,4,4,128]{3,2,1,0:T(4,128)} %param.14) | copy-start | bytes 98308
  34.3 0.7 collective-permute-start.8
  35.4 33.5 %collective-permute-start.9 = (f32[16,128]{1,0:T(8,128)S(1)}, f32[16,128]{1,0:T(8,128)S(1)}, u32[]{:S(2)}, u32[]{:S(2)}) collective-permute-start(f32[16,128]{1,0:T(8,128)S(1)} %get-tuple-element.100), channel_id=1, source_target_pairs={{128,0},{129,1},{130,2},{131,3},{132,4},{133,5},{134,6},{135,7},{1... | collective-permute-start | bytes 24584 | tf_op jit(solution)/shard_map/ppermute | solution.py:413
  71.0 18.2 %collective-permute-start.10 = (f32[16,128]{1,0:T(8,128)S(1)}, f32[16,128]{1,0:T(8,128)S(1)}, u32[]{:S(2)}, u32[]{:S(2)}) collective-permute-start(f32[16,128]{1,0:T(8,128)S(1)} %get-tuple-element.102), channel_id=1, source_target_pairs={{16,32},{32,16},{48,64},{64,48},{80,96},{96,80},{17,33},{33,17},{4... | collective-permute-start | bytes 24584 | tf_op jit(solution)/shard_map/ppermute | solution.py:181
  81.3 7.9 %collective-permute-start.11 = (f32[16,128]{1,0:T(8,128)S(1)}, f32[16,128]{1,0:T(8,128)S(1)}, u32[]{:S(2)}, u32[]{:S(2)}) collective-permute-start(f32[16,128]{1,0:T(8,128)S(1)} %get-tuple-element.103), channel_id=1, source_target_pairs={{0,1},{1,0},{2,3},{3,2},{4,5},{5,4},{6,7},{7,6},{8,9},{9,8},{10,11... | collective-permute-start | bytes 24584 | tf_op jit(solution)/shard_map/ppermute | solution.py:182
  86.6 2.6 %collective-permute-start.12 = (f32[16,128]{1,0:T(8,128)S(1)}, f32[16,128]{1,0:T(8,128)S(1)}, u32[]{:S(2)}, u32[]{:S(2)}) collective-permute-start(f32[16,128]{1,0:T(8,128)S(1)} %get-tuple-element.104), channel_id=1, source_target_pairs={{1,2},{2,1},{3,4},{4,3},{5,6},{6,5},{7,8},{8,7},{9,10},{10,9},{11,... | collective-permute-start | bytes 24584 | tf_op jit(solution)/shard_map/ppermute | solution.py:183
  87.2 3.1 %collective-permute-start.13 = (f32[16,128]{1,0:T(8,128)S(1)}, f32[16,128]{1,0:T(8,128)S(1)}, u32[]{:S(2)}, u32[]{:S(2)}) collective-permute-start(f32[16,128]{1,0:T(8,128)S(1)} %get-tuple-element.105), channel_id=1, source_target_pairs={{0,16},{16,0},{32,48},{48,32},{64,80},{80,64},{96,112},{112,96},{1... | collective-permute-start | bytes 24584 | tf_op jit(solution)/shard_map/ppermute | solution.py:184
  92.2 2.2 %collective-permute-start.14 = (f32[16,128]{1,0:T(8,128)S(1)}, f32[16,128]{1,0:T(8,128)S(1)}, u32[]{:S(2)}, u32[]{:S(2)}) collective-permute-start(f32[16,128]{1,0:T(8,128)S(1)} %get-tuple-element.106.first_ref), channel_id=1, source_target_pairs={{0,128},{1,129},{2,130},{3,131},{4,132},{5,133},{6,134},{7,135},{8... | collective-permute-start | bytes 24584 | tf_op jit(solution)/shard_map/ppermute | solution.py:394
  94.7 0.7 collective-permute-start.15
  95.8 2.2 %collective-permute-start.16 = (f32[16,128]{1,0:T(8,128)S(1)}, f32[16,128]{1,0:T(8,128)S(1)}, u32[]{:S(2)}, u32[]{:S(2)}) collective-permute-start(f32[16,128]{1,0:T(8,128)S(1)} %get-tuple-element.111), channel_id=1, source_target_pairs={{256,384},{257,385},{258,386},{259,387},{260,388},{261,389},{262,3... | collective-permute-start | bytes 24584 | tf_op jit(solution)/shard_map/ppermute | solution.py:403
  98.4 3.6 %collective-permute-start.17 = (f32[16,128]{1,0:T(8,128)S(1)}, f32[16,128]{1,0:T(8,128)S(1)}, u32[]{:S(2)}, u32[]{:S(2)}) collective-permute-start(f32[16,128]{1,0:T(8,128)S(1)} %get-tuple-element.112.after_ref), channel_id=1, source_target_pairs={{384,256},{385,257},{386,258},{387,259},{388,260},{389,261},{390,2... | collective-permute-start | bytes 24584 | tf_op jit(solution)/shard_map/ppermute | solution.py:409
  102.5 0.7 collective-permute-start.18
  103.5 10.2 %collective-permute-start.19 = (f32[16,128]{1,0:T(8,128)S(1)}, f32[16,128]{1,0:T(8,128)S(1)}, u32[]{:S(2)}, u32[]{:S(2)}) collective-permute-start(f32[16,128]{1,0:T(8,128)S(1)} %get-tuple-element.120), channel_id=1, source_target_pairs={{128,0},{129,1},{130,2},{131,3},{132,4},{133,5},{134,6},{135,7},{1... | collective-permute-start | bytes 24584 | tf_op jit(solution)/shard_map/ppermute | solution.py:413
  115.3 17.2 %collective-permute-start.20 = (f32[16,128]{1,0:T(8,128)S(1)}, f32[16,128]{1,0:T(8,128)S(1)}, u32[]{:S(2)}, u32[]{:S(2)}) collective-permute-start(f32[16,128]{1,0:T(8,128)S(1)} %get-tuple-element.122), channel_id=1, source_target_pairs={{16,32},{32,16},{48,64},{64,48},{80,96},{96,80},{17,33},{33,17},{4... | collective-permute-start | bytes 24584 | tf_op jit(solution)/shard_map/ppermute | solution.py:181
  124.2 8.2 %collective-permute-start.21 = (f32[16,128]{1,0:T(8,128)S(1)}, f32[16,128]{1,0:T(8,128)S(1)}, u32[]{:S(2)}, u32[]{:S(2)}) collective-permute-start(f32[16,128]{1,0:T(8,128)S(1)} %get-tuple-element.123), channel_id=1, source_target_pairs={{0,1},{1,0},{2,3},{3,2},{4,5},{5,4},{6,7},{7,6},{8,9},{9,8},{10,11... | collective-permute-start | bytes 24584 | tf_op jit(solution)/shard_map/ppermute | solution.py:182
  129.8 2.6 %collective-permute-start.22 = (f32[16,128]{1,0:T(8,128)S(1)}, f32[16,128]{1,0:T(8,128)S(1)}, u32[]{:S(2)}, u32[]{:S(2)}) collective-permute-start(f32[16,128]{1,0:T(8,128)S(1)} %get-tuple-element.124), channel_id=1, source_target_pairs={{1,2},{2,1},{3,4},{4,3},{5,6},{6,5},{7,8},{8,7},{9,10},{10,9},{11,... | collective-permute-start | bytes 24584 | tf_op jit(solution)/shard_map/ppermute | solution.py:183
  130.5 3.1 %collective-permute-start.23 = (f32[16,128]{1,0:T(8,128)S(1)}, f32[16,128]{1,0:T(8,128)S(1)}, u32[]{:S(2)}, u32[]{:S(2)}) collective-permute-start(f32[16,128]{1,0:T(8,128)S(1)} %get-tuple-element.125), channel_id=1, source_target_pairs={{0,16},{16,0},{32,48},{48,32},{64,80},{80,64},{96,112},{112,96},{1... | collective-permute-start | bytes 24584 | tf_op jit(solution)/shard_map/ppermute | solution.py:184
  149.1 9.9 %all-to-all-start.1 = ((f32[16,4,128]{2,1,0:T(4,128)}), f32[16,4,128]{2,1,0:T(4,128)S(1)}, u32[]{:S(2)}, u32[]{:S(2)}) async-start(f32[16,4,128]{2,1,0:T(4,128)} %shard_map.164), calls=%async_computation.1 | async-start | bytes 65536 | tf_op jit(solution)/shard_map/all_to_all | solution.py:461

commit v5 on v4

--- a/solution.py
+++ b/solution.py
@@ -101,7 +101,7 @@
     lines = lx * ly
     x = x_ref[...]
     even = is_even("tx")
-    b, c, d, a = (r[...] for r in got)
+    d, c, b, a = (r[...] for r in got)
     below, above = jnp.where(even, b, a), jnp.where(even, a, b)
     near[0] = pltpu.roll(x, ly, 0)
     near[1] = pltpu.roll(x, n * lines - ly, 0)
@@ -137,7 +137,7 @@
 
 def advance(prev, out, mat, w_ref, cols_ref, col, i, lines, base=None):
     group = lines // 2
-    stacked = jnp.concatenate([mat[0], mat[1]], 0)
+    left = jnp.concatenate([mat[0], mat[0], mat[1]], 1)
 
     def some(t, _):
         for j in range(group):
@@ -146,12 +146,11 @@
                 xh, xl = mat
             else:
                 hi, lo = halves(prev[l])
-                both = nn(stacked, jnp.concatenate([hi, lo], 1))
-                xh, xl = halves(both[:128, :128] + both[:128, 128:] + both[128:, :128])
+                xh, xl = halves(nn(left, jnp.concatenate([hi, lo, hi], 0)))
             at = i * lines + l
             w = w_ref[pl.ds(pl.multiple_of(at * 128, 128), 128), :]
-            y = nn(w, jnp.concatenate([xh, xl], 1))
-            y = (y[:, :128] + y[:, 128:]) * cols_ref[pl.ds(at, 1), col : col + 1]
+            y = nn(jnp.concatenate([w, w], 1), jnp.concatenate([xh, xl], 0))
+            y = y * cols_ref[pl.ds(at, 1), col : col + 1]
             out[l] = -y if base is None else base[l] - y
         return 0
 
@@ -178,11 +177,11 @@
 def exchange(sends):
     nx, ny = lax.axis_size("tx"), lax.axis_size("ty")
     a, b, c, d = sends
+    d = lax.ppermute(d, "ty", swaps(ny, 1))
+    c = lax.ppermute(c, "ty", swaps(ny, 0))
     b = lax.ppermute(b, "tx", swaps(nx, 1))
-    c = lax.ppermute(c, "ty", swaps(ny, 0))
-    d = lax.ppermute(d, "ty", swaps(ny, 1))
     a = lax.ppermute(a, "tx", swaps(nx, 0))
-    return b, c, d, a
+    return d, c, b, a
 
 
 def body(
@@ -341,6 +340,36 @@
                 prev = now
             put_halves(prev, high, low, lines)
 
+    def chain_forward(stage, g_ref, inc_ref, got_ref, cols_ref, lh_ref, ll_ref, w_ref, sum_ref, f_ref):
+        inc = inc_ref[...] + got_ref[...]
+        sum_ref[...] = inc
+
+        @pl.when(lax.axis_index("line") == stage)
+        def _():
+            ys = forward(g_ref[...], inc, w_ref, (lh_ref[...], ll_ref[...]), cols_ref[...], n, lines)
+            f_ref[...] = ys[-1]
+
+    def chain_turn(g_ref, inc_ref, got_ref, cols_ref, lh_ref, ll_ref, uh_ref, ul_ref, w_ref, after, after_too, y_ref, x_ref):
+        cols = cols_ref[...]
+        inc = inc_ref[...] + got_ref[...]
+        ys = forward(g_ref[...], inc, w_ref, (lh_ref[...], ll_ref[...]), cols, n, lines)
+        for i in range(n):
+            y_ref[i * lines : (i + 1) * lines, :] = ys[i]
+
+        @pl.when(lax.axis_index("line") == segments - 1)
+        def _():
+            zero = jnp.zeros((lines, width), F32)
+            x_ref[...] = backward(y_ref[...], zero, w_ref, (uh_ref[...], ul_ref[...]), cols, n, lines)[0]
+
+    def chain_backward(stage, y_ref, arr_ref, got_ref, cols_ref, uh_ref, ul_ref, w_ref, after, after_too, sum_ref, x_ref):
+        arr = arr_ref[...] + got_ref[...]
+        sum_ref[...] = arr
+
+        @pl.when(lax.axis_index("line") == stage)
+        def _():
+            xs = backward(y_ref[...], arr, w_ref, (uh_ref[...], ul_ref[...]), cols_ref[...], n, lines)
+            x_ref[...] = xs[0]
+
     def next_forward(first_ref, inc_ref, got_ref, high, low, sum_ref, f_ref):
         inc = inc_ref[...] + got_ref[...]
         sum_ref[...] = inc
@@ -388,28 +417,39 @@
             field, *got, cols, fh, fl, rhs, lh, ll, w,
             scratch=[pltpu.VMEM((4, rows, width), F32)],
         )
-        first = ahead
-        inc = jnp.zeros((lines, width), F32)
-        for k in range(segments - 2):
-            recv = lax.ppermute(ahead, "line", [(k, k + 1)])
-            if sweep == 0 and k == 0:
-                maps = [call(forward_map, pair, ahead, cols, lh, ll, w, scratch=two)]
-            inc, ahead = call(next_forward, [edge, edge], first, inc, recv, *maps[0])
-            if k == 0:
-                local = call(local_back, [edge], ahead, y, cols, uh, ul, w)[0]
-                if sweep == 0:
+        inc = arr = jnp.zeros((lines, width), F32)
+        if sweep == 0:
+            for k in range(segments - 2):
+                recv = lax.ppermute(ahead, "line", [(k, k + 1)])
+                step = functools.partial(chain_forward, k + 1)
+                inc, ahead = call(step, [edge, edge], g, inc, recv, cols, lh, ll, w)
+            recv = lax.ppermute(ahead, "line", [(segments - 2, segments - 1)])
+            back = call(backward_map, pair, ahead, cols, uh, ul, w, scratch=two)
+            y, behind = call(chain_turn, [block, edge], g, inc, recv, cols, lh, ll, uh, ul, w, *back)
+            for k in range(segments - 2):
+                recv = lax.ppermute(behind, "line", [(segments - 1 - k, segments - 2 - k)])
+                if k == 0:
                     steps = [pltpu.VMEM((n, lines, width, width), F32)]
-                    maps.append(call(turn_map, pair, ahead, cols, lh, ll, uh, ul, w, scratch=steps + two))
-        recv = lax.ppermute(ahead, "line", [(segments - 2, segments - 1)])
-        if sweep == 0:
-            maps.append(call(backward_map, pair, ahead, cols, uh, ul, w, scratch=two))
-        inc, behind = call(turn, [edge, edge], local, inc, recv, *maps[1])
-        arr = jnp.zeros((lines, width), F32)
-        for k in range(segments - 2):
-            recv = lax.ppermute(behind, "line", [(segments - 1 - k, segments - 2 - k)])
-            if k == 0:
-                y, first = call(settle, [block, edge], behind, g, inc, cols, lh, ll, uh, ul, w)
-            arr, behind = call(next_backward, [edge, edge], first, arr, recv, *maps[2])
+                    bend = call(turn_map, pair, behind, cols, lh, ll, uh, ul, w, scratch=steps + two)
+                if k == segments - 3:
+                    fore = call(forward_map, pair, behind, cols, lh, ll, w, scratch=two)
+                step = functools.partial(chain_backward, segments - 2 - k)
+                made = fore if k == segments - 3 else bend
+                arr, behind = call(step, [edge, edge], y, arr, recv, cols, uh, ul, w, *made)
+        else:
+            first = ahead
+            for k in range(segments - 2):
+                recv = lax.ppermute(ahead, "line", [(k, k + 1)])
+                inc, ahead = call(next_forward, [edge, edge], first, inc, recv, *fore)
+                if k == 0:
+                    local = call(local_back, [edge], ahead, y, cols, uh, ul, w)[0]
+            recv = lax.ppermute(ahead, "line", [(segments - 2, segments - 1)])
+            inc, behind = call(turn, [edge, edge], local, inc, recv, *bend)
+            for k in range(segments - 2):
+                recv = lax.ppermute(behind, "line", [(segments - 1 - k, segments - 2 - k)])
+                if k == 0:
+                    y, first = call(settle, [block, edge], behind, g, inc, cols, lh, ll, uh, ul, w)
+                arr, behind = call(next_backward, [edge, edge], first, arr, recv, *back)
         recv = lax.ppermute(behind, "line", [(1, 0)])
         out = call(
             functools.partial(close_backward, sweep == SWEEPS - 1),

time: 161 us -> 162 us (level)
  starting transfers between devices: 67.9 us -> 74.2 us
  Pallas kernels: 24.2 us -> 20.3 us
  blocking collectives: 14 us -> 11.7 us
    pallas_call x26 -> x24, Pallas kernels: 24.2 us -> 20.3 us  [call(): pl.pallas_call(kernel, in_specs=[pl.BlockSpec(memory_space=pltpu.HBM)] *...]
    ppermute x3, starting transfers between devices: 29.5 us -> 32.8 us  [exchange(): b = lax.ppermute(b, 'tx', swaps(nx, 1))]
    ppermute x3, starting transfers between devices: 14 us -> 17.2 us  [exchange(): c = lax.ppermute(c, 'ty', swaps(ny, 0))]
    all_to_all x1, blocking collectives: 14 us -> 11.7 us  [body(): lax.all_to_all(partial.reshape(owners, owned_rows, width), 'ty', 0, 0, ti...]
  transfers between devices with their start and end apart: 25 -> 25, of which waited for: 7 -> 7; matrix products, arithmetic and copies ran while one was open for 0% -> 0% of each run, Pallas kernels for 7% -> 4%
where the time goes in v5:
time: 162 us; the launch traced here: 161 us
  starting transfers between devices  74.2 us (46%)
  waiting for transfers between devices  51.2 us (32%)
  Pallas kernels  20.3 us (13%)
  blocking collectives  11.7 us (7%)
  local copies, waits for them, and re-layouts  2 us (1%)
    ppermute x2, waiting for transfers between devices, body(): recv = lax.ppermute(behind, 'line', [(1, 0)])  41.6 us
    ppermute x3, starting transfers between devices, exchange(): b = lax.ppermute(b, 'tx', swaps(nx, 1))  32.8 us
    pallas_call x24, Pallas kernels, call(): pl.pallas_call(kernel, in_specs=[pl.BlockSpec(memory_space=pltpu.HBM)] *...  20.3 us
    ppermute x3, starting transfers between devices, exchange(): c = lax.ppermute(c, 'ty', swaps(ny, 0))  17.2 us
    all_to_all x1, blocking collectives, body(): lax.all_to_all(partial.reshape(owners, owned_rows, width), 'ty', 0, 0, ti...  11.7 us
    ppermute x4, starting transfers between devices, body(): recv = lax.ppermute(ahead, 'line', [(k, k + 1)])  6.26 us
    all_to_all x1, waiting for transfers between devices, body(): update = lax.all_to_all(copies, 'ty', 0, 0, tiled=True)  5.77 us
    ppermute x3, starting transfers between devices, exchange(): a = lax.ppermute(a, 'tx', swaps(nx, 0))  5.76 us
  transfers between devices with their start and end apart: 25, of which 7 were waited for; matrix products, arithmetic and copies ran while one was open for 0% of the time, Pallas kernels for 4%

profile of v5, /device:TPU:1, one launch (start us, length us, event | category | flops | bytes accessed | tf_op | source)
XLA Modules:
  0.0 160.5 jit_solution(7658382309109065182)
XLA Ops:
  0.6 0.7 copy-done
  1.4 0.7 collective-permute-start
  2.1 6.4 %collective-permute-start.1 = (f32[16,128]{1,0:T(8,128)S(1)}, f32[16,128]{1,0:T(8,128)S(1)}, u32[]{:S(2)}, u32[]{:S(2)}) collective-permute-start(f32[16,128]{1,0:T(8,128)S(1)} %get-tuple-element.66), channel_id=1, source_target_pairs={{0,1},{1,0},{2,3},{3,2},{4,5},{5,4},{6,7},{7,6},{8,9},{9,8},{10,11... | collective-permute-start | bytes 24584 | tf_op jit(solution)/shard_map/ppermute | solution.py:181
  8.5 9.9 %collective-permute-start.2 = (f32[16,128]{1,0:T(8,128)S(1)}, f32[16,128]{1,0:T(8,128)S(1)}, u32[]{:S(2)}, u32[]{:S(2)}) collective-permute-start(f32[16,128]{1,0:T(8,128)S(1)} %get-tuple-element.67), channel_id=1, source_target_pairs={{16,32},{32,16},{48,64},{64,48},{80,96},{96,80},{17,33},{33,17},{4... | collective-permute-start | bytes 24584 | tf_op jit(solution)/shard_map/ppermute | solution.py:182
  18.4 1.9 %collective-permute-start.3 = (f32[16,128]{1,0:T(8,128)S(1)}, f32[16,128]{1,0:T(8,128)S(1)}, u32[]{:S(2)}, u32[]{:S(2)}) collective-permute-start(f32[16,128]{1,0:T(8,128)S(1)} %get-tuple-element.68), channel_id=1, source_target_pairs={{0,16},{16,0},{32,48},{48,32},{64,80},{80,64},{96,112},{112,96},{1... | collective-permute-start | bytes 24584 | tf_op jit(solution)/shard_map/ppermute | solution.py:183
  20.3 2.3 %shard_map.141 = (bf16[128,128]{1,0:T(8,128)(2,1)S(1)}, bf16[128,128]{1,0:T(8,128)(2,1)S(1)}, bf16[128,128]{1,0:T(8,128)(2,1)S(1)}, bf16[128,128]{1,0:T(8,128)(2...) custom-call(bf16[8192,128]{1,0:T(8,128)(2,1)} %bitcast.17, ...), custom_call_target="tpu_custom_call" | custom-call | tf_op jit(solution)/shard_map/pallas_call | solution.py:17
  22.7 2.5 %shard_map.142 = (f32[64,128]{1,0:T(8,128)S(1)}, f32[64,128]{1,0:T(8,128)}, f32[16,128]{1,0:T(8,128)S(1)}) custom-call(f32[64,128]{1,0:T(8,128)S(1)} %bitcast.11, f32[16,128]{1,0:T(8,128)S(1)} %collective-permute-done.a, f32[16,128]{1,0:T(8,128)S(1)} %collective-permute-done.1.b, f32[16,128]{1,0:T(8,128)S(1)} %collective-permute-done.2.c, ...), custom_call_target="tpu_custom_call" | custom-call | tf_op jit(solution)/shard_map/pallas_call | solution.py:17
  25.2 3.5 %collective-permute-start.4 = (f32[16,128]{1,0:T(8,128)S(1)}, f32[16,128]{1,0:T(8,128)S(1)}, u32[]{:S(2)}, u32[]{:S(2)}) collective-permute-start(f32[16,128]{1,0:T(8,128)S(1)} %get-tuple-element.76), channel_id=1, source_target_pairs={{0,128},{1,129},{2,130},{3,131},{4,132},{5,133},{6,134},{7,135},{8... | collective-permute-start | bytes 24584 | tf_op jit(solution)/shard_map/ppermute | solution.py:423
  28.8 0.8 collective-permute-done.4.got_ref
  29.6 0.6 collective-permute-start.5
  30.3 0.7 collective-permute-start.6
  31.0 1.5 shard_map.146
  32.5 0.7 collective-permute-start.7
  33.4 0.7 collective-permute-start.8
  34.1 1.3 collective-permute-start.9
  35.4 28.2 %collective-permute-done.9.got_ref = f32[16,128]{1,0:T(8,128)S(1)} collective-permute-done((f32[16,128]{1,0:T(8,128)S(1)}, f32[16,128]{1,0:T(8,128)S(1)}, u32[]{:S(2)}, u32[]{:S(2)}) %collective-permute-start.9) | collective-permute-done | bytes 8224 | tf_op jit(solution)/shard_map/ppermute | solution.py:453
  63.7 2.1 %shard_map.151 = (f32[64,128]{1,0:T(8,128)S(1)}, f32[64,128]{1,0:T(8,128)}, f32[16,128]{1,0:T(8,128)S(1)}, f32[16,128]{1,0:T(8,128)S(1)}, f32[16,128]{1,0:T(8,128)S(1)}, /*index=5*/f32[16,128]{1,0:T(8,128)S(1)}) custom-call(f32[64,128]{1,0:T(8,128)S(1)} %get-tuple-element.85.y_ref, f32[16,128]{1,0:T(8,128)S(1)} %get-tuple-element.93.arr_ref, ...), custom_call_target="tpu_custom_call" | custom-call | tf_op jit(solution)/shard_map/pallas_call | solution.py:17
  65.8 0.6 collective-permute-start.10
  66.5 5.3 %collective-permute-start.11 = (f32[16,128]{1,0:T(8,128)S(1)}, f32[16,128]{1,0:T(8,128)S(1)}, u32[]{:S(2)}, u32[]{:S(2)}) collective-permute-start(f32[16,128]{1,0:T(8,128)S(1)} %get-tuple-element.97), channel_id=1, source_target_pairs={{0,1},{1,0},{2,3},{3,2},{4,5},{5,4},{6,7},{7,6},{8,9},{9,8},{10,11... | collective-permute-start | bytes 24584 | tf_op jit(solution)/shard_map/ppermute | solution.py:181
  71.8 13.3 %collective-permute-start.12 = (f32[16,128]{1,0:T(8,128)S(1)}, f32[16,128]{1,0:T(8,128)S(1)}, u32[]{:S(2)}, u32[]{:S(2)}) collective-permute-start(f32[16,128]{1,0:T(8,128)S(1)} %get-tuple-element.98), channel_id=1, source_target_pairs={{16,32},{32,16},{48,64},{64,48},{80,96},{96,80},{17,33},{33,17},{4... | collective-permute-start | bytes 24584 | tf_op jit(solution)/shard_map/ppermute | solution.py:182
  85.1 1.9 %collective-permute-start.13 = (f32[16,128]{1,0:T(8,128)S(1)}, f32[16,128]{1,0:T(8,128)S(1)}, u32[]{:S(2)}, u32[]{:S(2)}) collective-permute-start(f32[16,128]{1,0:T(8,128)S(1)} %get-tuple-element.99), channel_id=1, source_target_pairs={{0,16},{16,0},{32,48},{48,32},{64,80},{80,64},{96,112},{112,96},{1... | collective-permute-start | bytes 24584 | tf_op jit(solution)/shard_map/ppermute | solution.py:183
  87.0 1.1 collective-permute-done.13.d
  88.2 1.9 %shard_map.152 = (f32[64,128]{1,0:T(8,128)S(1)}, f32[64,128]{1,0:T(8,128)S(1)}, f32[16,128]{1,0:T(8,128)S(1)}) custom-call(f32[64,128]{1,0:T(8,128)S(1)} %get-tuple-element.95.x_ref.prev_ref, f32[16,128]{1,0:T(8,128)S(1)} %collective-permute-done.10.a, f32[16,128]{1,0:T(8,128)S(1)} %collective-permute-done.11.b, f32[16,128]{1,0:T(8,128)S(1)} %collective-permute-done.12.c, ...), custom_call_target="tpu_custom_call" | custom-call | tf_op jit(solution)/shard_map/pallas_call | solution.py:17
  90.0 1.4 collective-permute-start.14
  91.4 0.8 collective-permute-done.14.got_ref
  92.6 0.7 collective-permute-start.15
  93.7 0.7 collective-permute-start.16
  94.4 1.5 shard_map.154.local_ref
  96.3 0.7 collective-permute-start.17
  97.0 2.9 %shard_map.157 = (f32[64,128]{1,0:T(8,128)S(1)}, f32[16,128]{1,0:T(8,128)S(1)}) custom-call(f32[16,128]{1,0:T(8,128)S(1)} %get-tuple-element.106.after_ref, f32[64,128]{1,0:T(8,128)S(1)} %get-tuple-element.107.g_ref, f32[16,128]{1,0:T(8,128)S(1)} %get-tuple-element.108.inc_ref, f32[64,128]{1,0:T(8,128)S(1)} %get-tuple-element.69.cols_ref, ...), custom_call_target="tpu_custom_call" | custom-call | tf_op jit(solution)/shard_map/pallas_call | solution.py:17
  99.9 0.4 shard_map.158
  100.3 0.7 collective-permute-start.18
  101.0 0.4 shard_map.159
  101.4 1.3 collective-permute-start.19
  102.7 13.3 %collective-permute-done.19.got_ref = f32[16,128]{1,0:T(8,128)S(1)} collective-permute-done((f32[16,128]{1,0:T(8,128)S(1)}, f32[16,128]{1,0:T(8,128)S(1)}, u32[]{:S(2)}, u32[]{:S(2)}) %collective-permute-start.19) | collective-permute-done | bytes 8224 | tf_op jit(solution)/shard_map/ppermute | solution.py:453
  116.1 1.5 shard_map.160
  117.6 0.7 collective-permute-start.20
  118.2 5.6 %collective-permute-start.21 = (f32[16,128]{1,0:T(8,128)S(1)}, f32[16,128]{1,0:T(8,128)S(1)}, u32[]{:S(2)}, u32[]{:S(2)}) collective-permute-start(f32[16,128]{1,0:T(8,128)S(1)} %get-tuple-element.117), channel_id=1, source_target_pairs={{0,1},{1,0},{2,3},{3,2},{4,5},{5,4},{6,7},{7,6},{8,9},{9,8},{10,11... | collective-permute-start | bytes 24584 | tf_op jit(solution)/shard_map/ppermute | solution.py:181
  123.8 9.5 %collective-permute-start.22 = (f32[16,128]{1,0:T(8,128)S(1)}, f32[16,128]{1,0:T(8,128)S(1)}, u32[]{:S(2)}, u32[]{:S(2)}) collective-permute-start(f32[16,128]{1,0:T(8,128)S(1)} %get-tuple-element.118), channel_id=1, source_target_pairs={{16,32},{32,16},{48,64},{64,48},{80,96},{96,80},{17,33},{33,17},{4... | collective-permute-start | bytes 24584 | tf_op jit(solution)/shard_map/ppermute | solution.py:182
  133.4 1.9 %collective-permute-start.23 = (f32[16,128]{1,0:T(8,128)S(1)}, f32[16,128]{1,0:T(8,128)S(1)}, u32[]{:S(2)}, u32[]{:S(2)}) collective-permute-start(f32[16,128]{1,0:T(8,128)S(1)} %get-tuple-element.119), channel_id=1, source_target_pairs={{0,16},{16,0},{32,48},{48,32},{64,80},{80,64},{96,112},{112,96},{1... | collective-permute-start | bytes 24584 | tf_op jit(solution)/shard_map/ppermute | solution.py:183
  135.3 1.1 collective-permute-done.23.d
  136.4 0.7 shard_map.161
  137.1 11.7 %all_to_all.10.parts_ref = f32[16,4,128]{2,1,0:T(4,128)S(1)} all-to-all(f32[16,4,128]{2,1,0:T(4,128)S(1)} %bitcast.16), channel_id=1, replica_groups=mesh['line'=4,'tx'=8,'ty'=16] {'ty'}, dimensions={0} | all-to-all | bytes 65536 | tf_op jit(solution)/shard_map/all_to_all | solution.py:481
  148.9 0.8 shard_map.162
  149.7 3.5 %all-to-all-start.1 = ((f32[16,4,128]{2,1,0:T(4,128)}), f32[16,4,128]{2,1,0:T(4,128)S(1)}, u32[]{:S(2)}, u32[]{:S(2)}) async-start(f32[16,4,128]{2,1,0:T(4,128)} %shard_map.162), calls=%async_computation.1 | async-start | bytes 65536 | tf_op jit(solution)/shard_map/all_to_all | solution.py:501
  153.2 0.6 copy.16
  153.8 5.8 %all-to-all-done.1 = f32[16,4,128]{2,1,0:T(4,128)S(1)} async-done(((f32[16,4,128]{2,1,0:T(4,128)}), f32[16,4,128]{2,1,0:T(4,128)S(1)}, u32[]{:S(2)}, u32[]{:S(2)}) %all-to-all-start.1) | async-done | bytes 32800 | tf_op jit(solution)/shard_map/all_to_all | solution.py:501
  159.9 0.6 copy.15
  (34 shorter events, 1.9 us)
Async XLA Ops:
  0.6 0.8 copy-start
  1.4 21.3 %copy-start.1 = (f32[4,4,4,128]{3,2,1,0:T(4,128)S(1)}, f32[4,4,4,128]{3,2,1,0:T(4,128)}, u32[]{:S(2)}) copy-start(f32[4,4,4,128]{3,2,1,0:T(4,128)} %param.13) | copy-start | bytes 98308
  1.4 21.3 %collective-permute-start = (f32[16,128]{1,0:T(8,128)S(1)}, f32[16,128]{1,0:T(8,128)S(1)}, u32[]{:S(2)}, u32[]{:S(2)}) collective-permute-start(f32[16,128]{1,0:T(8,128)S(1)} %get-tuple-element.65), channel_id=1, source_target_pairs={{1,2},{2,1},{3,4},{4,3},{5,6},{6,5},{7,8},{8,7},{9,10},{10,9},{11,... | collective-permute-start | bytes 24584 | tf_op jit(solution)/shard_map/ppermute | solution.py:180
  2.1 20.6 %collective-permute-start.1 = (f32[16,128]{1,0:T(8,128)S(1)}, f32[16,128]{1,0:T(8,128)S(1)}, u32[]{:S(2)}, u32[]{:S(2)}) collective-permute-start(f32[16,128]{1,0:T(8,128)S(1)} %get-tuple-element.66), channel_id=1, source_target_pairs={{0,1},{1,0},{2,3},{3,2},{4,5},{5,4},{6,7},{7,6},{8,9},{9,8},{10,11... | collective-permute-start | bytes 24584 | tf_op jit(solution)/shard_map/ppermute | solution.py:181
  8.5 14.2 %collective-permute-start.2 = (f32[16,128]{1,0:T(8,128)S(1)}, f32[16,128]{1,0:T(8,128)S(1)}, u32[]{:S(2)}, u32[]{:S(2)}) collective-permute-start(f32[16,128]{1,0:T(8,128)S(1)} %get-tuple-element.67), channel_id=1, source_target_pairs={{16,32},{32,16},{48,64},{64,48},{80,96},{96,80},{17,33},{33,17},{4... | collective-permute-start | bytes 24584 | tf_op jit(solution)/shard_map/ppermute | solution.py:182
  18.4 4.3 %collective-permute-start.3 = (f32[16,128]{1,0:T(8,128)S(1)}, f32[16,128]{1,0:T(8,128)S(1)}, u32[]{:S(2)}, u32[]{:S(2)}) collective-permute-start(f32[16,128]{1,0:T(8,128)S(1)} %get-tuple-element.68), channel_id=1, source_target_pairs={{0,16},{16,0},{32,48},{48,32},{64,80},{80,64},{96,112},{112,96},{1... | collective-permute-start | bytes 24584 | tf_op jit(solution)/shard_map/ppermute | solution.py:183
  25.2 4.3 %collective-permute-start.4 = (f32[16,128]{1,0:T(8,128)S(1)}, f32[16,128]{1,0:T(8,128)S(1)}, u32[]{:S(2)}, u32[]{:S(2)}) collective-permute-start(f32[16,128]{1,0:T(8,128)S(1)} %get-tuple-element.76), channel_id=1, source_target_pairs={{0,128},{1,129},{2,130},{3,131},{4,132},{5,133},{6,134},{7,135},{8... | collective-permute-start | bytes 24584 | tf_op jit(solution)/shard_map/ppermute | solution.py:423
  29.6 0.7 collective-permute-start.5
  30.3 0.7 collective-permute-start.6
  32.5 0.7 collective-permute-start.7
  33.4 0.7 collective-permute-start.8
  34.1 29.5 %collective-permute-start.9 = (f32[16,128]{1,0:T(8,128)S(1)}, f32[16,128]{1,0:T(8,128)S(1)}, u32[]{:S(2)}, u32[]{:S(2)}) collective-permute-start(f32[16,128]{1,0:T(8,128)S(1)} %get-tuple-element.94), channel_id=1, source_target_pairs={{128,0},{129,1},{130,2},{131,3},{132,4},{133,5},{134,6},{135,7},{1... | collective-permute-start | bytes 24584 | tf_op jit(solution)/shard_map/ppermute | solution.py:453
  65.8 21.2 %collective-permute-start.10 = (f32[16,128]{1,0:T(8,128)S(1)}, f32[16,128]{1,0:T(8,128)S(1)}, u32[]{:S(2)}, u32[]{:S(2)}) collective-permute-start(f32[16,128]{1,0:T(8,128)S(1)} %get-tuple-element.96), channel_id=1, source_target_pairs={{1,2},{2,1},{3,4},{4,3},{5,6},{6,5},{7,8},{8,7},{9,10},{10,9},{11,... | collective-permute-start | bytes 24584 | tf_op jit(solution)/shard_map/ppermute | solution.py:180
  66.5 20.5 %collective-permute-start.11 = (f32[16,128]{1,0:T(8,128)S(1)}, f32[16,128]{1,0:T(8,128)S(1)}, u32[]{:S(2)}, u32[]{:S(2)}) collective-permute-start(f32[16,128]{1,0:T(8,128)S(1)} %get-tuple-element.97), channel_id=1, source_target_pairs={{0,1},{1,0},{2,3},{3,2},{4,5},{5,4},{6,7},{7,6},{8,9},{9,8},{10,11... | collective-permute-start | bytes 24584 | tf_op jit(solution)/shard_map/ppermute | solution.py:181
  71.8 15.3 %collective-permute-start.12 = (f32[16,128]{1,0:T(8,128)S(1)}, f32[16,128]{1,0:T(8,128)S(1)}, u32[]{:S(2)}, u32[]{:S(2)}) collective-permute-start(f32[16,128]{1,0:T(8,128)S(1)} %get-tuple-element.98), channel_id=1, source_target_pairs={{16,32},{32,16},{48,64},{64,48},{80,96},{96,80},{17,33},{33,17},{4... | collective-permute-start | bytes 24584 | tf_op jit(solution)/shard_map/ppermute | solution.py:182
  85.1 3.1 %collective-permute-start.13 = (f32[16,128]{1,0:T(8,128)S(1)}, f32[16,128]{1,0:T(8,128)S(1)}, u32[]{:S(2)}, u32[]{:S(2)}) collective-permute-start(f32[16,128]{1,0:T(8,128)S(1)} %get-tuple-element.99), channel_id=1, source_target_pairs={{0,16},{16,0},{32,48},{48,32},{64,80},{80,64},{96,112},{112,96},{1... | collective-permute-start | bytes 24584 | tf_op jit(solution)/shard_map/ppermute | solution.py:183
  90.0 2.2 %collective-permute-start.14 = (f32[16,128]{1,0:T(8,128)S(1)}, f32[16,128]{1,0:T(8,128)S(1)}, u32[]{:S(2)}, u32[]{:S(2)}) collective-permute-start(f32[16,128]{1,0:T(8,128)S(1)} %get-tuple-element.100.first_ref), channel_id=1, source_target_pairs={{0,128},{1,129},{2,130},{3,131},{4,132},{5,133},{6,134},{7,135},{8... | collective-permute-start | bytes 24584 | tf_op jit(solution)/shard_map/ppermute | solution.py:442
  92.6 0.7 collective-permute-start.15
  93.7 2.2 %collective-permute-start.16 = (f32[16,128]{1,0:T(8,128)S(1)}, f32[16,128]{1,0:T(8,128)S(1)}, u32[]{:S(2)}, u32[]{:S(2)}) collective-permute-start(f32[16,128]{1,0:T(8,128)S(1)} %get-tuple-element.105), channel_id=1, source_target_pairs={{256,384},{257,385},{258,386},{259,387},{260,388},{261,389},{262,3... | collective-permute-start | bytes 24584 | tf_op jit(solution)/shard_map/ppermute | solution.py:446
  96.3 3.6 %collective-permute-start.17 = (f32[16,128]{1,0:T(8,128)S(1)}, f32[16,128]{1,0:T(8,128)S(1)}, u32[]{:S(2)}, u32[]{:S(2)}) collective-permute-start(f32[16,128]{1,0:T(8,128)S(1)} %get-tuple-element.106.after_ref), channel_id=1, source_target_pairs={{384,256},{385,257},{386,258},{387,259},{388,260},{389,261},{390,2... | collective-permute-start | bytes 24584 | tf_op jit(solution)/shard_map/ppermute | solution.py:449
  100.3 0.7 collective-permute-start.18
  101.4 14.7 %collective-permute-start.19 = (f32[16,128]{1,0:T(8,128)S(1)}, f32[16,128]{1,0:T(8,128)S(1)}, u32[]{:S(2)}, u32[]{:S(2)}) collective-permute-start(f32[16,128]{1,0:T(8,128)S(1)} %get-tuple-element.114), channel_id=1, source_target_pairs={{128,0},{129,1},{130,2},{131,3},{132,4},{133,5},{134,6},{135,7},{1... | collective-permute-start | bytes 24584 | tf_op jit(solution)/shard_map/ppermute | solution.py:453
  117.6 17.7 %collective-permute-start.20 = (f32[16,128]{1,0:T(8,128)S(1)}, f32[16,128]{1,0:T(8,128)S(1)}, u32[]{:S(2)}, u32[]{:S(2)}) collective-permute-start(f32[16,128]{1,0:T(8,128)S(1)} %get-tuple-element.116), channel_id=1, source_target_pairs={{1,2},{2,1},{3,4},{4,3},{5,6},{6,5},{7,8},{8,7},{9,10},{10,9},{11,... | collective-permute-start | bytes 24584 | tf_op jit(solution)/shard_map/ppermute | solution.py:180
  118.2 17.1 %collective-permute-start.21 = (f32[16,128]{1,0:T(8,128)S(1)}, f32[16,128]{1,0:T(8,128)S(1)}, u32[]{:S(2)}, u32[]{:S(2)}) collective-permute-start(f32[16,128]{1,0:T(8,128)S(1)} %get-tuple-element.117), channel_id=1, source_target_pairs={{0,1},{1,0},{2,3},{3,2},{4,5},{5,4},{6,7},{7,6},{8,9},{9,8},{10,11... | collective-permute-start | bytes 24584 | tf_op jit(solution)/shard_map/ppermute | solution.py:181
  123.8 11.5 %collective-permute-start.22 = (f32[16,128]{1,0:T(8,128)S(1)}, f32[16,128]{1,0:T(8,128)S(1)}, u32[]{:S(2)}, u32[]{:S(2)}) collective-permute-start(f32[16,128]{1,0:T(8,128)S(1)} %get-tuple-element.118), channel_id=1, source_target_pairs={{16,32},{32,16},{48,64},{64,48},{80,96},{96,80},{17,33},{33,17},{4... | collective-permute-start | bytes 24584 | tf_op jit(solution)/shard_map/ppermute | solution.py:182
  133.4 3.1 %collective-permute-start.23 = (f32[16,128]{1,0:T(8,128)S(1)}, f32[16,128]{1,0:T(8,128)S(1)}, u32[]{:S(2)}, u32[]{:S(2)}) collective-permute-start(f32[16,128]{1,0:T(8,128)S(1)} %get-tuple-element.119), channel_id=1, source_target_pairs={{0,16},{16,0},{32,48},{48,32},{64,80},{80,64},{96,112},{112,96},{1... | collective-permute-start | bytes 24584 | tf_op jit(solution)/shard_map/ppermute | solution.py:183
  149.7 9.9 %all-to-all-start.1 = ((f32[16,4,128]{2,1,0:T(4,128)}), f32[16,4,128]{2,1,0:T(4,128)S(1)}, u32[]{:S(2)}, u32[]{:S(2)}) async-start(f32[16,4,128]{2,1,0:T(4,128)} %shard_map.162), calls=%async_computation.1 | async-start | bytes 65536 | tf_op jit(solution)/shard_map/all_to_all | solution.py:501

commit v6 on v5

--- a/solution.py
+++ b/solution.py
@@ -101,7 +101,7 @@
     lines = lx * ly
     x = x_ref[...]
     even = is_even("tx")
-    d, c, b, a = (r[...] for r in got)
+    b, c, d, a = (r[...] for r in got)
     below, above = jnp.where(even, b, a), jnp.where(even, a, b)
     near[0] = pltpu.roll(x, ly, 0)
     near[1] = pltpu.roll(x, n * lines - ly, 0)
@@ -181,7 +181,7 @@
     c = lax.ppermute(c, "ty", swaps(ny, 0))
     b = lax.ppermute(b, "tx", swaps(nx, 1))
     a = lax.ppermute(a, "tx", swaps(nx, 0))
-    return d, c, b, a
+    return b, c, d, a
 
 
 def body(
@@ -302,18 +302,6 @@
         y_ref[...] = jnp.concatenate(ys, 0)
         f_ref[...] = ys[-1]
 
-    def forward_map(after_ref, cols_ref, lh_ref, ll_ref, w_ref, high, low, one, two):
-        pos = lax.axis_index("line")
-
-        @pl.when((pos > 0) & (pos < segments - 1))
-        def _():
-            mat, prev = (lh_ref[...], ll_ref[...]), None
-            for i in range(n):
-                now = (one, two)[i % 2]
-                advance(prev, now, mat, w_ref, cols_ref, 16, i, lines)
-                prev = now
-            put_halves(prev, high, low, lines)
-
     def backward_map(after_ref, cols_ref, uh_ref, ul_ref, w_ref, high, low, one, two):
         pos = lax.axis_index("line")
 
@@ -349,7 +337,7 @@
             ys = forward(g_ref[...], inc, w_ref, (lh_ref[...], ll_ref[...]), cols_ref[...], n, lines)
             f_ref[...] = ys[-1]
 
-    def chain_turn(g_ref, inc_ref, got_ref, cols_ref, lh_ref, ll_ref, uh_ref, ul_ref, w_ref, after, after_too, y_ref, x_ref):
+    def chain_turn(g_ref, inc_ref, got_ref, cols_ref, lh_ref, ll_ref, uh_ref, ul_ref, w_ref, y_ref, x_ref):
         cols = cols_ref[...]
         inc = inc_ref[...] + got_ref[...]
         ys = forward(g_ref[...], inc, w_ref, (lh_ref[...], ll_ref[...]), cols, n, lines)
@@ -369,11 +357,6 @@
         def _():
             xs = backward(y_ref[...], arr, w_ref, (uh_ref[...], ul_ref[...]), cols_ref[...], n, lines)
             x_ref[...] = xs[0]
-
-    def next_forward(first_ref, inc_ref, got_ref, high, low, sum_ref, f_ref):
-        inc = inc_ref[...] + got_ref[...]
-        sum_ref[...] = inc
-        f_ref[...] = first_ref[...] + each_line_pair(inc, high[...], low[...], lines)
 
     def local_back(after_ref, y_ref, cols_ref, uh_ref, ul_ref, w_ref, x_ref):
         zero = jnp.zeros((lines, width), F32)
@@ -424,23 +407,22 @@
                 step = functools.partial(chain_forward, k + 1)
                 inc, ahead = call(step, [edge, edge], g, inc, recv, cols, lh, ll, w)
             recv = lax.ppermute(ahead, "line", [(segments - 2, segments - 1)])
-            back = call(backward_map, pair, ahead, cols, uh, ul, w, scratch=two)
-            y, behind = call(chain_turn, [block, edge], g, inc, recv, cols, lh, ll, uh, ul, w, *back)
+            y, behind = call(chain_turn, [block, edge], g, inc, recv, cols, lh, ll, uh, ul, w)
             for k in range(segments - 2):
                 recv = lax.ppermute(behind, "line", [(segments - 1 - k, segments - 2 - k)])
                 if k == 0:
                     steps = [pltpu.VMEM((n, lines, width, width), F32)]
                     bend = call(turn_map, pair, behind, cols, lh, ll, uh, ul, w, scratch=steps + two)
                 if k == segments - 3:
-                    fore = call(forward_map, pair, behind, cols, lh, ll, w, scratch=two)
+                    back = call(backward_map, pair, behind, cols, uh, ul, w, scratch=two)
                 step = functools.partial(chain_backward, segments - 2 - k)
-                made = fore if k == segments - 3 else bend
+                made = back if k == segments - 3 else bend
                 arr, behind = call(step, [edge, edge], y, arr, recv, cols, uh, ul, w, *made)
         else:
-            first = ahead
             for k in range(segments - 2):
                 recv = lax.ppermute(ahead, "line", [(k, k + 1)])
-                inc, ahead = call(next_forward, [edge, edge], first, inc, recv, *fore)
+                step = functools.partial(chain_forward, k + 1)
+                inc, ahead = call(step, [edge, edge], g, inc, recv, cols, lh, ll, w)
                 if k == 0:
                     local = call(local_back, [edge], ahead, y, cols, uh, ul, w)[0]
             recv = lax.ppermute(ahead, "line", [(segments - 2, segments - 1)])

time: 162 us -> 150 us (0.926)
  waiting for transfers between devices: 51.2 us -> 42.4 us
  starting transfers between devices: 74.2 us -> 69.5 us
  blocking collectives: 11.7 us -> 14.1 us
    ppermute x2, waiting for transfers between devices: 41.6 us -> 32.8 us  [body(): recv = lax.ppermute(behind, 'line', [(1, 0)])]
    ppermute x3, starting transfers between devices: 17.2 us -> 14 us  [exchange(): c = lax.ppermute(c, 'ty', swaps(ny, 0))]
    all_to_all x1, blocking collectives: 11.7 us -> 14.1 us  [body(): lax.all_to_all(partial.reshape(owners, owned_rows, width), 'ty', 0, 0, ti...]
    pallas_call x24 -> x23, Pallas kernels: 20.3 us -> 19.5 us  [call(): pl.pallas_call(kernel, in_specs=[pl.BlockSpec(memory_space=pltpu.HBM)] *...]
  transfers between devices with their start and end apart: 25 -> 25, of which waited for: 7 -> 7; matrix products, arithmetic and copies ran while one was open for 0% -> 0% of each run, Pallas kernels for 4% -> 5%
where the time goes in v6:
time: 150 us; the launch traced here: 149 us
  starting transfers between devices  69.5 us (46%)
  waiting for transfers between devices  42.4 us (28%)
  Pallas kernels  19.5 us (13%)
  blocking collectives  14.1 us (9%)
  local copies, waits for them, and re-layouts  2 us (1%)
    ppermute x2, waiting for transfers between devices, body(): recv = lax.ppermute(behind, 'line', [(1, 0)])  32.8 us
    ppermute x3, starting transfers between devices, exchange(): b = lax.ppermute(b, 'tx', swaps(nx, 1))  31.5 us
    pallas_call x23, Pallas kernels, call(): pl.pallas_call(kernel, in_specs=[pl.BlockSpec(memory_space=pltpu.HBM)] *...  19.5 us
    all_to_all x1, blocking collectives, body(): lax.all_to_all(partial.reshape(owners, owned_rows, width), 'ty', 0, 0, ti...  14.1 us
    ppermute x3, starting transfers between devices, exchange(): c = lax.ppermute(c, 'ty', swaps(ny, 0))  14 us
    ppermute x4, starting transfers between devices, body(): recv = lax.ppermute(ahead, 'line', [(k, k + 1)])  6.2 us
    all_to_all x1, waiting for transfers between devices, body(): update = lax.all_to_all(copies, 'ty', 0, 0, tiled=True)  5.77 us
    ppermute x3, starting transfers between devices, exchange(): a = lax.ppermute(a, 'tx', swaps(nx, 0))  5.76 us
  transfers between devices with their start and end apart: 25, of which 7 were waited for; matrix products, arithmetic and copies ran while one was open for 0% of the time, Pallas kernels for 5%

profile of v6, /device:TPU:1, one launch (start us, length us, event | category | flops | bytes accessed | tf_op | source)
XLA Modules:
  0.0 148.6 jit_solution(17415114526099963482)
XLA Ops:
  0.6 0.7 copy-done
  1.4 10.2 %collective-permute-start = (f32[16,128]{1,0:T(8,128)S(1)}, f32[16,128]{1,0:T(8,128)S(1)}, u32[]{:S(2)}, u32[]{:S(2)}) collective-permute-start(f32[16,128]{1,0:T(8,128)S(1)} %get-tuple-element.63), channel_id=1, source_target_pairs={{16,32},{32,16},{48,64},{64,48},{80,96},{96,80},{17,33},{33,17},{4... | collective-permute-start | bytes 24584 | tf_op jit(solution)/shard_map/ppermute | solution.py:182
  11.6 3.1 %collective-permute-start.1 = (f32[16,128]{1,0:T(8,128)S(1)}, f32[16,128]{1,0:T(8,128)S(1)}, u32[]{:S(2)}, u32[]{:S(2)}) collective-permute-start(f32[16,128]{1,0:T(8,128)S(1)} %get-tuple-element.64), channel_id=1, source_target_pairs={{0,1},{1,0},{2,3},{3,2},{4,5},{5,4},{6,7},{7,6},{8,9},{9,8},{10,11... | collective-permute-start | bytes 24584 | tf_op jit(solution)/shard_map/ppermute | solution.py:181
  14.7 0.7 collective-permute-start.2
  15.4 1.9 %collective-permute-start.3 = (f32[16,128]{1,0:T(8,128)S(1)}, f32[16,128]{1,0:T(8,128)S(1)}, u32[]{:S(2)}, u32[]{:S(2)}) collective-permute-start(f32[16,128]{1,0:T(8,128)S(1)} %get-tuple-element.66), channel_id=1, source_target_pairs={{0,16},{16,0},{32,48},{48,32},{64,80},{80,64},{96,112},{112,96},{1... | collective-permute-start | bytes 24584 | tf_op jit(solution)/shard_map/ppermute | solution.py:183
  17.3 2.3 %shard_map.141 = (bf16[128,128]{1,0:T(8,128)(2,1)S(1)}, bf16[128,128]{1,0:T(8,128)(2,1)S(1)}, bf16[128,128]{1,0:T(8,128)(2,1)S(1)}, bf16[128,128]{1,0:T(8,128)(2...) custom-call(bf16[8192,128]{1,0:T(8,128)(2,1)} %bitcast.17, ...), custom_call_target="tpu_custom_call" | custom-call | tf_op jit(solution)/shard_map/pallas_call | solution.py:17
  19.7 2.5 %shard_map.142 = (f32[64,128]{1,0:T(8,128)S(1)}, f32[64,128]{1,0:T(8,128)}, f32[16,128]{1,0:T(8,128)S(1)}) custom-call(f32[64,128]{1,0:T(8,128)S(1)} %bitcast.11, f32[16,128]{1,0:T(8,128)S(1)} %collective-permute-done.a, f32[16,128]{1,0:T(8,128)S(1)} %collective-permute-done.1.b, f32[16,128]{1,0:T(8,128)S(1)} %collective-permute-done.2.c, ...), custom_call_target="tpu_custom_call" | custom-call | tf_op jit(solution)/shard_map/pallas_call | solution.py:17
  22.2 3.5 %collective-permute-start.4 = (f32[16,128]{1,0:T(8,128)S(1)}, f32[16,128]{1,0:T(8,128)S(1)}, u32[]{:S(2)}, u32[]{:S(2)}) collective-permute-start(f32[16,128]{1,0:T(8,128)S(1)} %get-tuple-element.74), channel_id=1, source_target_pairs={{0,128},{1,129},{2,130},{3,131},{4,132},{5,133},{6,134},{7,135},{8... | collective-permute-start | bytes 24584 | tf_op jit(solution)/shard_map/ppermute | solution.py:406
  25.8 0.8 collective-permute-done.4.got_ref
  26.6 0.6 collective-permute-start.5
  27.2 0.7 collective-permute-start.6
  27.9 1.5 %shard_map.145 = (f32[64,128]{1,0:T(8,128)S(1)}, f32[16,128]{1,0:T(8,128)S(1)}) custom-call(f32[64,128]{1,0:T(8,128)S(1)} %get-tuple-element.73.g_ref, f32[16,128]{1,0:T(8,128)S(1)} %get-tuple-element.77.inc_ref, f32[16,128]{1,0:T(8,128)S(1)} %collective-permute-done.6.got_ref, f32[64,128]{1,0:T(8,128)S(1)} %get-tuple-element.67.cols_ref, ...), custom_call_target="tpu_custom_call" | custom-call | tf_op jit(solution)/shard_map/pallas_call | solution.py:17
  29.4 0.7 collective-permute-start.7
  30.2 0.7 collective-permute-start.8
  31.1 1.3 collective-permute-start.9
  32.4 19.4 %collective-permute-done.9.got_ref = f32[16,128]{1,0:T(8,128)S(1)} collective-permute-done((f32[16,128]{1,0:T(8,128)S(1)}, f32[16,128]{1,0:T(8,128)S(1)}, u32[]{:S(2)}, u32[]{:S(2)}) %collective-permute-start.9) | collective-permute-done | bytes 8224 | tf_op jit(solution)/shard_map/ppermute | solution.py:435
  51.8 2.1 %shard_map.150 = (f32[64,128]{1,0:T(8,128)S(1)}, f32[64,128]{1,0:T(8,128)}, f32[16,128]{1,0:T(8,128)S(1)}, f32[16,128]{1,0:T(8,128)S(1)}, f32[16,128]{1,0:T(8,128)S(1)}, /*index=5*/f32[16,128]{1,0:T(8,128)S(1)}) custom-call(f32[64,128]{1,0:T(8,128)S(1)} %get-tuple-element.81.y_ref, f32[16,128]{1,0:T(8,128)S(1)} %get-tuple-element.89.arr_ref, ...), custom_call_target="tpu_custom_call" | custom-call | tf_op jit(solution)/shard_map/pallas_call | solution.py:17
  53.9 13.8 %collective-permute-start.10 = (f32[16,128]{1,0:T(8,128)S(1)}, f32[16,128]{1,0:T(8,128)S(1)}, u32[]{:S(2)}, u32[]{:S(2)}) collective-permute-start(f32[16,128]{1,0:T(8,128)S(1)} %get-tuple-element.92), channel_id=1, source_target_pairs={{16,32},{32,16},{48,64},{64,48},{80,96},{96,80},{17,33},{33,17},{4... | collective-permute-start | bytes 24584 | tf_op jit(solution)/shard_map/ppermute | solution.py:182
  67.7 5.3 %collective-permute-start.11 = (f32[16,128]{1,0:T(8,128)S(1)}, f32[16,128]{1,0:T(8,128)S(1)}, u32[]{:S(2)}, u32[]{:S(2)}) collective-permute-start(f32[16,128]{1,0:T(8,128)S(1)} %get-tuple-element.93), channel_id=1, source_target_pairs={{0,1},{1,0},{2,3},{3,2},{4,5},{5,4},{6,7},{7,6},{8,9},{9,8},{10,11... | collective-permute-start | bytes 24584 | tf_op jit(solution)/shard_map/ppermute | solution.py:181
  73.0 0.7 collective-permute-start.12
  73.7 1.9 %collective-permute-start.13 = (f32[16,128]{1,0:T(8,128)S(1)}, f32[16,128]{1,0:T(8,128)S(1)}, u32[]{:S(2)}, u32[]{:S(2)}) collective-permute-start(f32[16,128]{1,0:T(8,128)S(1)} %get-tuple-element.95), channel_id=1, source_target_pairs={{0,16},{16,0},{32,48},{48,32},{64,80},{80,64},{96,112},{112,96},{1... | collective-permute-start | bytes 24584 | tf_op jit(solution)/shard_map/ppermute | solution.py:183
  75.6 1.1 collective-permute-done.13.d
  76.7 1.9 %shard_map.151 = (f32[64,128]{1,0:T(8,128)S(1)}, f32[64,128]{1,0:T(8,128)S(1)}, f32[16,128]{1,0:T(8,128)S(1)}) custom-call(f32[64,128]{1,0:T(8,128)S(1)} %get-tuple-element.91.x_ref.prev_ref, f32[16,128]{1,0:T(8,128)S(1)} %collective-permute-done.10.a, f32[16,128]{1,0:T(8,128)S(1)} %collective-permute-done.11.b, f32[16,128]{1,0:T(8,128)S(1)} %collective-permute-done.12.c, ...), custom_call_target="tpu_custom_call" | custom-call | tf_op jit(solution)/shard_map/pallas_call | solution.py:17
  78.6 1.4 collective-permute-start.14
  80.0 0.8 collective-permute-done.14.got_ref
  80.8 0.6 collective-permute-start.15
  81.5 0.7 collective-permute-start.16
  82.2 1.5 shard_map.153.local_ref
  83.7 0.4 shard_map.155
  84.1 0.7 collective-permute-start.17
  84.8 2.9 %shard_map.156 = (f32[64,128]{1,0:T(8,128)S(1)}, f32[16,128]{1,0:T(8,128)S(1)}) custom-call(f32[16,128]{1,0:T(8,128)S(1)} %get-tuple-element.103.after_ref, f32[64,128]{1,0:T(8,128)S(1)} %get-tuple-element.96.g_ref, f32[16,128]{1,0:T(8,128)S(1)} %get-tuple-element.104.inc_ref, f32[64,128]{1,0:T(8,128)S(1)} %get-tuple-element.67.cols_ref, ...), custom_call_target="tpu_custom_call" | custom-call | tf_op jit(solution)/shard_map/pallas_call | solution.py:17
  88.1 0.7 collective-permute-start.18
  88.8 0.4 shard_map.158
  89.2 1.3 collective-permute-start.19
  90.5 13.4 %collective-permute-done.19.got_ref = f32[16,128]{1,0:T(8,128)S(1)} collective-permute-done((f32[16,128]{1,0:T(8,128)S(1)}, f32[16,128]{1,0:T(8,128)S(1)}, u32[]{:S(2)}, u32[]{:S(2)}) %collective-permute-start.19) | collective-permute-done | bytes 8224 | tf_op jit(solution)/shard_map/ppermute | solution.py:435
  103.9 1.5 %shard_map.159 = (f32[64,128]{1,0:T(8,128)S(1)}, f32[64,128]{1,0:T(8,128)S(1)}, f32[16,128]{1,0:T(8,128)S(1)}, f32[16,128]{1,0:T(8,128)S(1)}, f32[16,128]{1,0:T(8,128)S(1)}, /*index=5*/f32[16,128]{1,0:T(8,128)S(1)}) custom-call(f32[64,128]{1,0:T(8,128)S(1)} %get-tuple-element.105.y_ref, f32[16,128]{1,0:T(8,128)S(1)} %get-tuple-element.109.arr_ref, ...), custom_call_target="tpu_custom_call" | custom-call | tf_op jit(solution)/shard_map/pallas_call | solution.py:17
  105.4 7.5 %collective-permute-start.20 = (f32[16,128]{1,0:T(8,128)S(1)}, f32[16,128]{1,0:T(8,128)S(1)}, u32[]{:S(2)}, u32[]{:S(2)}) collective-permute-start(f32[16,128]{1,0:T(8,128)S(1)} %get-tuple-element.112), channel_id=1, source_target_pairs={{16,32},{32,16},{48,64},{64,48},{80,96},{96,80},{17,33},{33,17},{4... | collective-permute-start | bytes 24584 | tf_op jit(solution)/shard_map/ppermute | solution.py:182
  112.9 5.6 %collective-permute-start.21 = (f32[16,128]{1,0:T(8,128)S(1)}, f32[16,128]{1,0:T(8,128)S(1)}, u32[]{:S(2)}, u32[]{:S(2)}) collective-permute-start(f32[16,128]{1,0:T(8,128)S(1)} %get-tuple-element.113), channel_id=1, source_target_pairs={{0,1},{1,0},{2,3},{3,2},{4,5},{5,4},{6,7},{7,6},{8,9},{9,8},{10,11... | collective-permute-start | bytes 24584 | tf_op jit(solution)/shard_map/ppermute | solution.py:181
  118.4 0.7 collective-permute-start.22
  119.1 1.9 %collective-permute-start.23 = (f32[16,128]{1,0:T(8,128)S(1)}, f32[16,128]{1,0:T(8,128)S(1)}, u32[]{:S(2)}, u32[]{:S(2)}) collective-permute-start(f32[16,128]{1,0:T(8,128)S(1)} %get-tuple-element.115), channel_id=1, source_target_pairs={{0,16},{16,0},{32,48},{48,32},{64,80},{80,64},{96,112},{112,96},{1... | collective-permute-start | bytes 24584 | tf_op jit(solution)/shard_map/ppermute | solution.py:183
  121.1 1.1 collective-permute-done.23.d
  122.2 0.7 shard_map.160
  122.9 14.1 %all_to_all.10.parts_ref = f32[16,4,128]{2,1,0:T(4,128)S(1)} all-to-all(f32[16,4,128]{2,1,0:T(4,128)S(1)} %bitcast.16), channel_id=1, replica_groups=mesh['line'=4,'tx'=8,'ty'=16] {'ty'}, dimensions={0} | all-to-all | bytes 65536 | tf_op jit(solution)/shard_map/all_to_all | solution.py:463
  136.9 0.8 shard_map.161
  137.7 3.5 %all-to-all-start.1 = ((f32[16,4,128]{2,1,0:T(4,128)}), f32[16,4,128]{2,1,0:T(4,128)S(1)}, u32[]{:S(2)}, u32[]{:S(2)}) async-start(f32[16,4,128]{2,1,0:T(4,128)} %shard_map.161), calls=%async_computation.1 | async-start | bytes 65536 | tf_op jit(solution)/shard_map/all_to_all | solution.py:483
  141.2 0.6 copy.16
  141.8 5.8 %all-to-all-done.1 = f32[16,4,128]{2,1,0:T(4,128)S(1)} async-done(((f32[16,4,128]{2,1,0:T(4,128)}), f32[16,4,128]{2,1,0:T(4,128)S(1)}, u32[]{:S(2)}, u32[]{:S(2)}) %all-to-all-start.1) | async-done | bytes 32800 | tf_op jit(solution)/shard_map/all_to_all | solution.py:483
  147.9 0.6 copy.15
  (33 shorter events, 1.1 us)
Async XLA Ops:
  0.6 0.8 copy-start
  1.4 18.3 %copy-start.1 = (f32[4,4,4,128]{3,2,1,0:T(4,128)S(1)}, f32[4,4,4,128]{3,2,1,0:T(4,128)}, u32[]{:S(2)}) copy-start(f32[4,4,4,128]{3,2,1,0:T(4,128)} %param.13) | copy-start | bytes 98308
  1.4 18.2 %collective-permute-start = (f32[16,128]{1,0:T(8,128)S(1)}, f32[16,128]{1,0:T(8,128)S(1)}, u32[]{:S(2)}, u32[]{:S(2)}) collective-permute-start(f32[16,128]{1,0:T(8,128)S(1)} %get-tuple-element.63), channel_id=1, source_target_pairs={{16,32},{32,16},{48,64},{64,48},{80,96},{96,80},{17,33},{33,17},{4... | collective-permute-start | bytes 24584 | tf_op jit(solution)/shard_map/ppermute | solution.py:182
  11.6 8.1 %collective-permute-start.1 = (f32[16,128]{1,0:T(8,128)S(1)}, f32[16,128]{1,0:T(8,128)S(1)}, u32[]{:S(2)}, u32[]{:S(2)}) collective-permute-start(f32[16,128]{1,0:T(8,128)S(1)} %get-tuple-element.64), channel_id=1, source_target_pairs={{0,1},{1,0},{2,3},{3,2},{4,5},{5,4},{6,7},{7,6},{8,9},{9,8},{10,11... | collective-permute-start | bytes 24584 | tf_op jit(solution)/shard_map/ppermute | solution.py:181
  14.7 4.9 %collective-permute-start.2 = (f32[16,128]{1,0:T(8,128)S(1)}, f32[16,128]{1,0:T(8,128)S(1)}, u32[]{:S(2)}, u32[]{:S(2)}) collective-permute-start(f32[16,128]{1,0:T(8,128)S(1)} %get-tuple-element.65), channel_id=1, source_target_pairs={{1,2},{2,1},{3,4},{4,3},{5,6},{6,5},{7,8},{8,7},{9,10},{10,9},{11,... | collective-permute-start | bytes 24584 | tf_op jit(solution)/shard_map/ppermute | solution.py:180
  15.4 4.3 %collective-permute-start.3 = (f32[16,128]{1,0:T(8,128)S(1)}, f32[16,128]{1,0:T(8,128)S(1)}, u32[]{:S(2)}, u32[]{:S(2)}) collective-permute-start(f32[16,128]{1,0:T(8,128)S(1)} %get-tuple-element.66), channel_id=1, source_target_pairs={{0,16},{16,0},{32,48},{48,32},{64,80},{80,64},{96,112},{112,96},{1... | collective-permute-start | bytes 24584 | tf_op jit(solution)/shard_map/ppermute | solution.py:183
  22.2 4.3 %collective-permute-start.4 = (f32[16,128]{1,0:T(8,128)S(1)}, f32[16,128]{1,0:T(8,128)S(1)}, u32[]{:S(2)}, u32[]{:S(2)}) collective-permute-start(f32[16,128]{1,0:T(8,128)S(1)} %get-tuple-element.74), channel_id=1, source_target_pairs={{0,128},{1,129},{2,130},{3,131},{4,132},{5,133},{6,134},{7,135},{8... | collective-permute-start | bytes 24584 | tf_op jit(solution)/shard_map/ppermute | solution.py:406
  26.6 0.7 collective-permute-start.5
  27.2 0.7 collective-permute-start.6
  29.4 0.7 collective-permute-start.7
  30.2 0.9 collective-permute-start.8
  31.1 20.7 %collective-permute-start.9 = (f32[16,128]{1,0:T(8,128)S(1)}, f32[16,128]{1,0:T(8,128)S(1)}, u32[]{:S(2)}, u32[]{:S(2)}) collective-permute-start(f32[16,128]{1,0:T(8,128)S(1)} %get-tuple-element.90), channel_id=1, source_target_pairs={{128,0},{129,1},{130,2},{131,3},{132,4},{133,5},{134,6},{135,7},{1... | collective-permute-start | bytes 24584 | tf_op jit(solution)/shard_map/ppermute | solution.py:435
  53.9 21.7 %collective-permute-start.10 = (f32[16,128]{1,0:T(8,128)S(1)}, f32[16,128]{1,0:T(8,128)S(1)}, u32[]{:S(2)}, u32[]{:S(2)}) collective-permute-start(f32[16,128]{1,0:T(8,128)S(1)} %get-tuple-element.92), channel_id=1, source_target_pairs={{16,32},{32,16},{48,64},{64,48},{80,96},{96,80},{17,33},{33,17},{4... | collective-permute-start | bytes 24584 | tf_op jit(solution)/shard_map/ppermute | solution.py:182
  67.7 7.9 %collective-permute-start.11 = (f32[16,128]{1,0:T(8,128)S(1)}, f32[16,128]{1,0:T(8,128)S(1)}, u32[]{:S(2)}, u32[]{:S(2)}) collective-permute-start(f32[16,128]{1,0:T(8,128)S(1)} %get-tuple-element.93), channel_id=1, source_target_pairs={{0,1},{1,0},{2,3},{3,2},{4,5},{5,4},{6,7},{7,6},{8,9},{9,8},{10,11... | collective-permute-start | bytes 24584 | tf_op jit(solution)/shard_map/ppermute | solution.py:181
  73.0 2.6 %collective-permute-start.12 = (f32[16,128]{1,0:T(8,128)S(1)}, f32[16,128]{1,0:T(8,128)S(1)}, u32[]{:S(2)}, u32[]{:S(2)}) collective-permute-start(f32[16,128]{1,0:T(8,128)S(1)} %get-tuple-element.94), channel_id=1, source_target_pairs={{1,2},{2,1},{3,4},{4,3},{5,6},{6,5},{7,8},{8,7},{9,10},{10,9},{11,... | collective-permute-start | bytes 24584 | tf_op jit(solution)/shard_map/ppermute | solution.py:180
  73.7 3.1 %collective-permute-start.13 = (f32[16,128]{1,0:T(8,128)S(1)}, f32[16,128]{1,0:T(8,128)S(1)}, u32[]{:S(2)}, u32[]{:S(2)}) collective-permute-start(f32[16,128]{1,0:T(8,128)S(1)} %get-tuple-element.95), channel_id=1, source_target_pairs={{0,16},{16,0},{32,48},{48,32},{64,80},{80,64},{96,112},{112,96},{1... | collective-permute-start | bytes 24584 | tf_op jit(solution)/shard_map/ppermute | solution.py:183
  78.6 2.2 %collective-permute-start.14 = (f32[16,128]{1,0:T(8,128)S(1)}, f32[16,128]{1,0:T(8,128)S(1)}, u32[]{:S(2)}, u32[]{:S(2)}) collective-permute-start(f32[16,128]{1,0:T(8,128)S(1)} %get-tuple-element.97), channel_id=1, source_target_pairs={{0,128},{1,129},{2,130},{3,131},{4,132},{5,133},{6,134},{7,135},{8... | collective-permute-start | bytes 24584 | tf_op jit(solution)/shard_map/ppermute | solution.py:423
  80.8 0.7 collective-permute-start.15
  81.5 2.2 %collective-permute-start.16 = (f32[16,128]{1,0:T(8,128)S(1)}, f32[16,128]{1,0:T(8,128)S(1)}, u32[]{:S(2)}, u32[]{:S(2)}) collective-permute-start(f32[16,128]{1,0:T(8,128)S(1)} %get-tuple-element.102), channel_id=1, source_target_pairs={{256,384},{257,385},{258,386},{259,387},{260,388},{261,389},{262,3... | collective-permute-start | bytes 24584 | tf_op jit(solution)/shard_map/ppermute | solution.py:428
  84.1 3.6 %collective-permute-start.17 = (f32[16,128]{1,0:T(8,128)S(1)}, f32[16,128]{1,0:T(8,128)S(1)}, u32[]{:S(2)}, u32[]{:S(2)}) collective-permute-start(f32[16,128]{1,0:T(8,128)S(1)} %get-tuple-element.103.after_ref), channel_id=1, source_target_pairs={{384,256},{385,257},{386,258},{387,259},{388,260},{389,261},{390,2... | collective-permute-start | bytes 24584 | tf_op jit(solution)/shard_map/ppermute | solution.py:431
  88.1 0.7 collective-permute-start.18
  89.2 14.7 %collective-permute-start.19 = (f32[16,128]{1,0:T(8,128)S(1)}, f32[16,128]{1,0:T(8,128)S(1)}, u32[]{:S(2)}, u32[]{:S(2)}) collective-permute-start(f32[16,128]{1,0:T(8,128)S(1)} %get-tuple-element.110), channel_id=1, source_target_pairs={{128,0},{129,1},{130,2},{131,3},{132,4},{133,5},{134,6},{135,7},{1... | collective-permute-start | bytes 24584 | tf_op jit(solution)/shard_map/ppermute | solution.py:435
  105.4 15.6 %collective-permute-start.20 = (f32[16,128]{1,0:T(8,128)S(1)}, f32[16,128]{1,0:T(8,128)S(1)}, u32[]{:S(2)}, u32[]{:S(2)}) collective-permute-start(f32[16,128]{1,0:T(8,128)S(1)} %get-tuple-element.112), channel_id=1, source_target_pairs={{16,32},{32,16},{48,64},{64,48},{80,96},{96,80},{17,33},{33,17},{4... | collective-permute-start | bytes 24584 | tf_op jit(solution)/shard_map/ppermute | solution.py:182
  112.9 8.2 %collective-permute-start.21 = (f32[16,128]{1,0:T(8,128)S(1)}, f32[16,128]{1,0:T(8,128)S(1)}, u32[]{:S(2)}, u32[]{:S(2)}) collective-permute-start(f32[16,128]{1,0:T(8,128)S(1)} %get-tuple-element.113), channel_id=1, source_target_pairs={{0,1},{1,0},{2,3},{3,2},{4,5},{5,4},{6,7},{7,6},{8,9},{9,8},{10,11... | collective-permute-start | bytes 24584 | tf_op jit(solution)/shard_map/ppermute | solution.py:181
  118.4 2.6 %collective-permute-start.22 = (f32[16,128]{1,0:T(8,128)S(1)}, f32[16,128]{1,0:T(8,128)S(1)}, u32[]{:S(2)}, u32[]{:S(2)}) collective-permute-start(f32[16,128]{1,0:T(8,128)S(1)} %get-tuple-element.114), channel_id=1, source_target_pairs={{1,2},{2,1},{3,4},{4,3},{5,6},{6,5},{7,8},{8,7},{9,10},{10,9},{11,... | collective-permute-start | bytes 24584 | tf_op jit(solution)/shard_map/ppermute | solution.py:180
  119.1 3.1 %collective-permute-start.23 = (f32[16,128]{1,0:T(8,128)S(1)}, f32[16,128]{1,0:T(8,128)S(1)}, u32[]{:S(2)}, u32[]{:S(2)}) collective-permute-start(f32[16,128]{1,0:T(8,128)S(1)} %get-tuple-element.115), channel_id=1, source_target_pairs={{0,16},{16,0},{32,48},{48,32},{64,80},{80,64},{96,112},{112,96},{1... | collective-permute-start | bytes 24584 | tf_op jit(solution)/shard_map/ppermute | solution.py:183
  137.7 9.9 %all-to-all-start.1 = ((f32[16,4,128]{2,1,0:T(4,128)}), f32[16,4,128]{2,1,0:T(4,128)S(1)}, u32[]{:S(2)}, u32[]{:S(2)}) async-start(f32[16,4,128]{2,1,0:T(4,128)} %shard_map.161), calls=%async_computation.1 | async-start | bytes 65536 | tf_op jit(solution)/shard_map/all_to_all | solution.py:483

commit v7 on v6

--- a/solution.py
+++ b/solution.py
@@ -292,15 +292,16 @@
         whole=len(raw),
     )
 
-    def open_forward(x_ref, a, b, c, d, cols_ref, fh_ref, fl_ref, rhs_ref, lh_ref, ll_ref, w_ref, g_ref, y_ref, f_ref, near):
+    def open_forward(x_ref, a, b, c, d, cols_ref, fh_ref, fl_ref, rhs_ref, lh_ref, ll_ref, w_ref, g_ref, f_ref, near):
         cols = cols_ref[...]
         total = tangential(x_ref, (a, b, c, d), cols, (fh_ref, fl_ref), near, n, lx, ly)
         g = rhs_ref[...] - total
         g_ref[...] = g
-        zero = jnp.zeros((lines, width), F32)
-        ys = forward(g, zero, w_ref, (lh_ref[...], ll_ref[...]), cols, n, lines)
-        y_ref[...] = jnp.concatenate(ys, 0)
-        f_ref[...] = ys[-1]
+
+        @pl.when(lax.axis_index("line") == 0)
+        def _():
+            zero = jnp.zeros((lines, width), F32)
+            f_ref[...] = forward(g, zero, w_ref, (lh_ref[...], ll_ref[...]), cols, n, lines)[-1]
 
     def backward_map(after_ref, cols_ref, uh_ref, ul_ref, w_ref, high, low, one, two):
         pos = lax.axis_index("line")
@@ -358,9 +359,12 @@
             xs = backward(y_ref[...], arr, w_ref, (uh_ref[...], ul_ref[...]), cols_ref[...], n, lines)
             x_ref[...] = xs[0]
 
-    def local_back(after_ref, y_ref, cols_ref, uh_ref, ul_ref, w_ref, x_ref):
+    def local_back(after_ref, g_ref, cols_ref, lh_ref, ll_ref, uh_ref, ul_ref, w_ref, x_ref):
+        cols = cols_ref[...]
         zero = jnp.zeros((lines, width), F32)
-        x_ref[...] = backward(y_ref[...], zero, w_ref, (uh_ref[...], ul_ref[...]), cols_ref[...], n, lines)[0]
+        ys = forward(g_ref[...], zero, w_ref, (lh_ref[...], ll_ref[...]), cols, n, lines)
+        y = jnp.concatenate(ys, 0)
+        x_ref[...] = backward(y, zero, w_ref, (uh_ref[...], ul_ref[...]), cols, n, lines)[0]
 
     def turn(local_ref, inc_ref, got_ref, high, low, sum_ref, x_ref):
         inc = inc_ref[...] + got_ref[...]
@@ -394,9 +398,9 @@
     change = None
     for sweep in range(SWEEPS):
         got = exchange(sends)
-        g, y, ahead = call(
+        g, ahead = call(
             open_forward,
-            [block, block, edge],
+            [block, edge],
             field, *got, cols, fh, fl, rhs, lh, ll, w,
             scratch=[pltpu.VMEM((4, rows, width), F32)],
         )
@@ -424,7 +428,7 @@
                 step = functools.partial(chain_forward, k + 1)
                 inc, ahead = call(step, [edge, edge], g, inc, recv, cols, lh, ll, w)
                 if k == 0:
-                    local = call(local_back, [edge], ahead, y, cols, uh, ul, w)[0]
+                    local = call(local_back, [edge], ahead, g, cols, lh, ll, uh, ul, w)[0]
             recv = lax.ppermute(ahead, "line", [(segments - 2, segments - 1)])
             inc, behind = call(turn, [edge, edge], local, inc, recv, *bend)
             for k in range(segments - 2):

time: 150 us -> 149 us (level)
    ppermute x4, starting transfers between devices: 6.2 us -> 4.69 us  [body(): recv = lax.ppermute(ahead, 'line', [(k, k + 1)])]
  transfers between devices with their start and end apart: 25 -> 25, of which waited for: 7 -> 7; matrix products, arithmetic and copies ran while one was open for 0% -> 0% of each run, Pallas kernels for 5% -> 6%
where the time goes in v7:
time: 149 us; the launch traced here: 148 us
  starting transfers between devices  69.1 us (46%)
  waiting for transfers between devices  41 us (28%)
  Pallas kernels  20.3 us (14%)
  blocking collectives  14 us (9%)
  local copies, waits for them, and re-layouts  2 us (1%)
    ppermute x3, starting transfers between devices, exchange(): b = lax.ppermute(b, 'tx', swaps(nx, 1))  32.6 us
    ppermute x2, waiting for transfers between devices, body(): recv = lax.ppermute(behind, 'line', [(1, 0)])  31.4 us
    pallas_call x23, Pallas kernels, call(): pl.pallas_call(kernel, in_specs=[pl.BlockSpec(memory_space=pltpu.HBM)] *...  20.3 us
    all_to_all x1, blocking collectives, body(): lax.all_to_all(partial.reshape(owners, owned_rows, width), 'ty', 0, 0, ti...  14 us
    ppermute x3, starting transfers between devices, exchange(): c = lax.ppermute(c, 'ty', swaps(ny, 0))  14 us
    all_to_all x1, waiting for transfers between devices, body(): update = lax.all_to_all(copies, 'ty', 0, 0, tiled=True)  5.77 us
    ppermute x3, starting transfers between devices, exchange(): a = lax.ppermute(a, 'tx', swaps(nx, 0))  5.76 us
    ppermute x4, starting transfers between devices, body(): recv = lax.ppermute(ahead, 'line', [(k, k + 1)])  4.69 us
  transfers between devices with their start and end apart: 25, of which 7 were waited for; matrix products, arithmetic and copies ran while one was open for 0% of the time, Pallas kernels for 6%

profile of v7, /device:TPU:1, one launch (start us, length us, event | category | flops | bytes accessed | tf_op | source)
XLA Modules:
  0.0 147.5 jit_solution(11688142145376480610)
XLA Ops:
  0.6 0.7 copy-done
  1.4 10.2 %collective-permute-start = (f32[16,128]{1,0:T(8,128)S(1)}, f32[16,128]{1,0:T(8,128)S(1)}, u32[]{:S(2)}, u32[]{:S(2)}) collective-permute-start(f32[16,128]{1,0:T(8,128)S(1)} %get-tuple-element.62), channel_id=1, source_target_pairs={{16,32},{32,16},{48,64},{64,48},{80,96},{96,80},{17,33},{33,17},{4... | collective-permute-start | bytes 24584 | tf_op jit(solution)/shard_map/ppermute | solution.py:182
  11.6 3.1 %collective-permute-start.1 = (f32[16,128]{1,0:T(8,128)S(1)}, f32[16,128]{1,0:T(8,128)S(1)}, u32[]{:S(2)}, u32[]{:S(2)}) collective-permute-start(f32[16,128]{1,0:T(8,128)S(1)} %get-tuple-element.63), channel_id=1, source_target_pairs={{0,1},{1,0},{2,3},{3,2},{4,5},{5,4},{6,7},{7,6},{8,9},{9,8},{10,11... | collective-permute-start | bytes 24584 | tf_op jit(solution)/shard_map/ppermute | solution.py:181
  14.7 0.7 collective-permute-start.2
  15.4 1.9 %collective-permute-start.3 = (f32[16,128]{1,0:T(8,128)S(1)}, f32[16,128]{1,0:T(8,128)S(1)}, u32[]{:S(2)}, u32[]{:S(2)}) collective-permute-start(f32[16,128]{1,0:T(8,128)S(1)} %get-tuple-element.65), channel_id=1, source_target_pairs={{0,16},{16,0},{32,48},{48,32},{64,80},{80,64},{96,112},{112,96},{1... | collective-permute-start | bytes 24584 | tf_op jit(solution)/shard_map/ppermute | solution.py:183
  17.3 2.3 %shard_map.141 = (bf16[128,128]{1,0:T(8,128)(2,1)S(1)}, bf16[128,128]{1,0:T(8,128)(2,1)S(1)}, bf16[128,128]{1,0:T(8,128)(2,1)S(1)}, bf16[128,128]{1,0:T(8,128)(2...) custom-call(bf16[8192,128]{1,0:T(8,128)(2,1)} %bitcast.17, ...), custom_call_target="tpu_custom_call" | custom-call | tf_op jit(solution)/shard_map/pallas_call | solution.py:17
  19.7 1.9 %shard_map.142 = (f32[64,128]{1,0:T(8,128)S(1)}, f32[16,128]{1,0:T(8,128)S(1)}) custom-call(f32[64,128]{1,0:T(8,128)S(1)} %bitcast.11, f32[16,128]{1,0:T(8,128)S(1)} %collective-permute-done.a, f32[16,128]{1,0:T(8,128)S(1)} %collective-permute-done.1.b, f32[16,128]{1,0:T(8,128)S(1)} %collective-permute-done.2.c, f32[16,128]{1,0:T(8,128)S(1)} %collective-permute-done.3.d, ...), custom_call_target="tpu_custom_call" | custom-call | tf_op jit(solution)/shard_map/pallas_call | solution.py:17
  21.6 2.1 %collective-permute-start.4 = (f32[16,128]{1,0:T(8,128)S(1)}, f32[16,128]{1,0:T(8,128)S(1)}, u32[]{:S(2)}, u32[]{:S(2)}) collective-permute-start(f32[16,128]{1,0:T(8,128)S(1)} %get-tuple-element.73), channel_id=1, source_target_pairs={{0,128},{1,129},{2,130},{3,131},{4,132},{5,133},{6,134},{7,135},{8... | collective-permute-start | bytes 24584 | tf_op jit(solution)/shard_map/ppermute | solution.py:410
  23.7 0.8 collective-permute-done.4.got_ref
  24.5 0.6 collective-permute-start.5
  25.2 0.7 collective-permute-start.6
  25.8 1.5 %shard_map.145 = (f32[64,128]{1,0:T(8,128)S(1)}, f32[16,128]{1,0:T(8,128)S(1)}) custom-call(f32[64,128]{1,0:T(8,128)S(1)} %get-tuple-element.72.g_ref, f32[16,128]{1,0:T(8,128)S(1)} %get-tuple-element.76.inc_ref, f32[16,128]{1,0:T(8,128)S(1)} %collective-permute-done.6.got_ref, f32[64,128]{1,0:T(8,128)S(1)} %get-tuple-element.66.cols_ref, ...), custom_call_target="tpu_custom_call" | custom-call | tf_op jit(solution)/shard_map/pallas_call | solution.py:17
  27.3 0.7 collective-permute-start.7
  28.1 0.7 collective-permute-start.8
  29.0 1.3 collective-permute-start.9
  30.3 19.4 %collective-permute-done.9.got_ref = f32[16,128]{1,0:T(8,128)S(1)} collective-permute-done((f32[16,128]{1,0:T(8,128)S(1)}, f32[16,128]{1,0:T(8,128)S(1)}, u32[]{:S(2)}, u32[]{:S(2)}) %collective-permute-start.9) | collective-permute-done | bytes 8224 | tf_op jit(solution)/shard_map/ppermute | solution.py:439
  49.7 2.1 %shard_map.150 = (f32[64,128]{1,0:T(8,128)S(1)}, f32[64,128]{1,0:T(8,128)}, f32[16,128]{1,0:T(8,128)S(1)}, f32[16,128]{1,0:T(8,128)S(1)}, f32[16,128]{1,0:T(8,128)S(1)}, /*index=5*/f32[16,128]{1,0:T(8,128)S(1)}) custom-call(f32[64,128]{1,0:T(8,128)S(1)} %get-tuple-element.80.y_ref, f32[16,128]{1,0:T(8,128)S(1)} %get-tuple-element.88.arr_ref, ...), custom_call_target="tpu_custom_call" | custom-call | tf_op jit(solution)/shard_map/pallas_call | solution.py:17
  51.8 13.8 %collective-permute-start.10 = (f32[16,128]{1,0:T(8,128)S(1)}, f32[16,128]{1,0:T(8,128)S(1)}, u32[]{:S(2)}, u32[]{:S(2)}) collective-permute-start(f32[16,128]{1,0:T(8,128)S(1)} %get-tuple-element.91), channel_id=1, source_target_pairs={{16,32},{32,16},{48,64},{64,48},{80,96},{96,80},{17,33},{33,17},{4... | collective-permute-start | bytes 24584 | tf_op jit(solution)/shard_map/ppermute | solution.py:182
  65.6 5.3 %collective-permute-start.11 = (f32[16,128]{1,0:T(8,128)S(1)}, f32[16,128]{1,0:T(8,128)S(1)}, u32[]{:S(2)}, u32[]{:S(2)}) collective-permute-start(f32[16,128]{1,0:T(8,128)S(1)} %get-tuple-element.92), channel_id=1, source_target_pairs={{0,1},{1,0},{2,3},{3,2},{4,5},{5,4},{6,7},{7,6},{8,9},{9,8},{10,11... | collective-permute-start | bytes 24584 | tf_op jit(solution)/shard_map/ppermute | solution.py:181
  70.9 0.7 collective-permute-start.12
  71.6 1.9 %collective-permute-start.13 = (f32[16,128]{1,0:T(8,128)S(1)}, f32[16,128]{1,0:T(8,128)S(1)}, u32[]{:S(2)}, u32[]{:S(2)}) collective-permute-start(f32[16,128]{1,0:T(8,128)S(1)} %get-tuple-element.94), channel_id=1, source_target_pairs={{0,16},{16,0},{32,48},{48,32},{64,80},{80,64},{96,112},{112,96},{1... | collective-permute-start | bytes 24584 | tf_op jit(solution)/shard_map/ppermute | solution.py:183
  73.5 1.1 collective-permute-done.13.d
  74.6 1.9 %shard_map.151 = (f32[64,128]{1,0:T(8,128)S(1)}, f32[16,128]{1,0:T(8,128)S(1)}) custom-call(f32[64,128]{1,0:T(8,128)S(1)} %get-tuple-element.90.x_ref.prev_ref, f32[16,128]{1,0:T(8,128)S(1)} %collective-permute-done.10.a, f32[16,128]{1,0:T(8,128)S(1)} %collective-permute-done.11.b, f32[16,128]{1,0:T(8,128)S(1)} %collective-permute-done.12.c, ...), custom_call_target="tpu_custom_call" | custom-call | tf_op jit(solution)/shard_map/pallas_call | solution.py:17
  76.5 1.3 collective-permute-start.14
  77.8 0.8 collective-permute-done.14.got_ref
  78.6 0.6 collective-permute-start.15
  79.3 0.7 collective-permute-start.16
  80.0 2.9 %shard_map.153.local_ref = f32[16,128]{1,0:T(8,128)S(1)} custom-call(f32[16,128]{1,0:T(8,128)S(1)} %get-tuple-element.97.after_ref, f32[64,128]{1,0:T(8,128)S(1)} %get-tuple-element.95.g_ref, f32[64,128]{1,0:T(8,128)S(1)} %get-tuple-element.66.cols_ref, bf16[128,128]{1,0:T(8,128)(2,1)S(1)} %get-tuple-element.69.lh_ref, ...), custom_call_target="tpu_custom_call" | custom-call | tf_op jit(solution)/shard_map/pallas_call | solution.py:17
  82.9 0.4 shard_map.155
  83.3 0.7 collective-permute-start.17
  84.0 2.9 %shard_map.156 = (f32[64,128]{1,0:T(8,128)S(1)}, f32[16,128]{1,0:T(8,128)S(1)}) custom-call(f32[16,128]{1,0:T(8,128)S(1)} %get-tuple-element.101.after_ref, f32[64,128]{1,0:T(8,128)S(1)} %get-tuple-element.95.g_ref, f32[16,128]{1,0:T(8,128)S(1)} %get-tuple-element.102.inc_ref, f32[64,128]{1,0:T(8,128)S(1)} %get-tuple-element.66.cols_ref, ...), custom_call_target="tpu_custom_call" | custom-call | tf_op jit(solution)/shard_map/pallas_call | solution.py:17
  86.9 0.4 shard_map.157
  87.3 0.7 collective-permute-start.18
  88.4 1.3 collective-permute-start.19
  89.7 12.0 %collective-permute-done.19.got_ref = f32[16,128]{1,0:T(8,128)S(1)} collective-permute-done((f32[16,128]{1,0:T(8,128)S(1)}, f32[16,128]{1,0:T(8,128)S(1)}, u32[]{:S(2)}, u32[]{:S(2)}) %collective-permute-start.19) | collective-permute-done | bytes 8224 | tf_op jit(solution)/shard_map/ppermute | solution.py:439
  101.7 1.5 %shard_map.159 = (f32[64,128]{1,0:T(8,128)S(1)}, f32[64,128]{1,0:T(8,128)S(1)}, f32[16,128]{1,0:T(8,128)S(1)}, f32[16,128]{1,0:T(8,128)S(1)}, f32[16,128]{1,0:T(8,128)S(1)}, /*index=5*/f32[16,128]{1,0:T(8,128)S(1)}) custom-call(f32[64,128]{1,0:T(8,128)S(1)} %get-tuple-element.103.y_ref, f32[16,128]{1,0:T(8,128)S(1)} %get-tuple-element.107.arr_ref, ...), custom_call_target="tpu_custom_call" | custom-call | tf_op jit(solution)/shard_map/pallas_call | solution.py:17
  103.2 8.6 %collective-permute-start.20 = (f32[16,128]{1,0:T(8,128)S(1)}, f32[16,128]{1,0:T(8,128)S(1)}, u32[]{:S(2)}, u32[]{:S(2)}) collective-permute-start(f32[16,128]{1,0:T(8,128)S(1)} %get-tuple-element.110), channel_id=1, source_target_pairs={{16,32},{32,16},{48,64},{64,48},{80,96},{96,80},{17,33},{33,17},{4... | collective-permute-start | bytes 24584 | tf_op jit(solution)/shard_map/ppermute | solution.py:182
  111.8 5.6 %collective-permute-start.21 = (f32[16,128]{1,0:T(8,128)S(1)}, f32[16,128]{1,0:T(8,128)S(1)}, u32[]{:S(2)}, u32[]{:S(2)}) collective-permute-start(f32[16,128]{1,0:T(8,128)S(1)} %get-tuple-element.111), channel_id=1, source_target_pairs={{0,1},{1,0},{2,3},{3,2},{4,5},{5,4},{6,7},{7,6},{8,9},{9,8},{10,11... | collective-permute-start | bytes 24584 | tf_op jit(solution)/shard_map/ppermute | solution.py:181
  117.4 0.7 collective-permute-start.22
  118.1 1.9 %collective-permute-start.23 = (f32[16,128]{1,0:T(8,128)S(1)}, f32[16,128]{1,0:T(8,128)S(1)}, u32[]{:S(2)}, u32[]{:S(2)}) collective-permute-start(f32[16,128]{1,0:T(8,128)S(1)} %get-tuple-element.113), channel_id=1, source_target_pairs={{0,16},{16,0},{32,48},{48,32},{64,80},{80,64},{96,112},{112,96},{1... | collective-permute-start | bytes 24584 | tf_op jit(solution)/shard_map/ppermute | solution.py:183
  120.0 1.1 collective-permute-done.23.d
  121.1 0.7 shard_map.160
  121.8 14.0 %all_to_all.10.parts_ref = f32[16,4,128]{2,1,0:T(4,128)S(1)} all-to-all(f32[16,4,128]{2,1,0:T(4,128)S(1)} %bitcast.16), channel_id=1, replica_groups=mesh['line'=4,'tx'=8,'ty'=16] {'ty'}, dimensions={0} | all-to-all | bytes 65536 | tf_op jit(solution)/shard_map/all_to_all | solution.py:467
  135.9 0.8 shard_map.161
  136.7 3.5 %all-to-all-start.1 = ((f32[16,4,128]{2,1,0:T(4,128)}), f32[16,4,128]{2,1,0:T(4,128)S(1)}, u32[]{:S(2)}, u32[]{:S(2)}) async-start(f32[16,4,128]{2,1,0:T(4,128)} %shard_map.161), calls=%async_computation.1 | async-start | bytes 65536 | tf_op jit(solution)/shard_map/all_to_all | solution.py:487
  140.2 0.6 copy.16
  140.8 5.8 %all-to-all-done.1 = f32[16,4,128]{2,1,0:T(4,128)S(1)} async-done(((f32[16,4,128]{2,1,0:T(4,128)}), f32[16,4,128]{2,1,0:T(4,128)S(1)}, u32[]{:S(2)}, u32[]{:S(2)}) %all-to-all-start.1) | async-done | bytes 32800 | tf_op jit(solution)/shard_map/all_to_all | solution.py:487
  146.9 0.6 copy.15
  (33 shorter events, 1.1 us)
Async XLA Ops:
  0.6 0.8 copy-start
  1.4 18.3 %copy-start.1 = (f32[4,4,4,128]{3,2,1,0:T(4,128)S(1)}, f32[4,4,4,128]{3,2,1,0:T(4,128)}, u32[]{:S(2)}) copy-start(f32[4,4,4,128]{3,2,1,0:T(4,128)} %param.13) | copy-start | bytes 98308
  1.4 18.2 %collective-permute-start = (f32[16,128]{1,0:T(8,128)S(1)}, f32[16,128]{1,0:T(8,128)S(1)}, u32[]{:S(2)}, u32[]{:S(2)}) collective-permute-start(f32[16,128]{1,0:T(8,128)S(1)} %get-tuple-element.62), channel_id=1, source_target_pairs={{16,32},{32,16},{48,64},{64,48},{80,96},{96,80},{17,33},{33,17},{4... | collective-permute-start | bytes 24584 | tf_op jit(solution)/shard_map/ppermute | solution.py:182
  11.6 8.1 %collective-permute-start.1 = (f32[16,128]{1,0:T(8,128)S(1)}, f32[16,128]{1,0:T(8,128)S(1)}, u32[]{:S(2)}, u32[]{:S(2)}) collective-permute-start(f32[16,128]{1,0:T(8,128)S(1)} %get-tuple-element.63), channel_id=1, source_target_pairs={{0,1},{1,0},{2,3},{3,2},{4,5},{5,4},{6,7},{7,6},{8,9},{9,8},{10,11... | collective-permute-start | bytes 24584 | tf_op jit(solution)/shard_map/ppermute | solution.py:181
  14.7 4.9 %collective-permute-start.2 = (f32[16,128]{1,0:T(8,128)S(1)}, f32[16,128]{1,0:T(8,128)S(1)}, u32[]{:S(2)}, u32[]{:S(2)}) collective-permute-start(f32[16,128]{1,0:T(8,128)S(1)} %get-tuple-element.64), channel_id=1, source_target_pairs={{1,2},{2,1},{3,4},{4,3},{5,6},{6,5},{7,8},{8,7},{9,10},{10,9},{11,... | collective-permute-start | bytes 24584 | tf_op jit(solution)/shard_map/ppermute | solution.py:180
  15.4 4.3 %collective-permute-start.3 = (f32[16,128]{1,0:T(8,128)S(1)}, f32[16,128]{1,0:T(8,128)S(1)}, u32[]{:S(2)}, u32[]{:S(2)}) collective-permute-start(f32[16,128]{1,0:T(8,128)S(1)} %get-tuple-element.65), channel_id=1, source_target_pairs={{0,16},{16,0},{32,48},{48,32},{64,80},{80,64},{96,112},{112,96},{1... | collective-permute-start | bytes 24584 | tf_op jit(solution)/shard_map/ppermute | solution.py:183
  21.6 2.9 %collective-permute-start.4 = (f32[16,128]{1,0:T(8,128)S(1)}, f32[16,128]{1,0:T(8,128)S(1)}, u32[]{:S(2)}, u32[]{:S(2)}) collective-permute-start(f32[16,128]{1,0:T(8,128)S(1)} %get-tuple-element.73), channel_id=1, source_target_pairs={{0,128},{1,129},{2,130},{3,131},{4,132},{5,133},{6,134},{7,135},{8... | collective-permute-start | bytes 24584 | tf_op jit(solution)/shard_map/ppermute | solution.py:410
  24.5 0.7 collective-permute-start.5
  25.2 0.7 collective-permute-start.6
  27.3 0.7 collective-permute-start.7
  28.1 0.9 collective-permute-start.8
  29.0 20.7 %collective-permute-start.9 = (f32[16,128]{1,0:T(8,128)S(1)}, f32[16,128]{1,0:T(8,128)S(1)}, u32[]{:S(2)}, u32[]{:S(2)}) collective-permute-start(f32[16,128]{1,0:T(8,128)S(1)} %get-tuple-element.89), channel_id=1, source_target_pairs={{128,0},{129,1},{130,2},{131,3},{132,4},{133,5},{134,6},{135,7},{1... | collective-permute-start | bytes 24584 | tf_op jit(solution)/shard_map/ppermute | solution.py:439
  51.8 21.7 %collective-permute-start.10 = (f32[16,128]{1,0:T(8,128)S(1)}, f32[16,128]{1,0:T(8,128)S(1)}, u32[]{:S(2)}, u32[]{:S(2)}) collective-permute-start(f32[16,128]{1,0:T(8,128)S(1)} %get-tuple-element.91), channel_id=1, source_target_pairs={{16,32},{32,16},{48,64},{64,48},{80,96},{96,80},{17,33},{33,17},{4... | collective-permute-start | bytes 24584 | tf_op jit(solution)/shard_map/ppermute | solution.py:182
  65.6 7.9 %collective-permute-start.11 = (f32[16,128]{1,0:T(8,128)S(1)}, f32[16,128]{1,0:T(8,128)S(1)}, u32[]{:S(2)}, u32[]{:S(2)}) collective-permute-start(f32[16,128]{1,0:T(8,128)S(1)} %get-tuple-element.92), channel_id=1, source_target_pairs={{0,1},{1,0},{2,3},{3,2},{4,5},{5,4},{6,7},{7,6},{8,9},{9,8},{10,11... | collective-permute-start | bytes 24584 | tf_op jit(solution)/shard_map/ppermute | solution.py:181
  70.9 2.6 %collective-permute-start.12 = (f32[16,128]{1,0:T(8,128)S(1)}, f32[16,128]{1,0:T(8,128)S(1)}, u32[]{:S(2)}, u32[]{:S(2)}) collective-permute-start(f32[16,128]{1,0:T(8,128)S(1)} %get-tuple-element.93), channel_id=1, source_target_pairs={{1,2},{2,1},{3,4},{4,3},{5,6},{6,5},{7,8},{8,7},{9,10},{10,9},{11,... | collective-permute-start | bytes 24584 | tf_op jit(solution)/shard_map/ppermute | solution.py:180
  71.6 3.1 %collective-permute-start.13 = (f32[16,128]{1,0:T(8,128)S(1)}, f32[16,128]{1,0:T(8,128)S(1)}, u32[]{:S(2)}, u32[]{:S(2)}) collective-permute-start(f32[16,128]{1,0:T(8,128)S(1)} %get-tuple-element.94), channel_id=1, source_target_pairs={{0,16},{16,0},{32,48},{48,32},{64,80},{80,64},{96,112},{112,96},{1... | collective-permute-start | bytes 24584 | tf_op jit(solution)/shard_map/ppermute | solution.py:183
  76.5 2.1 %collective-permute-start.14 = (f32[16,128]{1,0:T(8,128)S(1)}, f32[16,128]{1,0:T(8,128)S(1)}, u32[]{:S(2)}, u32[]{:S(2)}) collective-permute-start(f32[16,128]{1,0:T(8,128)S(1)} %get-tuple-element.96), channel_id=1, source_target_pairs={{0,128},{1,129},{2,130},{3,131},{4,132},{5,133},{6,134},{7,135},{8... | collective-permute-start | bytes 24584 | tf_op jit(solution)/shard_map/ppermute | solution.py:427
  78.6 0.7 collective-permute-start.15
  79.3 3.6 %collective-permute-start.16 = (f32[16,128]{1,0:T(8,128)S(1)}, f32[16,128]{1,0:T(8,128)S(1)}, u32[]{:S(2)}, u32[]{:S(2)}) collective-permute-start(f32[16,128]{1,0:T(8,128)S(1)} %get-tuple-element.100), channel_id=1, source_target_pairs={{256,384},{257,385},{258,386},{259,387},{260,388},{261,389},{262,3... | collective-permute-start | bytes 24584 | tf_op jit(solution)/shard_map/ppermute | solution.py:432
  83.3 3.6 %collective-permute-start.17 = (f32[16,128]{1,0:T(8,128)S(1)}, f32[16,128]{1,0:T(8,128)S(1)}, u32[]{:S(2)}, u32[]{:S(2)}) collective-permute-start(f32[16,128]{1,0:T(8,128)S(1)} %get-tuple-element.101.after_ref), channel_id=1, source_target_pairs={{384,256},{385,257},{386,258},{387,259},{388,260},{389,261},{390,2... | collective-permute-start | bytes 24584 | tf_op jit(solution)/shard_map/ppermute | solution.py:435
  87.3 0.7 collective-permute-start.18
  88.4 13.3 %collective-permute-start.19 = (f32[16,128]{1,0:T(8,128)S(1)}, f32[16,128]{1,0:T(8,128)S(1)}, u32[]{:S(2)}, u32[]{:S(2)}) collective-permute-start(f32[16,128]{1,0:T(8,128)S(1)} %get-tuple-element.108), channel_id=1, source_target_pairs={{128,0},{129,1},{130,2},{131,3},{132,4},{133,5},{134,6},{135,7},{1... | collective-permute-start | bytes 24584 | tf_op jit(solution)/shard_map/ppermute | solution.py:439
  103.2 16.8 %collective-permute-start.20 = (f32[16,128]{1,0:T(8,128)S(1)}, f32[16,128]{1,0:T(8,128)S(1)}, u32[]{:S(2)}, u32[]{:S(2)}) collective-permute-start(f32[16,128]{1,0:T(8,128)S(1)} %get-tuple-element.110), channel_id=1, source_target_pairs={{16,32},{32,16},{48,64},{64,48},{80,96},{96,80},{17,33},{33,17},{4... | collective-permute-start | bytes 24584 | tf_op jit(solution)/shard_map/ppermute | solution.py:182
  111.8 8.2 %collective-permute-start.21 = (f32[16,128]{1,0:T(8,128)S(1)}, f32[16,128]{1,0:T(8,128)S(1)}, u32[]{:S(2)}, u32[]{:S(2)}) collective-permute-start(f32[16,128]{1,0:T(8,128)S(1)} %get-tuple-element.111), channel_id=1, source_target_pairs={{0,1},{1,0},{2,3},{3,2},{4,5},{5,4},{6,7},{7,6},{8,9},{9,8},{10,11... | collective-permute-start | bytes 24584 | tf_op jit(solution)/shard_map/ppermute | solution.py:181
  117.4 2.6 %collective-permute-start.22 = (f32[16,128]{1,0:T(8,128)S(1)}, f32[16,128]{1,0:T(8,128)S(1)}, u32[]{:S(2)}, u32[]{:S(2)}) collective-permute-start(f32[16,128]{1,0:T(8,128)S(1)} %get-tuple-element.112), channel_id=1, source_target_pairs={{1,2},{2,1},{3,4},{4,3},{5,6},{6,5},{7,8},{8,7},{9,10},{10,9},{11,... | collective-permute-start | bytes 24584 | tf_op jit(solution)/shard_map/ppermute | solution.py:180
  118.1 3.1 %collective-permute-start.23 = (f32[16,128]{1,0:T(8,128)S(1)}, f32[16,128]{1,0:T(8,128)S(1)}, u32[]{:S(2)}, u32[]{:S(2)}) collective-permute-start(f32[16,128]{1,0:T(8,128)S(1)} %get-tuple-element.113), channel_id=1, source_target_pairs={{0,16},{16,0},{32,48},{48,32},{64,80},{80,64},{96,112},{112,96},{1... | collective-permute-start | bytes 24584 | tf_op jit(solution)/shard_map/ppermute | solution.py:183
  136.7 9.9 %all-to-all-start.1 = ((f32[16,4,128]{2,1,0:T(4,128)}), f32[16,4,128]{2,1,0:T(4,128)S(1)}, u32[]{:S(2)}, u32[]{:S(2)}) async-start(f32[16,4,128]{2,1,0:T(4,128)} %shard_map.161), calls=%async_computation.1 | async-start | bytes 65536 | tf_op jit(solution)/shard_map/all_to_all | solution.py:487
